TPU v7x, 16 devices: a whole 2x2x2 slice. The times are simulated.
16 devices in a mesh: fsdp: 16 (over z, y, x, core).
Axes of the slice: x: 2, y: 2, z: 2, core: 2. Of those that a mesh axis runs over, the one named last changes fastest.
Arguments:
- tokens: int32 [32, 512], P('fsdp')
- positions: int32 [32, 512], P('fsdp')
- embed_table: bfloat16 [49152, 960], P('fsdp')
- attn_norm: bfloat16 [960], P('fsdp')
- w_query: bfloat16 [960, 960], P('fsdp')
- w_key: bfloat16 [960, 320], P('fsdp')
- w_value: bfloat16 [960, 320], P('fsdp')
- q_norm: bfloat16 [64], replicated
- k_norm: bfloat16 [64], replicated
- w_out: bfloat16 [960, 960], P('fsdp')
- mlp_norm: bfloat16 [960], P('fsdp')
- w_gate: bfloat16 [960, 2560], P('fsdp')
- w_up: bfloat16 [960, 2560], P('fsdp')
- w_down: bfloat16 [2560, 960], P('fsdp')
- dy_out: bfloat16 [32, 512, 960], P('fsdp')
Outputs:
- output 1: bfloat16 [32, 512, 960], P('fsdp')
- output 2: float32 [49152, 960], P('fsdp')
- output 3: float32 [960], P('fsdp')
- output 4: float32 [960, 960], P('fsdp')
- output 5: float32 [960, 320], P('fsdp')
- output 6: float32 [960, 320], P('fsdp')
- output 7: float32 [64], replicated
- output 8: float32 [64], replicated
- output 9: float32 [960, 960], P('fsdp')
- output 10: float32 [960], P('fsdp')
- output 11: float32 [960, 2560], P('fsdp')
- output 12: float32 [960, 2560], P('fsdp')
- output 13: float32 [2560, 960], P('fsdp')
All inputs are finite; a program needn't handle non-finite values.
Results may differ from a plain program's by a relative error of at most 0.0185032.
Values are sent between devices in bfloat16 or wider.
A program may use at most 1 GiB of HBM per device.

v0:
```python
import math
import jax
import jax.numpy as jnp
from jax import lax
from jax.sharding import PartitionSpec as P

NORM_EPS = 1e-6
ROPE_THETA = 1.0e6
AXIS_NAME = 'fsdp'
SHARDED = (True, True, True, True, False, False, True, True, True, True, True)


def rope_tables(positions, head_dim):
    half_dim = head_dim // 2
    inv_freq = jnp.exp(jnp.arange(half_dim, dtype=jnp.float32) * (-2.0 * math.log(ROPE_THETA) / head_dim))
    angles = positions.astype(jnp.float32)[:, :, None] * inv_freq
    return jnp.cos(angles), jnp.sin(angles)


def rotate(values, cos_t, sin_t):
    half_dim = values.shape[-1] // 2
    lead_half = values[..., :half_dim]
    tail_half = values[..., half_dim:]
    return jnp.concatenate([lead_half * cos_t - tail_half * sin_t, tail_half * cos_t + lead_half * sin_t], axis=-1)


def norm_fwd(values):
    values_f = values.astype(jnp.float32)
    inv_rms = lax.rsqrt(jnp.mean(values_f * values_f, axis=-1, keepdims=True) + NORM_EPS)
    return values_f * inv_rms, inv_rms


def norm_bwd(grad_out, normed, inv_rms, norm_gain):
    grad_normed = grad_out * norm_gain.astype(jnp.float32)
    mean_term = jnp.mean(grad_normed * normed, axis=-1, keepdims=True)
    return inv_rms * (grad_normed - normed * mean_term)


def attn_fwd(q_rot, k_rot, v_raw):
    seq_len = q_rot.shape[1]
    attn_scale = q_rot.shape[-1] ** -0.5
    scores = jnp.einsum('bqgrh,bkgh->bgrqk', q_rot, k_rot, preferred_element_type=jnp.float32) * attn_scale
    causal = lax.broadcasted_iota(jnp.int32, (seq_len, seq_len), 0) >= lax.broadcasted_iota(jnp.int32, (seq_len, seq_len), 1)
    attn_probs = jax.nn.softmax(jnp.where(causal, scores, -1e30), axis=-1)
    attn_heads = jnp.einsum('bgrqk,bkgh->bqgrh', attn_probs.astype(jnp.bfloat16), v_raw, preferred_element_type=jnp.float32)
    return attn_heads.astype(jnp.bfloat16), attn_probs


def attn_bwd(grad_out, q_rot, k_rot, v_raw, attn_probs):
    attn_scale = q_rot.shape[-1] ** -0.5
    grad_b = grad_out.astype(jnp.bfloat16)
    probs_b = attn_probs.astype(jnp.bfloat16)
    grad_probs = jnp.einsum('bqgrh,bkgh->bgrqk', grad_b, v_raw, preferred_element_type=jnp.float32)
    grad_v = jnp.einsum('bgrqk,bqgrh->bkgh', probs_b, grad_b, preferred_element_type=jnp.float32)
    grad_scores = attn_probs * (grad_probs - jnp.sum(grad_probs * attn_probs, axis=-1, keepdims=True)) * attn_scale
    scores_b = grad_scores.astype(jnp.bfloat16)
    grad_q = jnp.einsum('bgrqk,bkgh->bqgrh', scores_b, k_rot, preferred_element_type=jnp.float32)
    grad_k = jnp.einsum('bgrqk,bqgrh->bkgh', scores_b, q_rot, preferred_element_type=jnp.float32)
    return grad_q, grad_k, grad_v


def layer_fwd(x_emb, positions, weights):
    attn_norm, w_query, w_key, w_value, q_norm, k_norm, w_out, mlp_norm, w_gate, w_up, w_down = weights
    batch_len, seq_len, model_dim = x_emb.shape
    head_dim = q_norm.shape[0]
    kv_heads = w_key.shape[1] // head_dim
    q_per_kv = w_query.shape[1] // w_key.shape[1]
    cos_t, sin_t = rope_tables(positions, head_dim)
    cos_q = cos_t[:, :, None, None, :]
    sin_q = sin_t[:, :, None, None, :]
    cos_k = cos_t[:, :, None, :]
    sin_k = sin_t[:, :, None, :]
    normed1, norm1_inv = norm_fwd(x_emb)
    attn_in = (normed1 * attn_norm.astype(jnp.float32)).astype(jnp.bfloat16)
    q_raw = jnp.einsum('bsd,dn->bsn', attn_in, w_query, preferred_element_type=jnp.float32).astype(jnp.bfloat16).reshape(batch_len, seq_len, kv_heads, q_per_kv, head_dim)
    k_raw = jnp.einsum('bsd,dn->bsn', attn_in, w_key, preferred_element_type=jnp.float32).astype(jnp.bfloat16).reshape(batch_len, seq_len, kv_heads, head_dim)
    v_raw = jnp.einsum('bsd,dn->bsn', attn_in, w_value, preferred_element_type=jnp.float32).astype(jnp.bfloat16).reshape(batch_len, seq_len, kv_heads, head_dim)
    q_normed, q_inv = norm_fwd(q_raw)
    k_normed, k_inv = norm_fwd(k_raw)
    q_rot = rotate(q_normed * q_norm.astype(jnp.float32), cos_q, sin_q).astype(jnp.bfloat16)
    k_rot = rotate(k_normed * k_norm.astype(jnp.float32), cos_k, sin_k).astype(jnp.bfloat16)
    attn_heads, attn_probs = attn_fwd(q_rot, k_rot, v_raw)
    attn_flat = attn_heads.reshape(batch_len, seq_len, -1)
    attn_proj = jnp.einsum('bsn,nd->bsd', attn_flat, w_out, preferred_element_type=jnp.float32)
    hidden = (x_emb.astype(jnp.float32) + attn_proj).astype(jnp.bfloat16)
    normed2, norm2_inv = norm_fwd(hidden)
    mlp_in = (normed2 * mlp_norm.astype(jnp.float32)).astype(jnp.bfloat16)
    gate_pre = jnp.einsum('bsd,df->bsf', mlp_in, w_gate, preferred_element_type=jnp.float32)
    up_proj = jnp.einsum('bsd,df->bsf', mlp_in, w_up, preferred_element_type=jnp.float32)
    mlp_act = (jax.nn.silu(gate_pre) * up_proj).astype(jnp.bfloat16)
    mlp_proj = jnp.einsum('bsf,fd->bsd', mlp_act, w_down, preferred_element_type=jnp.float32)
    layer_out = (hidden.astype(jnp.float32) + mlp_proj).astype(jnp.bfloat16)
    saved_acts = (normed1, norm1_inv, attn_in, q_normed, q_inv, k_normed, k_inv, q_rot, k_rot, v_raw, attn_probs, attn_flat, normed2, norm2_inv, mlp_in, gate_pre, up_proj, mlp_act, cos_q, sin_q, cos_k, sin_k)
    return layer_out, saved_acts


def layer_bwd(dy_out, saved_acts, weights):
    attn_norm, w_query, w_key, w_value, q_norm, k_norm, w_out, mlp_norm, w_gate, w_up, w_down = weights
    (normed1, norm1_inv, attn_in, q_normed, q_inv, k_normed, k_inv, q_rot, k_rot, v_raw, attn_probs, attn_flat, normed2, norm2_inv, mlp_in, gate_pre, up_proj, mlp_act, cos_q, sin_q, cos_k, sin_k) = saved_acts
    batch_len, seq_len, model_dim = dy_out.shape
    grad_w_down = jnp.einsum('bsf,bsd->fd', mlp_act, dy_out, preferred_element_type=jnp.float32)
    grad_act = jnp.einsum('bsd,fd->bsf', dy_out, w_down, preferred_element_type=jnp.float32)
    gate_sig = jax.nn.sigmoid(gate_pre)
    grad_gate = (grad_act * up_proj * gate_sig * (1.0 + gate_pre * (1.0 - gate_sig))).astype(jnp.bfloat16)
    grad_up = (grad_act * gate_pre * gate_sig).astype(jnp.bfloat16)
    grad_w_gate = jnp.einsum('bsd,bsf->df', mlp_in, grad_gate, preferred_element_type=jnp.float32)
    grad_w_up = jnp.einsum('bsd,bsf->df', mlp_in, grad_up, preferred_element_type=jnp.float32)
    grad_mlp_in = jnp.einsum('bsf,df->bsd', grad_gate, w_gate, preferred_element_type=jnp.float32) + jnp.einsum('bsf,df->bsd', grad_up, w_up, preferred_element_type=jnp.float32)
    grad_mlp_norm = jnp.sum(grad_mlp_in * normed2, axis=(0, 1))
    grad_hidden = dy_out.astype(jnp.float32) + norm_bwd(grad_mlp_in, normed2, norm2_inv, mlp_norm)
    hidden_b = grad_hidden.astype(jnp.bfloat16)
    grad_w_out = jnp.einsum('bsn,bsd->nd', attn_flat, hidden_b, preferred_element_type=jnp.float32)
    grad_heads = jnp.einsum('bsd,nd->bsn', hidden_b, w_out, preferred_element_type=jnp.float32).reshape(q_rot.shape)
    grad_q, grad_k, grad_v = attn_bwd(grad_heads, q_rot, k_rot, v_raw, attn_probs)
    grad_qt = rotate(grad_q, cos_q, -sin_q)
    grad_kt = rotate(grad_k, cos_k, -sin_k)
    grad_q_norm = jnp.sum(grad_qt * q_normed, axis=(0, 1, 2, 3))
    grad_k_norm = jnp.sum(grad_kt * k_normed, axis=(0, 1, 2))
    grad_q_raw = norm_bwd(grad_qt, q_normed, q_inv, q_norm).astype(jnp.bfloat16).reshape(batch_len, seq_len, -1)
    grad_k_raw = norm_bwd(grad_kt, k_normed, k_inv, k_norm).astype(jnp.bfloat16).reshape(batch_len, seq_len, -1)
    grad_v_raw = grad_v.astype(jnp.bfloat16).reshape(batch_len, seq_len, -1)
    grad_w_query = jnp.einsum('bsd,bsn->dn', attn_in, grad_q_raw, preferred_element_type=jnp.float32)
    grad_w_key = jnp.einsum('bsd,bsn->dn', attn_in, grad_k_raw, preferred_element_type=jnp.float32)
    grad_w_value = jnp.einsum('bsd,bsn->dn', attn_in, grad_v_raw, preferred_element_type=jnp.float32)
    grad_attn_in = (jnp.einsum('bsn,dn->bsd', grad_q_raw, w_query, preferred_element_type=jnp.float32)
                    + jnp.einsum('bsn,dn->bsd', grad_k_raw, w_key, preferred_element_type=jnp.float32)
                    + jnp.einsum('bsn,dn->bsd', grad_v_raw, w_value, preferred_element_type=jnp.float32))
    grad_attn_norm = jnp.sum(grad_attn_in * normed1, axis=(0, 1))
    grad_x_emb = grad_hidden + norm_bwd(grad_attn_in, normed1, norm1_inv, attn_norm)
    return grad_x_emb, (grad_attn_norm, grad_w_query, grad_w_key, grad_w_value, grad_q_norm, grad_k_norm, grad_w_out, grad_mlp_norm, grad_w_gate, grad_w_up, grad_w_down)


def solution(mesh):
    row_spec = P(AXIS_NAME, None)
    vec_spec = P(AXIS_NAME)
    full_spec = P(None)
    batch_spec = P(AXIS_NAME, None, None)
    weight_specs = (vec_spec, row_spec, row_spec, row_spec, full_spec, full_spec, row_spec, vec_spec, row_spec, row_spec, row_spec)

    def device_step(tokens, positions, table_shard, attn_norm, w_query, w_key, w_value, q_norm, k_norm, w_out, mlp_norm, w_gate, w_up, w_down, dy_out):
        shards = (attn_norm, w_query, w_key, w_value, q_norm, k_norm, w_out, mlp_norm, w_gate, w_up, w_down)
        weights = tuple(lax.all_gather(w_shard, AXIS_NAME, tiled=True) if is_sharded else w_shard for w_shard, is_sharded in zip(shards, SHARDED))
        batch_len, seq_len = tokens.shape
        rows_local, model_dim = table_shard.shape
        all_ids = lax.all_gather(tokens.reshape(-1), AXIS_NAME, tiled=True)
        local_ids = all_ids - lax.axis_index(AXIS_NAME) * rows_local
        is_owner = (local_ids >= 0) & (local_ids < rows_local)
        picked = jnp.take(table_shard, jnp.clip(local_ids, 0, rows_local - 1), axis=0)
        picked = jnp.where(is_owner[:, None], picked, jnp.zeros((), picked.dtype))
        x_emb = lax.psum_scatter(picked, AXIS_NAME, scatter_dimension=0, tiled=True).reshape(batch_len, seq_len, model_dim)
        layer_out, saved_acts = layer_fwd(x_emb, positions, weights)
        grad_x_emb, grad_full = layer_bwd(dy_out, saved_acts, weights)
        grad_shards = tuple(lax.psum_scatter(grad_part, AXIS_NAME, scatter_dimension=0, tiled=True) if is_sharded else lax.psum(grad_part, AXIS_NAME) for grad_part, is_sharded in zip(grad_full, SHARDED))
        all_rows = lax.all_gather(grad_x_emb.reshape(-1, model_dim), AXIS_NAME, tiled=True)
        d_table = jax.ops.segment_sum(all_rows, jnp.where(is_owner, local_ids, rows_local), num_segments=rows_local)
        return (layer_out, d_table) + grad_shards

    return jax.shard_map(device_step, mesh=mesh, in_specs=(row_spec, row_spec, row_spec) + weight_specs + (batch_spec,), out_specs=(batch_spec, row_spec) + weight_specs, check_vma=False)
```

profile of v0, /device:TPU:0, one launch (start us, length us, event | category | flops | bytes accessed | tf_op | source)
XLA Modules:
  0.0 1721.7 jit_solution(13429454109751852328)
XLA Ops:
  10.7 8.5 copy.79
  19.2 14.9 all_gather.33
  34.8 84.1 %gather_fusion = bf16[16384,960]{1,0:T(8,128)(2,1)} fusion(bf16[3072,960]{1,0:T(8,128)(2,1)} %copy.79, s32[16384]{0:T(1024)S(1)} %get-tuple-element.94), kind=kCustom, calls=%fused_computation | custom fusion | bytes 62980096 | tf_op jit(solution)/shard_map/jit(_take)/gather | solution.py:148
  118.9 22.7 %select_select_fusion = bf16[16384,960]{1,0:T(8,128)(2,1)} fusion(bf16[16384,960]{1,0:T(8,128)(2,1)} %gather_fusion, pred[16384]{0:T(1024)(128)(4,1)S(1)} %get-tuple-element.96, pred[16384]{0:T(1024)(128)(4,1)S(1)} %get-tuple-element.95), kind=kLoop, calls=%fused_computation.4 | loop fusion | flops 31457280 | bytes 62947328 | tf_op jit(solution)/shard_map/jit(_where)/select_n | solution.py:149
  143.7 32.5 %all-reduce.17 = (bf16[960]{0:T(1024)(128)(2,1)S(1)}, bf16[960]{0:T(1024)(128)(2,1)S(1)}) all-reduce(bf16[960]{0:T(1024)(128)(2,1)S(1)} %dynamic-update-slice, bf16[960]{0:T(1024)(128)(2,1)S(1)} %dynamic-update-slice.1), channel_id=1, replica_groups=mesh['fsdp'=16] {'fsdp'}, use_global_device_ids=true, to_apply=%add | all-reduce | flops 1920 | bytes 7680
  177.5 16.1 all-gather.1
  193.9 15.4 all-gather
  223.7 7.4 reshape.207
  231.1 7.3 reshape.208
  238.4 269.2 %reduce-scatter.15.cloned.1.call-done = bf16[1024,960]{1,0:T(8,128)(2,1)} async-done(((bf16[16384,960]{1,0:T(8,128)(2,1)}), bf16[1024,960]{1,0:T(8,128)(2,1)}) %reduce-scatter.15.cloned.1.call-update) | async-done | bytes 1966096 | tf_op jit(solution)/shard_map/reduce_scatter | solution.py:150
  525.7 19.3 %fusion.96 = (f32[2,5,3,512]{3,2,1,0:T(4,128)}, f32[2,5,3,512,512]{3,4,2,1,0:T(8,128)}) fusion(pred[512,512]{0,1:T(8,128)(4,1)} %iota_compare_fusion, bf16[2,512,5,3,32]{1,4,3,2,0:T(8,128)(2,1)S(1)} %get-tuple-element.80, bf16[2,512,5,3,32]{1,4,3,2,0:T(8,128)(2,1)S(1)} %get-tuple-element.79, bf16[2,512,5,32]{1,3,2,0:T(8,128)(2,1)} %get-tuple-element.88, ...), kind=kOutput, calls=%fused_computation.153 | convolution fusion | flops 1043333632 | bytes 34402304 | tf_op jit(solution)/shard_map/sub | solution.py:44
  545.1 13.1 fusion.53
  558.2 4.8 fusion.38
  563.1 8.6 fusion.91
  571.8 8.8 fusion.93
  580.6 18.8 %multiply_convert_fusion = (bf16[2,512,2560]{2,1,0:T(8,128)(2,1)}, bf16[2,512,2560]{2,1,0:T(8,128)(2,1)}, bf16[2,512,2560]{2,1,0:T(8,128)(2,1)}) fusion(f32[2,512,2560]{2,1,0:T(8,128)} %fusion.93, f32[2,512,2560]{2,1,0:T(8,128)} %fusion.91, bf16[2,512,960]{1,2,0:T(8,128)(2,1)S(1)} %copy-done.12, bf16[2560,960]{1,0:T(8,128)(2,1)} %all-gather.13.cloned.1.call-done), kind=kOutput, calls=%fused_computation.20 | convolution fusion | flops 5075107840 | bytes 43581440 | tf_op jit(solution)/shard_map/bsd,fd->bsf/dot_general | solution.py:102
  599.4 9.0 fusion.97
  608.4 8.7 fusion.37
  622.3 13.4 fusion.63
  635.7 12.5 fusion.98
  648.2 40.6 %fusion.61 = f32[2,512,5,64]{1,3,2,0:T(8,128)S(1)} fusion(f32[2,5,512,512,3]{3,2,4,1,0:T(8,128)} %fusion.98, bf16[2,512,5,3,32]{1,4,3,2,0:T(8,128)(2,1)} %copy-done.44, bf16[2,512,5,3,32]{1,4,3,2,0:T(8,128)(2,1)} %copy-done.43, f32[2,5,3,512,512]{3,4,2,1,0:T(8,128)} %get-tuple-element.101, f32[2,5,3,512]{3,2,1,0:T(4,128)} %get-tuple-element.100), kind=kOutput, calls=%fused_computation.92 | convolution fusion | flops 1065631232 | bytes 66252800 | tf_op jit(solution)/shard_map/bgrqk,bqgrh->bkgh/dot_general | solution.py:58
  688.8 42.1 %fusion.44 = f32[2,512,5,3,64]{1,4,3,2,0:T(8,128)} fusion(f32[2,5,512,512,3]{3,2,4,1,0:T(8,128)} %fusion.98, bf16[2,512,5,32]{1,3,2,0:T(8,128)(2,1)S(1)} %copy-done.50, bf16[2,512,5,32]{1,3,2,0:T(8,128)(2,1)S(1)} %copy-done.49, f32[2,5,3,512,512]{3,4,2,1,0:T(8,128)} %get-tuple-element.101, f32[2,5,3,512]{3,2,1,0:T(4,128)S(1)} %copy-done.80), kind=kOutput, calls=%fused_computation.71 | convolution fusion | flops 1063009792 | bytes 67563520 | tf_op jit(solution)/shard_map/bgrqk,bkgh->bqgrh/dot_general | solution.py:57
  755.2 10.8 convolution_bitcast_fusion
  782.2 8.1 convolution_bitcast_fusion.1
  790.3 8.2 convolution_bitcast_fusion.2
  798.5 606.1 %fusion.95 = (f32[64,960]{1,0:T(8,128)}, f32[64,320]{1,0:T(8,128)S(1)}, f32[64,320]{1,0:T(8,128)S(1)}, f32[64,960]{1,0:T(8,128)}, f32[64,2560]{1,0:T(8,128)}, /*index=5*/f32[64,2560]{1,0:T(8,128)}) fusion(f32[960,960]{1,0:T(8,128)} %convolution_bitcast_fusion.4, f32[960,320]{1,0:T(8,128)} %convolution_bitcast_fusion.6, ...), kind=kCustom, calls=%all-reduce-scatter.6 | all-reduce-scatter fusion | flops 7864321 | bytes 31457280
  1427.5 8.4 fusion.39
  1438.9 34.1 %all-reduce.16 = (f32[960]{0:T(1024)S(1)}, f32[64]{0:T(128)}, f32[64]{0:T(128)}, f32[960]{0:T(1024)S(1)}) all-reduce(f32[960]{0:T(1024)S(1)} %get-tuple-element.52, f32[64]{0:T(128)S(1)} %reduce_sum.153, f32[64]{0:T(128)S(1)} %reduce_sum.156, f32[960]{0:T(1024)S(1)} %copy-done.68), channel_id=3, replica_groups=mesh['fsdp'=16] {'fsdp'}, use_global_device_ids=true, to_apply=%region_14.15.clone | all-reduce | flops 2048 | bytes 16384
  1483.4 5.7 concatenate.28
  1492.0 64.6 %copy.94 = f32[16384,960]{1,0:T(8,128)} copy(f32[16384,960]{0,1:T(8,128)} %all-gather.15.cloned.1.call-done) | data formatting | bytes 125829120 | tf_op jit(solution)/shard_map/all_gather | solution.py:154
  1556.6 145.7 %scatter_custom_fusion = f32[3072,960]{1,0:T(8,128)} fusion(s32[16384]{0:T(1024)} %get-tuple-element.93, f32[16384,960]{1,0:T(8,128)} %copy.94, f32[]{:T(128)} %constant.22.clone.1), kind=kCustom, calls=%fused_computation.29 | custom fusion | flops 15728640 | bytes 11796992 | tf_op jit(solution)/shard_map/scatter-add | solution.py:155
  1702.3 12.3 copy.97
  (311 shorter events, 124.3 us)
Async XLA Ops:
  7.2 204.6 %all-gather.19.cloned.1.call-start = ((), (), s32[]{:S(2)}) async-start(), calls=%async_computation.7 | async-start | bytes 2228224 | tf_op jit(solution)/shard_map/all_gather | solution.py:142
  7.9 209.9 %all-gather.17.cloned.1.call-start = ((), (), s32[]{:S(2)}) async-start(), calls=%async_computation.6 | async-start | bytes 2228224 | tf_op jit(solution)/shard_map/all_gather | solution.py:142
  8.7 215.0 %all-gather.21.cloned.1.call-start = ((), (), s32[]{:S(2)}) async-start(), calls=%async_computation.8 | async-start | bytes 5570560 | tf_op jit(solution)/shard_map/all_gather | solution.py:142
  9.4 221.7 %all-gather.23.cloned.1.call-start = ((), (), s32[]{:S(2)}) async-start(), calls=%async_computation.9 | async-start | bytes 5570560 | tf_op jit(solution)/shard_map/all_gather | solution.py:142
  10.0 497.6 %reduce-scatter.15.cloned.1.call-start = ((), (), s32[]{:S(2)}) async-start(), calls=%async_computation.2 | async-start | bytes 35651584 | tf_op jit(solution)/shard_map/reduce_scatter | solution.py:150
  141.7 52.2 %copy-start.56 = (bf16[60,320]{1,0:T(8,128)(2,1)S(1)}, bf16[60,320]{1,0:T(8,128)(2,1)}, u32[]{:S(2)}) copy-start(bf16[60,320]{1,0:T(8,128)(2,1)} %param.21) | copy-start | bytes 115204
  141.7 438.9 %all-gather.13.cloned.1.call-start = ((), (), s32[]{:S(2)}) async-start(), calls=%async_computation.3 | async-start | bytes 5570560 | tf_op jit(solution)/shard_map/all_gather | solution.py:142
  142.3 1349.7 %all-gather.15.cloned.1.call-start = ((), (), s32[]{:S(2)}) async-start(), calls=%async_computation.4 | async-start | bytes 66846720 | tf_op jit(solution)/shard_map/all_gather | solution.py:154
  143.1 381.0 %copy-start.69 = (f32[64]{0:T(128)}, f32[64]{0:T(128)S(1)}, u32[]{:S(2)}) copy-start(f32[64]{0:T(128)S(1)} %convert_element_type.144) | copy-start | bytes 772
  143.2 379.4 %copy-start.71 = (f32[64]{0:T(128)}, f32[64]{0:T(128)S(1)}, u32[]{:S(2)}) copy-start(f32[64]{0:T(128)S(1)} %convert_element_type.139) | copy-start | bytes 772
  176.1 337.7 %copy-start.51 = (f32[960]{0:T(1024)}, f32[960]{0:T(1024)S(1)}, u32[]{:S(2)}) copy-start(f32[960]{0:T(1024)S(1)} %convert_element_type.133) | copy-start | bytes 11524
  176.1 441.0 %copy-start.59 = (f32[960]{0:T(1024)}, f32[960]{0:T(1024)S(1)}, u32[]{:S(2)}) copy-start(f32[960]{0:T(1024)S(1)} %convert_element_type.150) | copy-start | bytes 11524
  193.9 324.2 %copy-start.23 = (bf16[960,320]{1,0:T(8,128)(2,1)}, bf16[960,320]{1,0:T(8,128)(2,1)S(1)}, u32[]{:S(2)}) copy-start(bf16[960,320]{1,0:T(8,128)(2,1)S(1)} %reshape.192) | copy-start | bytes 1843204
  211.7 313.3 %copy-start.21 = (f32[2,512,32]{1,2,0:T(8,128)}, f32[2,512,32]{1,2,0:T(8,128)S(1)}, u32[]{:S(2)}) copy-start(f32[2,512,32]{1,2,0:T(8,128)S(1)} %get-tuple-element.99) | copy-start | bytes 393220
  525.7 37.4 %slice-start.2 = ((s8[4915200]{0:T(1024)(128)(4,1)}), s8[720896]{0:T(1024)(128)(4,1)S(1)}, s32[]{:S(2)}) async-start(s8[4915200]{0:T(1024)(128)(4,1)} %bitcast.219), calls=%async_computation.12 | async-start | bytes 1441792
  563.1 54.0 %copy-start.61 = (f32[2,512]{1,0:T(2,128)}, f32[2,512]{1,0:T(2,128)S(1)}, u32[]{:S(2)}) copy-start(f32[2,512]{1,0:T(2,128)S(1)} %add_rsqrt_fusion.2) | copy-start | bytes 12292
  648.2 40.6 %copy-start.49 = (bf16[2,512,5,32]{1,3,2,0:T(8,128)(2,1)S(1)}, bf16[2,512,5,32]{1,3,2,0:T(8,128)(2,1)}, u32[]{:S(2)}) copy-start(bf16[2,512,5,32]{1,3,2,0:T(8,128)(2,1)} %get-tuple-element.87) | copy-start | bytes 983044
  648.2 40.6 %copy-start.50 = (bf16[2,512,5,32]{1,3,2,0:T(8,128)(2,1)S(1)}, bf16[2,512,5,32]{1,3,2,0:T(8,128)(2,1)}, u32[]{:S(2)}) copy-start(bf16[2,512,5,32]{1,3,2,0:T(8,128)(2,1)} %get-tuple-element.88) | copy-start | bytes 983044
  648.2 40.6 %copy-start.80 = (f32[2,5,3,512]{3,2,1,0:T(4,128)S(1)}, f32[2,5,3,512]{3,2,1,0:T(4,128)}, u32[]{:S(2)}) copy-start(f32[2,5,3,512]{3,2,1,0:T(4,128)} %get-tuple-element.100) | copy-start | bytes 184324
  688.8 42.1 %copy-start.22 = (f32[2,512,32]{1,2,0:T(8,128)S(1)}, f32[2,512,32]{1,2,0:T(8,128)}, u32[]{:S(2)}) copy-start(f32[2,512,32]{1,2,0:T(8,128)} %copy-done.21) | copy-start | bytes 393220
  688.8 42.1 %copy-start.42 = (f32[2,512,32]{1,2,0:T(8,128)S(1)}, f32[2,512,32]{1,2,0:T(8,128)}, u32[]{:S(2)}) copy-start(f32[2,512,32]{1,2,0:T(8,128)} %get-tuple-element.97) | copy-start | bytes 393220
  754.9 959.7 %reduce-scatter.17.cloned.1.call-start = ((), (), s32[]{:S(2)}) async-start(), calls=%async_computation.5 | async-start | bytes 11141120 | tf_op jit(solution)/shard_map/reduce_scatter | solution.py:153
  1405.8 31.5 %collective-permute-start.2 = (f32[60,320]{1,0:T(8,128)}, f32[60,320]{1,0:T(8,128)}, u32[]{:S(2)}, u32[]{:S(2)}) collective-permute-start(f32[60,320]{1,0:T(8,128)} %slice.44), channel_id=1, source_target_pairs={{0,1},{1,2},{2,3},{3,4},{4,5},{5,6},{6,7},{7,8},{8,9},{9,10},{10,1... | collective-permute-start | bytes 230408
  1407.9 67.5 %collective-permute-start.1 = (f32[60,320]{1,0:T(8,128)}, f32[60,320]{1,0:T(8,128)}, u32[]{:S(2)}, u32[]{:S(2)}) collective-permute-start(f32[60,320]{1,0:T(8,128)} %slice.43), channel_id=1, source_target_pairs={{0,1},{1,2},{2,3},{3,4},{4,5},{5,6},{6,7},{7,8},{8,9},{9,10},{10,1... | collective-permute-start | bytes 230408
  1411.5 66.3 %collective-permute-start.3 = (f32[60,960]{1,0:T(8,128)}, f32[60,960]{1,0:T(8,128)}, u32[]{:S(2)}, u32[]{:S(2)}) collective-permute-start(f32[60,960]{1,0:T(8,128)} %slice.45), channel_id=1, source_target_pairs={{0,1},{1,2},{2,3},{3,4},{4,5},{5,6},{6,7},{7,8},{8,9},{9,10},{10,1... | collective-permute-start | bytes 691208
  1417.5 63.3 %collective-permute-start.5 = (f32[60,2560]{1,0:T(8,128)}, f32[60,2560]{1,0:T(8,128)}, u32[]{:S(2)}, u32[]{:S(2)}) collective-permute-start(f32[60,2560]{1,0:T(8,128)} %slice.47), channel_id=1, source_target_pairs={{0,1},{1,2},{2,3},{3,4},{4,5},{5,6},{6,7},{7,8},{8,9},{9,10},{10,1... | collective-permute-start | bytes 1843208
  1421.5 61.9 %collective-permute-start.4 = (f32[60,2560]{1,0:T(8,128)}, f32[60,2560]{1,0:T(8,128)}, u32[]{:S(2)}, u32[]{:S(2)}) collective-permute-start(f32[60,2560]{1,0:T(8,128)} %slice.46), channel_id=1, source_target_pairs={{0,1},{1,2},{2,3},{3,4},{4,5},{5,6},{6,7},{7,8},{8,9},{9,10},{10,1... | collective-permute-start | bytes 1843208
  1435.8 42.0 %copy-start.29 = (f32[64,960]{1,0:T(8,128)S(1)}, f32[64,960]{1,0:T(8,128)}, u32[]{:S(2)}) copy-start(f32[64,960]{1,0:T(8,128)} %get-tuple-element.71) | copy-start | bytes 737284
  1435.8 43.2 %copy-start.28 = (f32[64,960]{1,0:T(8,128)S(1)}, f32[64,960]{1,0:T(8,128)}, u32[]{:S(2)}) copy-start(f32[64,960]{1,0:T(8,128)} %get-tuple-element.68) | copy-start | bytes 737284
  1435.8 45.0 %copy-start.19 = (f32[64,2560]{1,0:T(8,128)S(1)}, f32[64,2560]{1,0:T(8,128)}, u32[]{:S(2)}) copy-start(f32[64,2560]{1,0:T(8,128)} %get-tuple-element.73) | copy-start | bytes 1966084
  1436.1 47.3 %copy-start.18 = (f32[64,2560]{1,0:T(8,128)S(1)}, f32[64,2560]{1,0:T(8,128)}, u32[]{:S(2)}) copy-start(f32[64,2560]{1,0:T(8,128)} %get-tuple-element.72) | copy-start | bytes 1966084
  1437.4 41.7 %collective-permute-start = (f32[60,960]{1,0:T(8,128)S(1)}, f32[60,960]{1,0:T(8,128)S(1)}, u32[]{:S(2)}, u32[]{:S(2)}) collective-permute-start(f32[60,960]{1,0:T(8,128)S(1)} %slice.42), channel_id=1, source_target_pairs={{0,1},{1,2},{2,3},{3,4},{4,5},{5,6},{6,7},{7,8},{8,9},{9,10},{10,1... | collective-permute-start | bytes 691208
  (73 other events, 448.8 us)
Sparse Core Ops, SparseCore 0:
  10.2 31.3 all-gather.18
  43.9 28.2 all-gather.16
  74.5 38.3 all-gather.20
  115.0 38.8 all-gather.22
  156.0 351.5 reduce-scatter.14
  509.7 36.6 all-gather.12
  755.1 390.2 all-gather.14
  1148.2 220.2 reduce-scatter.16
where the time goes:
time: 1730 us; the launch traced here: 1720 us
  blocking collectives  719 us (42%)
  waiting for transfers between devices  272 us (16%)
  matrix products  263 us (15%)
  local copies, waits for them, and re-layouts  240 us (14%)
  other arithmetic  197 us (11%)
    unnamed x3, blocking collectives  673 us
    reduce_scatter x1, waiting for transfers between devices, device_step(): lax.psum_scatter(picked, AXIS_NAME, scatter_dimension=0, tiled=True)  269 us
    scatter-add x1, other arithmetic, device_step(): jax.ops.segment_sum(all_rows, jnp.where(is_owner, local_ids, rows_local),...  146 us
    gather x1, local copies, waits for them, and re-layouts, device_step(): jnp.take(table_shard, jnp.clip(local_ids, 0, rows_local - 1), axis=0)  84.1 us
    unnamed x217, local copies, waits for them, and re-layouts  83.7 us
    all_gather x1, local copies, waits for them, and re-layouts, device_step(): lax.all_gather(grad_x_emb.reshape(-1, model_dim), AXIS_NAME, tiled=True)  64.6 us
    dot_general x1, matrix products, attn_bwd(): jnp.einsum('bgrqk,bkgh->bqgrh', scores_b, k_rot, preferred_element_type=j...  42.1 us
    dot_general x1, matrix products, attn_bwd(): jnp.einsum('bgrqk,bqgrh->bkgh', scores_b, q_rot, preferred_element_type=j...  40.6 us
  transfers between devices with their start and end apart: 14, of which 1 were waited for; matrix products, arithmetic and copies ran while one was open for 66% of the time, Pallas kernels for 0%

commit v1 on v0

v1 whole, which is shorter than its diff:
```python
import math
import jax
import jax.numpy as jnp
from jax import lax
from jax.experimental import pallas as pl
from jax.experimental.pallas import tpu as pltpu
from jax.sharding import PartitionSpec as P

NORM_EPS = 1e-6
ROPE_THETA = 1.0e6
AXIS_NAME = 'fsdp'
D = 960
DP = 1024
SHARDS = 16
SUB = 60
SUBP = 64
QKVP = 1920
FF = 2560
ROWS_FF = 160
MESH_ID = pl.DeviceIdType.MESH
BITS = {'z': 8, 'y': 4, 'x': 2, 'c': 1}
AG_PIECES = ((0, 0, 896, 'xyz'), (0, 896, 1024, 'yzx'), (1, 0, DP, 'zxy'), (2, 0, FF, 'xyz'), (3, 0, FF, 'yzx'), (4, 0, DP, 'zxy'))
RS_PIECES = AG_PIECES[3:] + AG_PIECES[:3] + ((5, 0, 128, 'yzx'),)
ROW_PIECES = tuple((0, half + lo, count, order) for half in (0, 512) for lo, count, order in ((0, 176, 'xyz'), (176, 176, 'yzx'), (352, 160, 'zxy')))
ROWS = (SUBP, SUBP, SUBP, SUBP, ROWS_FF, SUBP)
COLS = (QKVP, DP, FF, FF, DP, 128)
TOKS = 1024
ROWS_TABLE = 3072
UNROLL = 8
HEADS, KV_HEADS, GROUP, HEAD, SEQ, HALF = 15, 5, 3, 64, 512, 256
GROUP_IN = 384
GROUP_OUT = 256
MIB = 1024 * 1024
FIRST_ORDER = (3, 7, 5, 1, 2, 6, 4, 0)
ANY_SPEC = pl.BlockSpec(memory_space=pl.ANY)
VMEM_SPEC = pl.BlockSpec(memory_space=pltpu.VMEM)
HOPS = ((0, 0), (0, 2), (0, 4), (0, 6), (1, 0), (1, 4), (2, 0))


def own_bits():
    me = lax.axis_index(AXIS_NAME)
    return {'z': me // 8, 'y': (me // 4) % 2, 'x': (me // 2) % 2, 'c': me % 2}


def device_at(bits, flips):
    total = 0
    for name, weight in BITS.items():
        total = total + ((1 - bits[name]) if name in flips else bits[name]) * weight
    return total


def flips_of(code, order):
    return ''.join(order[i] for i in range(3) if (code >> i) & 1)


def greet(bits):
    barrier = pltpu.get_barrier_semaphore()
    for name in BITS:
        pl.semaphore_signal(barrier, inc=1, device_id=(device_at(bits, name),), device_id_type=MESH_ID)
    pl.semaphore_wait(barrier, 4)


class Doubling:
    def __init__(self, bits, pieces, ins, outs, view, send_sem, recv_sem):
        self.bits, self.pieces, self.ins, self.outs, self.view = bits, pieces, ins, outs, view
        self.send_sem, self.recv_sem = send_sem, recv_sem
        self.started = []

    def begin(self, p, code, step, src_code):
        piece = self.pieces[p]
        a, order = piece[0], piece[3]
        shard = device_at(self.bits, flips_of(src_code, order))
        src = self.ins[a] if src_code == 0 else self.outs[a].at[shard]
        target = device_at(self.bits, 'c' if step == 3 else order[step])
        slot = 8 + src_code if step == 3 else code
        desc = pltpu.make_async_remote_copy(
            src_ref=self.view(src, piece), dst_ref=self.view(self.outs[a].at[shard], piece),
            send_sem=self.send_sem.at[p, slot], recv_sem=self.recv_sem.at[p, slot],
            device_id=(target,), device_id_type=MESH_ID)
        desc.start()
        self.started.append(desc)

    def arrived(self, p, slot):
        piece = self.pieces[p]
        flips = flips_of(slot % 8, piece[3]) + ('c' if slot >= 8 else '')
        dst = self.view(self.outs[piece[0]].at[device_at(self.bits, flips)], piece)
        pltpu.make_async_remote_copy(
            src_ref=dst, dst_ref=dst, send_sem=self.send_sem.at[p, slot], recv_sem=self.recv_sem.at[p, slot],
            device_id=(device_at(self.bits, 'c'),), device_id_type=MESH_ID).wait_recv()

    def open(self):
        for step in range(3):
            for p in range(len(self.pieces)):
                self.begin(p, 1 << step, step, 0)
        for p in range(len(self.pieces)):
            self.begin(p, 0, 3, 0)

    def forward(self, code):
        top = 0 if code == 1 else (1 if code < 4 else 2)
        for p in range(len(self.pieces)):
            self.arrived(p, code)
            for step in range(top + 1, 3):
                self.begin(p, code | (1 << step), step, code)
            self.begin(p, 0, 3, code)

    def close(self):
        for code in range(8):
            for p in range(len(self.pieces)):
                self.arrived(p, 8 + code)
        for desc in self.started:
            desc.wait_send()


def columns_of(ref, piece):
    return ref.at[:, pl.ds(piece[1], piece[2])]


def rows_of(ref, piece):
    return ref.at[pl.ds(piece[1], piece[2])]


class Halving:
    def __init__(self, bits, pieces, source, acc, got, send_sem, recv_sem):
        self.bits, self.pieces, self.source, self.acc, self.got = bits, pieces, source, acc, got
        self.send_sem, self.recv_sem = send_sem, recv_sem

    def cross(self, p, code):
        return pltpu.make_async_remote_copy(
            src_ref=self.source(p, code), dst_ref=self.acc[p].at[code],
            send_sem=self.send_sem.at[p, code], recv_sem=self.recv_sem.at[p, code],
            device_id=(device_at(self.bits, 'c'),), device_id_type=MESH_ID)

    def hop(self, p, step, code):
        sem = UNROLL + HOPS.index((step, code))
        return pltpu.make_async_remote_copy(
            src_ref=self.acc[p].at[code | (1 << step)], dst_ref=self.got[step][p].at[code >> (step + 1)],
            send_sem=self.send_sem.at[p, sem], recv_sem=self.recv_sem.at[p, sem],
            device_id=(device_at(self.bits, self.pieces[p][3][step]),), device_id_type=MESH_ID)

    def total(self, p, code, at, steps):
        total = self.acc[p][code, at]
        for step in steps:
            total = total + self.got[step][p][code >> (step + 1), at]
        return total

    def add(self, p, code, steps, put=None):
        for step in steps:
            self.hop(p, step, code).wait_recv()

        def chunk(i, carry):
            at = pl.ds(pl.multiple_of(i * UNROLL, UNROLL), UNROLL)
            total = self.total(p, code, at, steps)
            if put is None:
                self.acc[p][code, at] = total
            else:
                put(p, at, total)
            return carry

        lax.fori_loop(0, self.acc[p].shape[1] // UNROLL, chunk, 0)

    def first(self, fill):
        for n, code in enumerate(FIRST_ORDER):
            for p in range(len(self.pieces)):
                self.cross(p, code).wait_recv()
                fill(p, n, code)
                if code & 1:
                    self.hop(p, 0, code - 1).start()

    def rest(self, put):
        pieces = range(len(self.pieces))
        for code in (2, 6):
            for p in pieces:
                self.add(p, code, (0,))
                self.hop(p, 1, code - 2).start()
        for p in pieces:
            self.add(p, 4, (0, 1))
            self.hop(p, 2, 0).start()
        for p in pieces:
            self.add(p, 0, (0, 1, 2), put)
        for p in pieces:
            for code in FIRST_ORDER:
                self.cross(p, code).wait_send()
            for step, code in HOPS:
                self.hop(p, step, code).wait_send()


def columns_of(ref, piece):
    return ref.at[:, pl.ds(piece[1], piece[2])]


def rows_of(ref, piece):
    return ref.at[pl.ds(piece[1], piece[2])]


def sems(count):
    return [pltpu.SemaphoreType.DMA((count, 16))] * 2


def cost(gflops):
    return pl.CostEstimate(flops=gflops * 10 ** 9, bytes_accessed=10 ** 8, transcendentals=0)


def front_body(*refs):
    num = 5
    np_ = len(ROW_PIECES)
    where_ref, table_ref, *refs = refs
    ins, outs, x_ref, stage, rest = refs[:num], refs[num:2 * num], refs[2 * num], refs[2 * num + 1:3 * num + 1], refs[3 * num + 1:]
    away, acc, *got = (rest[i * np_:(i + 1) * np_] for i in range(num))
    w_send, w_recv, load_sem, store_sem, x_send, x_recv = rest[num * np_:]
    bits = own_bits()
    pieces = range(np_)
    loads = [pltpu.make_async_copy(ins[a], stage[a], load_sem.at[a]) for a in range(num)]
    stores = [pltpu.make_async_copy(stage[a], outs[a].at[device_at(bits, '')], store_sem.at[a]) for a in range(num)]
    for load in loads:
        load.start()
    greet(bits)
    ring = Doubling(bits, AG_PIECES, ins, outs, columns_of, w_send, w_recv)
    ring.open()
    tree = Halving(bits, ROW_PIECES, lambda p, code: away[p].at[code], acc, got, x_send, x_recv)

    def pick(p, code, other):
        first, count, order = ROW_PIECES[p][1:]
        base = device_at(bits, flips_of(code, order) + ('c' if other else '')) * TOKS + first

        def step(i, carry):
            for k in range(UNROLL):
                t = i * UNROLL + k
                row = table_ref[where_ref[base + t]]
                if other:
                    away[p][code, t] = row
                else:
                    acc[p][code, t] = acc[p][code, t] + row
            return carry

        lax.fori_loop(0, count // UNROLL, step, 0)

    for code in FIRST_ORDER:
        for p in pieces:
            pick(p, code, True)
            tree.cross(p, code).start()
    for load, store in zip(loads, stores):
        load.wait()
        store.start()
    for code in range(1, 4):
        ring.forward(code)
    tree.first(lambda p, n, code: pick(p, code, False))
    for code in range(4, UNROLL):
        ring.forward(code)

    def put(p, at, total):
        x_ref[pl.ds(ROW_PIECES[p][1] + at.start, UNROLL)] = total

    tree.rest(put)
    ring.close()
    for store in stores:
        store.wait()


def front(where, table, shards):
    num = len(shards)
    scratch = [pltpu.VMEM((ROWS[a], COLS[a]), jnp.bfloat16) for a in range(num)]
    for lead in (8, 8, 4, 2, 1):
        scratch += [pltpu.VMEM((lead, piece[2], 8, 128), jnp.bfloat16) for piece in ROW_PIECES]
    scratch += sems(len(AG_PIECES)) + [pltpu.SemaphoreType.DMA((num,))] * 2 + sems(len(ROW_PIECES))
    return pl.pallas_call(
        front_body,
        out_shape=tuple(jax.ShapeDtypeStruct((SHARDS, ROWS[a], COLS[a]), jnp.bfloat16) for a in range(num)) + (jax.ShapeDtypeStruct((TOKS, 8, 128), jnp.bfloat16),),
        in_specs=[pl.BlockSpec(memory_space=pltpu.SMEM), VMEM_SPEC] + [ANY_SPEC] * num,
        out_specs=(ANY_SPEC,) * num + (VMEM_SPEC,),
        scratch_shapes=scratch,
        compiler_params=pltpu.CompilerParams(collective_id=1, has_side_effects=True, vmem_limit_bytes=63 * MIB),
        cost_estimate=cost(60),
        name='front',
    )(where, table, *shards)


def rows_body(in_ref, out_ref, stage, send_sem, recv_sem, own_sem):
    bits = own_bits()
    load = pltpu.make_async_copy(in_ref, stage, own_sem.at[0])
    load.start()
    greet(bits)
    ring = Doubling(bits, ROW_PIECES, (in_ref,), (out_ref,), rows_of, send_sem, recv_sem)
    ring.open()
    load.wait()
    store = pltpu.make_async_copy(stage, out_ref.at[device_at(bits, '')], own_sem.at[1])
    store.start()
    for code in range(1, UNROLL):
        ring.forward(code)
    ring.close()
    store.wait()


def gather_rows(rows):
    return pl.pallas_call(
        rows_body,
        out_shape=jax.ShapeDtypeStruct((SHARDS, TOKS, 8, 128), jnp.float32),
        in_specs=[ANY_SPEC],
        out_specs=ANY_SPEC,
        scratch_shapes=[pltpu.VMEM((TOKS, 8, 128), jnp.float32)] + sems(len(ROW_PIECES)) + [pltpu.SemaphoreType.DMA((2,))],
        compiler_params=pltpu.CompilerParams(collective_id=3, has_side_effects=True),
        cost_estimate=cost(80),
        name='gather_rows',
    )(rows)


def scatter_body(*refs):
    num = len(ROWS)
    np_ = len(RS_PIECES)
    ins, outs, rest = refs[:num], refs[num:2 * num], refs[2 * num:]
    acc, own, *got = (rest[i * np_:(i + 1) * np_] for i in range(5))
    send_sem, recv_sem, own_sem = rest[5 * np_:]
    bits = own_bits()
    pieces = range(np_)

    def part(p, code, flips):
        shard = device_at(bits, flips_of(code, RS_PIECES[p][3]) + flips)
        return columns_of(ins[RS_PIECES[p][0]].at[shard], RS_PIECES[p])

    tree = Halving(bits, RS_PIECES, lambda p, code: part(p, code, 'c'), acc, got, send_sem, recv_sem)

    def own_copy(p, n):
        return pltpu.make_async_copy(part(p, FIRST_ORDER[n], ''), own[p].at[n % 2], own_sem.at[p, n % 2])

    for p in pieces:
        own_copy(p, 0).start()
        own_copy(p, 1).start()
    greet(bits)
    for code in FIRST_ORDER:
        for p in pieces:
            tree.cross(p, code).start()

    def fill(p, n, code):
        own_copy(p, n).wait()

        def chunk(i, carry):
            at = pl.ds(pl.multiple_of(i * UNROLL, UNROLL), UNROLL)
            acc[p][code, at] = acc[p][code, at] + own[p][n % 2, at]
            return carry

        lax.fori_loop(0, acc[p].shape[1] // UNROLL, chunk, 0)
        if n + 2 < len(FIRST_ORDER):
            own_copy(p, n + 2).start()

    def put(p, at, total):
        a, first, cols, order = RS_PIECES[p]
        outs[a][at, pl.ds(first, cols)] = total

    tree.first(fill)
    tree.rest(put)


def scatter_grads(parts):
    num = len(ROWS)
    np_ = len(RS_PIECES)
    scratch = []
    for lead in (8, 2, 4, 2, 1):
        scratch += [pltpu.VMEM((lead, ROWS[piece[0]], piece[2]), jnp.float32) for piece in RS_PIECES]
    scratch += sems(np_) + [pltpu.SemaphoreType.DMA((np_, 2))]
    return pl.pallas_call(
        scatter_body,
        out_shape=tuple(jax.ShapeDtypeStruct(shape, jnp.float32) for shape in zip(ROWS, COLS)),
        in_specs=[ANY_SPEC] * num,
        out_specs=(VMEM_SPEC,) * num,
        scratch_shapes=scratch,
        compiler_params=pltpu.CompilerParams(collective_id=2, has_side_effects=True, vmem_limit_bytes=60 * MIB),
        cost_estimate=cost(60),
        name='scatter_grads',
    )(*parts)


def spread_matrix():
    src = lax.broadcasted_iota(jnp.int32, (D, DP), 0)
    dst = lax.broadcasted_iota(jnp.int32, (D, DP), 1)
    return ((src // SUB) * SUBP + src % SUB == dst).astype(jnp.bfloat16)


def heads_matrix():
    src = lax.broadcasted_iota(jnp.int32, (KV_HEADS * GROUP_OUT, DP), 0)
    dst = lax.broadcasted_iota(jnp.int32, (KV_HEADS * GROUP_OUT, DP), 1)
    lane = src % GROUP_OUT
    feature = (src // GROUP_OUT) * GROUP * HEAD + lane
    return ((lane < GROUP * HEAD) & ((feature // SUB) * SUBP + feature % SUB == dst)).astype(jnp.bfloat16)


def matmul(spec, lhs, rhs):
    return jnp.einsum(spec, lhs, rhs, preferred_element_type=jnp.float32)


def spread(values, matrix):
    return matmul('...d,de->...e', values, matrix).astype(jnp.bfloat16)


def gather_back(values, matrix):
    return matmul('...e,de->...d', values, matrix).astype(jnp.bfloat16)


def unspread_columns(values):
    rows = values.shape[0]
    return values.reshape(rows, SHARDS, SUBP)[:, :, :SUB].reshape(rows, D)


def merge_groups(w_query, w_key, w_value, gains):
    parts = []
    for g in range(KV_HEADS):
        at = slice(g * HEAD, (g + 1) * HEAD)
        spare = jnp.pad(gains if g == 0 else gains[:, :0], ((0, 0), (0, HEAD - (2 if g == 0 else 0))))
        parts += [w_query[:, g * GROUP * HEAD:(g + 1) * GROUP * HEAD], w_key[:, at], w_value[:, at], spare]
    return jnp.concatenate(parts, axis=1)


def split_groups(merged):
    grouped = merged.reshape(merged.shape[0], KV_HEADS, GROUP_IN)
    edges = (0, GROUP * HEAD, (GROUP + 1) * HEAD, (GROUP + 2) * HEAD)
    return tuple(grouped[:, :, lo:hi].reshape(merged.shape[0], -1) for lo, hi in zip(edges, edges[1:]))


def sort_by_owner(tok):
    owner = tok // ROWS_TABLE
    onehot = (owner[:, None] == jnp.arange(SHARDS, dtype=jnp.int32)[None, :]).astype(jnp.bfloat16)
    row = lax.broadcasted_iota(jnp.int32, (TOKS, TOKS), 0)
    col = lax.broadcasted_iota(jnp.int32, (TOKS, TOKS), 1)
    rank = jnp.dot((row > col).astype(jnp.bfloat16), onehot, preferred_element_type=jnp.float32)
    count = jnp.sum(onehot.astype(jnp.float32), axis=0)
    before = lax.broadcasted_iota(jnp.int32, (SHARDS, SHARDS), 0) < lax.broadcasted_iota(jnp.int32, (SHARDS, SHARDS), 1)
    first = jnp.sum(jnp.where(before, count[:, None], 0.0), axis=0)
    place = jnp.sum(onehot.astype(jnp.float32) * (rank + first[None, :]), axis=1).astype(jnp.int32)
    order_m = (row == place[None, :]).astype(jnp.bfloat16)
    local = tok - owner * ROWS_TABLE
    halves = jnp.stack([local // 64, local % 64], axis=-1).astype(jnp.bfloat16)
    halves = jnp.dot(order_m, halves, preferred_element_type=jnp.float32).astype(jnp.int32)
    return place, halves[:, 0] * 64 + halves[:, 1], count.astype(jnp.int32), first.astype(jnp.int32)


def order_body(place_ref, in_ref, out_ref):
    def step(i, carry):
        for k in range(UNROLL):
            t = i * UNROLL + k
            out_ref[place_ref[t]] = in_ref[t]
        return carry

    lax.fori_loop(0, TOKS // UNROLL, step, 0)


def order_rows(place, rows):
    whole = pl.BlockSpec((TOKS, 8, 128), lambda i, *_: (0, 0, 0))
    return pl.pallas_call(
        order_body,
        grid_spec=pltpu.PrefetchScalarGridSpec(num_scalar_prefetch=1, grid=(1,), in_specs=[whole], out_specs=whole),
        out_shape=jax.ShapeDtypeStruct((TOKS, 8, 128), jnp.float32),
        compiler_params=pltpu.CompilerParams(vmem_limit_bytes=40 * MIB),
        name='order_rows',
    )(place, rows)


def add_body(ids_ref, first_ref, count_ref, in_ref, out_ref, acc0, acc1):
    j = pl.program_id(0)
    first = first_ref[j]
    count = count_ref[j]
    zero = jnp.zeros((UNROLL, 8, 128), jnp.float32)

    @pl.when(j == 0)
    def _():
        def clear(i, carry):
            at = pl.ds(i * UNROLL, UNROLL)
            acc0[at] = zero
            acc1[at] = zero
            return carry

        lax.fori_loop(0, ROWS_TABLE // UNROLL, clear, 0)

    def step(i, carry):
        for k in range(4):
            at = first + i * 8 + 2 * k
            r0 = ids_ref[j * TOKS + at]
            r1 = ids_ref[j * TOKS + at + 1]
            acc0[r0] = acc0[r0] + in_ref[at]
            acc1[r1] = acc1[r1] + in_ref[at + 1]
        return carry

    lax.fori_loop(0, count // 8, step, 0)

    def tail(i, carry):
        r = ids_ref[j * TOKS + first + i]
        acc0[r] = acc0[r] + in_ref[first + i]
        return carry

    lax.fori_loop((count // 8) * 8, count, tail, 0)

    @pl.when(j == SHARDS - 1)
    def _():
        def flush(i, carry):
            for part in range(UNROLL):
                at = pl.ds(pl.multiple_of((i * UNROLL + part) * 8, 8), 8)
                for k in range(8):
                    both = acc0[at, k, :] + acc1[at, k, :]
                    for half in range(2):
                        out_ref[at, pl.ds((2 * k + half) * SUB, SUB)] = both[:, half * SUBP:half * SUBP + SUB]
            return carry

        lax.fori_loop(0, ROWS_TABLE // 8 // UNROLL, flush, 0)


def add_rows(ids, first, count, rows):
    return pl.pallas_call(
        add_body,
        grid_spec=pltpu.PrefetchScalarGridSpec(
            num_scalar_prefetch=3, grid=(SHARDS,),
            in_specs=[pl.BlockSpec((TOKS, 8, 128), lambda j, *_: (j, 0, 0))],
            out_specs=pl.BlockSpec((ROWS_TABLE, D), lambda j, *_: (0, 0)),
            scratch_shapes=[pltpu.VMEM((ROWS_TABLE, 8, 128), jnp.float32)] * 2),
        out_shape=jax.ShapeDtypeStruct((ROWS_TABLE, D), jnp.float32),
        compiler_params=pltpu.CompilerParams(vmem_limit_bytes=60 * MIB),
        name='add_rows',
    )(ids, first, count, rows)


def rope_tables(positions):
    half_dim = HEAD // 2
    inv_freq = jnp.exp(jnp.arange(half_dim, dtype=jnp.float32) * (-2.0 * math.log(ROPE_THETA) / HEAD))
    angles = positions.astype(jnp.float32)[:, :, None] * inv_freq
    cos_t, sin_t = jnp.cos(angles), jnp.sin(angles)
    return jnp.concatenate([cos_t, cos_t], axis=-1), jnp.concatenate([-sin_t, sin_t], axis=-1)


def swap_halves(values):
    half_dim = HEAD // 2
    return jnp.concatenate([values[:, half_dim:], values[:, :half_dim]], axis=-1)


def norm_fwd(values, width=HEAD):
    values_f = values.astype(jnp.float32)
    inv_rms = lax.rsqrt(jnp.sum(values_f * values_f, axis=-1, keepdims=True) * (1.0 / width) + NORM_EPS)
    return values_f * inv_rms, inv_rms


def norm_bwd(grad_out, normed, inv_rms, norm_gain, width=HEAD):
    grad_normed = grad_out * norm_gain.astype(jnp.float32)
    mean_term = jnp.sum(grad_normed * normed, axis=-1, keepdims=True) * (1.0 / width)
    return inv_rms * (grad_normed - normed * mean_term)


def rope_fwd(normed, gain, cos_w, sin_w):
    scaled = normed * gain
    return (scaled * cos_w + swap_halves(scaled) * sin_w).astype(jnp.bfloat16)


def dot_nt(lhs, rhs):
    return lax.dot_general(lhs, rhs, (((1,), (1,)), ((), ())), preferred_element_type=jnp.float32)


def dot_nn(lhs, rhs):
    return lax.dot_general(lhs, rhs, (((1,), (0,)), ((), ())), preferred_element_type=jnp.float32)


def dot_tn(lhs, rhs):
    return lax.dot_general(lhs, rhs, (((0,), (0,)), ((), ())), preferred_element_type=jnp.float32)


def mask_last(scores, axis):
    split = scores.shape[axis] - HALF
    key = lax.broadcasted_iota(jnp.int32, (HALF, HALF), axis)
    query = lax.broadcasted_iota(jnp.int32, (HALF, HALF), 1 - axis)
    last = jnp.where(key <= query, lax.slice_in_dim(scores, split, split + HALF, axis=axis), -1e30)
    if split == 0:
        return last
    return jnp.concatenate([lax.slice_in_dim(scores, 0, split, axis=axis), last], axis=axis)


def softmax_of(scores, axis):
    scores = mask_last(scores * (HEAD ** -0.5), axis)
    weights = jnp.exp(scores - jnp.max(scores, axis=axis, keepdims=True))
    return weights * (1.0 / jnp.sum(weights, axis=axis, keepdims=True))


def head_of(ref, h):
    return ref[0, :, h * HEAD:(h + 1) * HEAD]


def attn_fwd_body(qkv_ref, cos_ref, sin_ref, gq_ref, gk_ref, o_ref):
    cos_w, sin_w = cos_ref[0], sin_ref[0]
    k_rot = rope_fwd(norm_fwd(head_of(qkv_ref, GROUP))[0], gk_ref[...], cos_w, sin_w)
    v_raw = head_of(qkv_ref, GROUP + 1)
    for r in range(GROUP):
        at = slice(r * HEAD, (r + 1) * HEAD)
        q_rot = rope_fwd(norm_fwd(head_of(qkv_ref, r))[0], gq_ref[...], cos_w, sin_w)
        for lo in range(0, SEQ, HALF):
            hi = lo + HALF
            probs = softmax_of(dot_nt(k_rot[:hi], q_rot[lo:hi]), 0)
            o_ref[0, lo:hi, at] = dot_tn(probs.astype(jnp.bfloat16), v_raw[:hi]).astype(jnp.bfloat16)
    o_ref[0, :, GROUP * HEAD:] = jnp.zeros((SEQ, HEAD), jnp.bfloat16)


def attn_bwd_body(qkv_ref, cos_ref, sin_ref, gq_ref, gk_ref, do_ref, d_ref, dgq_ref, dgk_ref, dq_acc, dk_acc, dv_acc):
    cos_w, sin_w = cos_ref[0], sin_ref[0]
    gain_q, gain_k = gq_ref[...], gk_ref[...]
    k_normed, k_inv = norm_fwd(head_of(qkv_ref, GROUP))
    k_rot = rope_fwd(k_normed, gain_k, cos_w, sin_w)
    v_raw = head_of(qkv_ref, GROUP + 1)
    dk_acc[...] = jnp.zeros_like(dk_acc)
    dv_acc[...] = jnp.zeros_like(dv_acc)
    gain_total = jnp.zeros((1, HEAD), jnp.float32)
    for r in range(GROUP):
        q_normed, q_inv = norm_fwd(head_of(qkv_ref, r))
        q_rot = rope_fwd(q_normed, gain_q, cos_w, sin_w)
        head_grad = head_of(do_ref, r)
        for lo in range(0, SEQ, HALF):
            hi = lo + HALF
            out_grad = head_grad[lo:hi]
            q_part = q_rot[lo:hi]
            probs = softmax_of(dot_nt(k_rot[:hi], q_part), 0)
            grad_probs = dot_nt(v_raw[:hi], out_grad)
            dv_acc[:hi] += dot_nn(probs.astype(jnp.bfloat16), out_grad)
            delta = jnp.sum(grad_probs * probs, axis=0, keepdims=True)
            grad_scores = (probs * (grad_probs - delta) * (HEAD ** -0.5)).astype(jnp.bfloat16)
            dk_acc[:hi] += dot_nn(grad_scores, q_part)
            dq_acc[lo:hi] = dot_tn(grad_scores, k_rot[:hi])
        grad_q = dq_acc[...]
        grad_q = grad_q * cos_w - swap_halves(grad_q) * sin_w
        gain_total = gain_total + jnp.sum(grad_q * q_normed, axis=0, keepdims=True)
        d_ref[0, :, r * HEAD:(r + 1) * HEAD] = norm_bwd(grad_q, q_normed, q_inv, gain_q).astype(jnp.bfloat16)
    grad_k = dk_acc[...]
    grad_k = grad_k * cos_w - swap_halves(grad_k) * sin_w
    dgq_ref[0, 0] = gain_total
    dgk_ref[0, 0] = jnp.sum(grad_k * k_normed, axis=0, keepdims=True)
    d_ref[0, :, GROUP * HEAD:(GROUP + 1) * HEAD] = norm_bwd(grad_k, k_normed, k_inv, gain_k).astype(jnp.bfloat16)
    d_ref[0, :, (GROUP + 1) * HEAD:] = jnp.concatenate([dv_acc[...], jnp.zeros((SEQ, HEAD), jnp.float32)], axis=-1).astype(jnp.bfloat16)


def attn_specs():
    def lanes(width):
        return pl.BlockSpec((1, SEQ, width), lambda b, g: (b, 0, g))

    table = pl.BlockSpec((1, SEQ, HEAD), lambda b, g: (b, 0, 0))
    gain = pl.BlockSpec((1, HEAD), lambda b, g: (0, 0))
    return lanes, [lanes(GROUP_IN), table, table, gain, gain]


def attn_fwd(qkv, *tables):
    batch_len = qkv.shape[0]
    lanes, specs = attn_specs()
    return pl.pallas_call(
        attn_fwd_body,
        grid=(batch_len, KV_HEADS),
        out_shape=jax.ShapeDtypeStruct((batch_len, SEQ, KV_HEADS * GROUP_OUT), jnp.bfloat16),
        in_specs=specs,
        out_specs=lanes(GROUP_OUT),
        compiler_params=pltpu.CompilerParams(vmem_limit_bytes=40 * MIB),
        cost_estimate=cost(8),
        name='attn_fwd',
    )(qkv, *tables)


def attn_bwd(qkv, *tables):
    batch_len = qkv.shape[0]
    lanes, specs = attn_specs()
    gain_out = pl.BlockSpec((1, 1, 1, HEAD), lambda b, g: (b, g, 0, 0))
    gain_shape = jax.ShapeDtypeStruct((batch_len, KV_HEADS, 1, HEAD), jnp.float32)
    return pl.pallas_call(
        attn_bwd_body,
        grid=(batch_len, KV_HEADS),
        out_shape=(jax.ShapeDtypeStruct(qkv.shape, jnp.bfloat16), gain_shape, gain_shape),
        in_specs=specs + [lanes(GROUP_OUT)],
        out_specs=(lanes(GROUP_IN), gain_out, gain_out),
        scratch_shapes=[pltpu.VMEM((SEQ, HEAD), jnp.float32)] * 3,
        compiler_params=pltpu.CompilerParams(vmem_limit_bytes=40 * MIB),
        cost_estimate=cost(16),
        name='attn_bwd',
    )(qkv, *tables)


def layer_fwd(x_emb, positions, weights):
    attn_norm, w_qkv, q_norm, k_norm, w_out, mlp_norm, w_gate, w_up, w_down = weights
    cos_w, sin_w = rope_tables(positions)
    gain_q = q_norm.astype(jnp.float32)[None, :]
    gain_k = k_norm.astype(jnp.float32)[None, :]
    normed1, norm1_inv = norm_fwd(x_emb, D)
    attn_in = (normed1 * attn_norm.astype(jnp.float32)).astype(jnp.bfloat16)
    attn_args = (matmul('bsd,dn->bsn', attn_in, w_qkv).astype(jnp.bfloat16), cos_w, sin_w, gain_q, gain_k)
    attn_flat = spread(attn_fwd(*attn_args), heads_matrix())
    hidden = (x_emb.astype(jnp.float32) + matmul('bsn,nd->bsd', attn_flat, w_out)).astype(jnp.bfloat16)
    normed2, norm2_inv = norm_fwd(hidden, D)
    mlp_in = (normed2 * mlp_norm.astype(jnp.float32)).astype(jnp.bfloat16)
    gate_pre = matmul('bsd,df->bsf', mlp_in, w_gate)
    up_proj = matmul('bsd,df->bsf', mlp_in, w_up)
    mlp_act = (jax.nn.silu(gate_pre) * up_proj).astype(jnp.bfloat16)
    layer_out = (hidden.astype(jnp.float32) + matmul('bsf,fd->bsd', mlp_act, w_down)).astype(jnp.bfloat16)
    return layer_out, (normed1, norm1_inv, attn_in, attn_args, attn_flat, normed2, norm2_inv, mlp_in, gate_pre, up_proj, mlp_act)


def layer_bwd(dy_out, saved_acts, weights):
    attn_norm, w_qkv, q_norm, k_norm, w_out, mlp_norm, w_gate, w_up, w_down = weights
    normed1, norm1_inv, attn_in, attn_args, attn_flat, normed2, norm2_inv, mlp_in, gate_pre, up_proj, mlp_act = saved_acts
    grad_w_down = matmul('bsf,bsd->fd', mlp_act, dy_out)
    grad_act = matmul('bsd,fd->bsf', dy_out, w_down)
    gate_sig = jax.nn.sigmoid(gate_pre)
    grad_gate = (grad_act * up_proj * gate_sig * (1.0 + gate_pre * (1.0 - gate_sig))).astype(jnp.bfloat16)
    grad_up = (grad_act * gate_pre * gate_sig).astype(jnp.bfloat16)
    grad_w_gate = matmul('bsd,bsf->df', mlp_in, grad_gate)
    grad_w_up = matmul('bsd,bsf->df', mlp_in, grad_up)
    grad_mlp_in = matmul('bsf,df->bsd', grad_gate, w_gate) + matmul('bsf,df->bsd', grad_up, w_up)
    grad_mlp_norm = jnp.sum(grad_mlp_in * normed2, axis=(0, 1))
    grad_hidden = dy_out.astype(jnp.float32) + norm_bwd(grad_mlp_in, normed2, norm2_inv, mlp_norm, D)
    hidden_b = grad_hidden.astype(jnp.bfloat16)
    grad_w_out = matmul('bsn,bsd->nd', attn_flat, hidden_b)
    grad_heads = gather_back(matmul('bsd,nd->bsn', hidden_b, w_out).astype(jnp.bfloat16), heads_matrix())
    grad_qkv, gains_q, gains_k = attn_bwd(*attn_args, grad_heads)
    grad_w_qkv = matmul('bsd,bsn->dn', attn_in, grad_qkv)
    grad_attn_in = matmul('bsn,dn->bsd', grad_qkv, w_qkv)
    grad_attn_norm = jnp.sum(grad_attn_in * normed1, axis=(0, 1))
    grad_x_emb = grad_hidden + norm_bwd(grad_attn_in, normed1, norm1_inv, attn_norm, D)
    head_grads = [jnp.tile(jnp.sum(gains, axis=(0, 1, 2)), SHARDS) for gains in (gains_q, gains_k)]
    small = jnp.stack([grad_attn_norm, grad_mlp_norm] + head_grads, axis=-1)
    small = jnp.pad(small, ((0, 0), (0, COLS[5] - small.shape[-1])))
    parts = tuple(g.reshape(SHARDS, -1, g.shape[-1]) for g in (grad_w_qkv, grad_w_out, grad_w_gate, grad_w_up, grad_w_down, small))
    return grad_x_emb, parts


def solution(mesh):
    row_spec = P(AXIS_NAME, None)
    vec_spec = P(AXIS_NAME)
    full_spec = P(None)
    batch_spec = P(AXIS_NAME, None, None)
    weight_specs = (vec_spec, row_spec, row_spec, row_spec, full_spec, full_spec, row_spec, vec_spec, row_spec, row_spec, row_spec)

    def device_step(tokens, positions, table_shard, attn_norm, w_query, w_key, w_value, q_norm, k_norm, w_out, mlp_norm, w_gate, w_up, w_down, dy_out):
        batch_len, seq_len = tokens.shape
        me = lax.axis_index(AXIS_NAME)
        tok = tokens.reshape(-1)
        place, ids, count, first = sort_by_owner(tok)
        meta = lax.all_gather(jnp.concatenate([tok, ids, count, first, jnp.zeros((TOKS - 2 * SHARDS,), jnp.int32)]), AXIS_NAME)
        local = meta[:, :TOKS].reshape(-1) - me * ROWS_TABLE
        where = jnp.where((local >= 0) & (local < ROWS_TABLE), local, ROWS_TABLE)
        all_ids = meta[:, TOKS:2 * TOKS].reshape(-1)
        mine = lax.dynamic_index_in_dim(meta[:, 2 * TOKS:2 * TOKS + 2 * SHARDS].reshape(SHARDS, 2, SHARDS), me, 2, keepdims=False)
        sent, sent_first = mine[:, 0], mine[:, 1]
        spread_m = spread_matrix()
        table_rows = jnp.pad(table_shard, ((0, UNROLL), (0, DP - D))).reshape(ROWS_TABLE + UNROLL, 8, 128)
        pad_rows = ((0, SUBP - SUB), (0, 0))
        sh_qkv = merge_groups(w_query, w_key, w_value, jnp.stack([attn_norm, mlp_norm], axis=-1))
        shards = [jnp.pad(w, pad_rows) for w in (sh_qkv, spread(w_out, spread_m), w_gate, w_up)]
        *full, got = front(where, table_rows, (*shards, spread(w_down, spread_m)))
        f_qkv, f_out, f_gate, f_up, f_down = (w.reshape(-1, w.shape[-1]) for w in full)
        spare = GROUP_IN - HEAD
        weights = (f_qkv[:, spare], f_qkv, q_norm, k_norm, f_out, f_qkv[:, spare + 1], f_gate, f_up, f_down)
        layer_out, saved_acts = layer_fwd(spread(got.reshape(batch_len, seq_len, DP)[..., :D], spread_m), positions, weights)
        layer_out = gather_back(layer_out, spread_m)
        grad_x_emb, parts = layer_bwd(spread(dy_out, spread_m), saved_acts, weights)
        grad_rows = grad_x_emb.reshape(TOKS, 8, 128)
        grad_rows = order_rows(place, grad_rows)
        r_qkv, r_out, r_gate, r_up, r_down, r_small = scatter_grads(parts)
        back = gather_rows(grad_rows)
        d_table = add_rows(all_ids, sent_first, sent, back.reshape(SHARDS * TOKS, 8, 128))
        g_query, g_key, g_value = split_groups(r_qkv[:SUB])
        g_attn, g_mlp, g_q, g_k = (r_small[:, i] for i in range(4))
        return (layer_out, d_table, g_attn[:SUB], g_query, g_key, g_value, g_q, g_k, unspread_columns(r_out[:SUB]), g_mlp[:SUB], r_gate[:SUB], r_up[:SUB], unspread_columns(r_down))

    return jax.shard_map(device_step, mesh=mesh, in_specs=(row_spec, row_spec, row_spec) + weight_specs + (batch_spec,), out_specs=(batch_spec, row_spec) + weight_specs, check_vma=False)
```

time: 1730 us -> 951 us (0.55)
  Pallas kernels: 0 us -> 708 us
  blocking collectives: 719 us -> 15.1 us
  waiting for transfers between devices: 272 us -> 0 us
  other arithmetic: 197 us -> 10.4 us
  local copies, waits for them, and re-layouts: 240 us -> 54 us
  matrix products: 263 us -> 152 us
    pallas_call x0 -> x7, Pallas kernels: none -> 708 us  [the longest x1 222 us: gather_rows(): pl.pallas_call(rows_body, out_shape=jax.ShapeDtypeStruct((SHARDS, TOKS, 8...]
    unnamed x3 -> x0, blocking collectives: 673 us -> none
    reduce_scatter x2 -> x0, waiting for transfers between devices: 269 us -> none  [the longest x1 269 us: device_step(): lax.psum_scatter(picked, AXIS_NAME, scatter_dimension=0, tiled=True)]
    scatter-add x1 -> x0, other arithmetic: 146 us -> none  [device_step(): jax.ops.segment_sum(all_rows, jnp.where(is_owner, local_ids, rows_local),...]
    dot_general x26 -> x24, matrix products: 243 us -> 152 us  [the longest x22 151 us: matmul(): return jnp.einsum(spec, lhs, rhs, preferred_element_type=jnp.float32)]
    gather x1 -> x0, local copies, waits for them, and re-layouts: 84.1 us -> none  [device_step(): jnp.take(table_shard, jnp.clip(local_ids, 0, rows_local - 1), axis=0)]
    all_gather x1, local copies, waits for them, and re-layouts: 64.6 us -> 0.04 us  [device_step(): lax.all_gather(jnp.concatenate([tok, ids, count, first, jnp.zeros((TOKS -...]
    unnamed x217 -> x109, local copies, waits for them, and re-layouts: 83.7 us -> 23.6 us
  transfers between devices with their start and end apart: 14 -> 0, of which waited for: 1 -> 0; matrix products, arithmetic and copies ran while one was open for 66% -> 0% of each run, Pallas kernels for 0% -> 0%
where the time goes in v1:
time: 951 us; the launch traced here: 942 us
  Pallas kernels  708 us (74%)
  matrix products  152 us (16%)
  local copies, waits for them, and re-layouts  54 us (6%)
  blocking collectives  15.1 us (2%)
  other arithmetic  10.4 us (1%)
    pallas_call x1, Pallas kernels, gather_rows(): pl.pallas_call(rows_body, out_shape=jax.ShapeDtypeStruct((SHARDS, TOKS, 8...  222 us
    pallas_call x1, Pallas kernels, front(): pl.pallas_call(front_body, out_shape=tuple((jax.ShapeDtypeStruct((SHARDS,...  186 us
    dot_general x22, matrix products, matmul(): return jnp.einsum(spec, lhs, rhs, preferred_element_type=jnp.float32)  151 us
    pallas_call x1, Pallas kernels, scatter_grads(): pl.pallas_call(scatter_body, out_shape=tuple((jax.ShapeDtypeStruct(shape,...  149 us
    pallas_call x1, Pallas kernels, attn_bwd(): pl.pallas_call(attn_bwd_body, grid=(batch_len, KV_HEADS), out_shape=(jax....  60.7 us
    pallas_call x1, Pallas kernels, add_rows(): pl.pallas_call(add_body, grid_spec=pltpu.PrefetchScalarGridSpec(num_scala...  54.5 us
    pallas_call x1, Pallas kernels, attn_fwd(): pl.pallas_call(attn_fwd_body, grid=(batch_len, KV_HEADS), out_shape=jax.S...  33.4 us
    unnamed x109, local copies, waits for them, and re-layouts  23.6 us

profile of v1, /device:TPU:0, one launch (start us, length us, event | category | flops | bytes accessed | tf_op | source)
XLA Modules:
  0.0 941.5 jit_solution(14433328809988329358)
XLA Ops:
  9.9 15.1 %all-gather = s32[49152]{0:T(1024)S(1)} all-gather(s32[3072]{0:T(1024)S(1)} %concatenate.12), channel_id=2, replica_groups=mesh['fsdp'=16] {'fsdp'}, dimensions={0}, use_global_device_ids=true | all-gather | bytes 208896 | tf_op jit(solution)/shard_map/all_gather | solution.py:730
  33.7 4.1 fusion.55
  37.8 3.2 pad.34
  41.0 9.9 %copy.100.refs_1_ = bf16[3080,8,128]{2,1,0:T(8,128)(2,1)} copy(bf16[3080,8,128]{0,2,1:T(8,128)(2,1)} %bitcast.150) | data formatting | bytes 12615680 | tf_op jit(solution)/shard_map/reshape | solution.py:737
  50.9 186.1 %front.1 = (bf16[16,64,1920]{2,1,0:T(8,128)(2,1)}, bf16[16,64,1024]{2,1,0:T(8,128)(2,1)}, bf16[16,64,2560]{2,1,0:T(8,128)(2,1)}, bf16[16,64,2560]{2,1,0:T(8,128)...) custom-call(s32[16384]{0:T(1024)} %and_select_fusion.refs_0_, bf16[3080,8,128]{2,1,0:T(8,128)(2,1)} %copy.100.refs_1_, ...), custom_call_target="tpu_custom_call" | custom-call | flops 60000002048 | bytes 100000000 | tf_op jit(solution)/shard_map/front/pallas_call | solution.py:265
  237.0 2.8 reshape.307
  239.8 4.0 fusion.24
  245.5 7.4 convolution_convert_fusion.1.qkv_ref
  253.0 33.4 %attn_fwd.1 = bf16[2,512,1280]{2,1,0:T(8,128)(2,1)S(1)} custom-call(bf16[2,512,1920]{2,1,0:T(8,128)(2,1)S(1)} %convolution_convert_fusion.1.qkv_ref, f32[2,512,64]{2,1,0:T(8,128)S(1)} %get-tuple-element.151.cos_ref, f32[2,512,64]{2,1,0:T(8,128)S(1)} %copy-done.3, f32[1,64]{1,0:T(1,128)S(1)} %get-tuple-element.154.gq_ref, f32[1,64]{1,0:T(1,128)S(1)} %get-tuple-element.153.gk_ref), custom_call_target="tpu_custom_call" | custom-call | flops 8000000000 | bytes 100000000 | tf_op jit(solution)/shard_map/attn_fwd/pallas_call | solution.py:641
  286.4 3.5 convolution_convert_fusion.2
  290.0 2.7 fusion.32
  292.7 8.4 fusion.84
  301.1 8.3 fusion.86
  309.4 19.6 %multiply_convert_fusion = (bf16[2,512,2560]{2,1,0:T(8,128)(2,1)}, bf16[2,512,2560]{2,1,0:T(8,128)(2,1)}, bf16[2,512,2560]{2,1,0:T(8,128)(2,1)}) fusion(f32[2,512,2560]{2,1,0:T(8,128)} %fusion.86, f32[2,512,2560]{2,1,0:T(8,128)} %fusion.84, bf16[2560,1024,1]{1,0,2:T(8,128)(2,1)} %bitcast.203, bf16[1024,2,512]{0,2,1:T(8,128)(2,1)} %fusion.55), kind=kOutput, calls=%fused_computation | convolution fusion | flops 5410652160 | bytes 44040192 | tf_op jit(solution)/shard_map/bsd,fd->bsf/dot_general | solution.py:386
  329.1 9.4 fusion.172
  338.5 4.5 fusion.58
  343.0 7.7 fusion.117
  350.7 8.4 fusion.31
  360.7 2.4 fusion.168
  363.1 5.5 convolution_convert_fusion.do_ref
  368.7 60.7 %attn_bwd.1 = (bf16[2,512,1920]{2,1,0:T(8,128)(2,1)S(1)}, f32[2,5,1,64]{3,2,1,0:T(1,128)S(1)}, f32[2,5,1,64]{3,2,1,0:T(1,128)S(1)}) custom-call(bf16[2,512,1920]{2,1,0:T(8,128)(2,1)S(1)} %copy-done.8, f32[2,512,64]{2,1,0:T(8,128)S(1)} %get-tuple-element.151.cos_ref, f32[2,512,64]{2,1,0:T(8,128)S(1)} %copy-done.3, f32[1,64]{1,0:T(1,128)S(1)} %get-tuple-element.154.gq_ref, ...), custom_call_target="tpu_custom_call" | custom-call | flops 16000000000 | bytes 100000000 | tf_op jit(solution)/shard_map/attn_bwd/pallas_call | solution.py:658
  431.5 8.9 fusion.23
  442.0 4.5 fusion.76
  447.6 2.4 order_rows.1.in_ref
  453.0 9.2 fusion.63
  462.2 11.0 %fusion.44 = f32[2560,1024,1]{1,0,2:T(8,128)} fusion(bf16[2,512,2560]{2,1,0:T(8,128)(2,1)} %get-tuple-element.107, bf16[1024,2,512]{0,2,1:T(8,128)(2,1)S(1)} %copy-done.12), kind=kOutput, calls=%fused_computation.63 | convolution fusion | flops 5368709120 | bytes 17825792 | tf_op jit(solution)/shard_map/bsf,bsd->fd/dot_general | solution.py:386
  473.2 8.6 fusion.80
  481.8 8.9 fusion.82
  490.7 149.5 %scatter_grads.1 = (f32[64,1920]{1,0:T(8,128)}, f32[64,1024]{1,0:T(8,128)}, f32[64,2560]{1,0:T(8,128)}, f32[64,2560]{1,0:T(8,128)}, f32[160,1024]{1,0:T(8,128)}, /*index=5*/f32[64,128]{1,0:T(8,128)}) custom-call(f32[16,64,1920]{2,1,0:T(8,128)} %bitcast.192, f32[16,64,1024]{2,1,0:T(8,128)} %bitcast.205, f32[16,64,2560]{2,1,0:T(8,128)} %bitcast.191, ...), custom_call_target="tpu_custom_call" | custom-call | flops 60000002048 | bytes 100000000 | tf_op jit(solution)/shard_map/scatter_grads/pallas_call | solution.py:359
  651.0 221.5 %gather_rows.1 = f32[16,1024,8,128]{3,2,1,0:T(8,128)} custom-call(f32[1024,8,128]{2,1,0:T(8,128)} %copy-done.2), custom_call_target="tpu_custom_call" | custom-call | flops 80000000000 | bytes 100000000 | tf_op jit(solution)/shard_map/gather_rows/pallas_call | solution.py:294
  872.5 54.5 %add_rows.1 = f32[3072,960]{1,0:T(8,128)} custom-call(s32[16384]{0:T(1024)} %bitcast.162, s32[16]{0:T(128)} %get-tuple-element.133.first_ref, s32[16]{0:T(128)} %get-tuple-element.132.count_ref, f32[16384,8,128]{2,1,0:T(8,128)} %bitcast.33.in_ref), custom_call_target="tpu_custom_call" | custom-call | tf_op jit(solution)/shard_map/add_rows/pallas_call | solution.py:504
  927.0 12.4 %copy.91 = f32[3072,960]{0,1:T(8,128)} copy(f32[3072,960]{1,0:T(8,128)} %add_rows.1) | data formatting | bytes 23592960
  (186 shorter events, 41.3 us)
Async XLA Ops:
  0.6 26.6 %copy-start = (bf16[160,960]{1,0:T(8,128)(2,1)S(1)}, bf16[160,960]{1,0:T(8,128)(2,1)}, u32[]{:S(2)}) copy-start(bf16[160,960]{1,0:T(8,128)(2,1)} %param.28) | copy-start | bytes 921604
  29.2 4.5 copy-start.30
  32.6 5.2 slice-start
  243.9 9.0 copy-start.28
  245.5 7.4 copy-start.26
  245.5 7.4 copy-start.3
  252.9 33.5 %copy-start.7 = (bf16[2,512,1920]{2,1,0:T(8,128)(2,1)}, bf16[2,512,1920]{2,1,0:T(8,128)(2,1)S(1)}, u32[]{:S(2)}) copy-start(bf16[2,512,1920]{2,1,0:T(8,128)(2,1)S(1)} %convolution_convert_fusion.1.qkv_ref) | copy-start | bytes 11796484
  252.9 39.8 %slice-start.2 = ((s8[5242880]{0:T(1024)(128)(4,1)}), s8[4194304]{0:T(1024)(128)(4,1)S(1)}, s32[]{:S(2)}) async-start(s8[5242880]{0:T(1024)(128)(4,1)} %bitcast.193), calls=%async_computation.2 | async-start | bytes 8388608
  286.4 6.3 slice-start.3
  290.0 11.2 %slice-start.6 = ((s8[5242880]{0:T(1024)(128)(4,1)}), s8[4194304]{0:T(1024)(128)(4,1)S(1)}, s32[]{:S(2)}) async-start(s8[5242880]{0:T(1024)(128)(4,1)} %bitcast.200), calls=%async_computation.6 | async-start | bytes 8388608
  292.7 8.5 copy-start.13
  292.7 8.4 slice-start.7
  338.5 4.5 copy-start.33
  338.5 12.2 %slice-start.4 = ((s8[5242880]{0:T(1024)(128)(4,1)}), s8[4194304]{0:T(1024)(128)(4,1)S(1)}, s32[]{:S(2)}) async-start(s8[5242880]{0:T(1024)(128)(4,1)} %bitcast.196), calls=%async_computation.4 | async-start | bytes 8388608
  343.0 7.7 copy-start.14
  343.0 7.7 slice-start.5
  350.7 8.4 copy-start.11
  363.1 5.5 copy-start.8
  368.6 62.9 %copy-start.27 = (f32[1024,1]{0,1:T(1,128)S(1)}, f32[1024,1]{0,1:T(1,128)}, u32[]{:S(2)}) copy-start(f32[1024,1]{0,1:T(1,128)} %copy-done.26) | copy-start | bytes 12292
  368.6 62.9 %copy-start.29 = (f32[2,512]{1,0:T(2,128)S(1)}, f32[2,512]{1,0:T(2,128)}, u32[]{:S(2)}) copy-start(f32[2,512]{1,0:T(2,128)} %copy-done.28) | copy-start | bytes 12292
  431.5 8.9 copy-start.10
  431.5 8.9 copy-start.17
  453.0 9.2 copy-start.12
  453.0 20.2 %slice-start.10 = ((s8[5242880]{0:T(1024)(128)(4,1)}), s8[4194304]{0:T(1024)(128)(4,1)S(1)}, s32[]{:S(2)}) async-start(s8[5242880]{0:T(1024)(128)(4,1)} %bitcast.210), calls=%async_computation.10 | async-start | bytes 8388608
  453.0 28.8 %slice-start.8 = ((s8[5242880]{0:T(1024)(128)(4,1)}), s8[4194304]{0:T(1024)(128)(4,1)S(1)}, s32[]{:S(2)}) async-start(s8[5242880]{0:T(1024)(128)(4,1)} %bitcast.208), calls=%async_computation.8 | async-start | bytes 8388608
  462.2 11.0 %copy-start.15 = (bf16[2,512,1024]{2,1,0:T(8,128)(2,1)S(1)}, bf16[2,512,1024]{2,1,0:T(8,128)(2,1)}, u32[]{:S(2)}) copy-start(bf16[2,512,1024]{2,1,0:T(8,128)(2,1)} %copy-done.13) | copy-start | bytes 6291460
  462.2 11.0 %slice-start.11 = ((s8[5242880]{0:T(1024)(128)(4,1)}), s8[1048576]{0:T(1024)(128)(4,1)S(1)}, s32[]{:S(2)}) async-start(s8[5242880]{0:T(1024)(128)(4,1)} %bitcast.210), calls=%async_computation.11 | async-start | bytes 2097152
  462.2 19.6 %slice-start.9 = ((s8[5242880]{0:T(1024)(128)(4,1)}), s8[1048576]{0:T(1024)(128)(4,1)S(1)}, s32[]{:S(2)}) async-start(s8[5242880]{0:T(1024)(128)(4,1)} %bitcast.208), calls=%async_computation.9 | async-start | bytes 2097152
  640.2 9.0 copy-start.20
  927.0 12.4 %copy-start.19 = (f32[64,2560]{1,0:T(8,128)S(1)}, f32[64,2560]{1,0:T(8,128)}, u32[]{:S(2)}) copy-start(f32[64,2560]{1,0:T(8,128)} %get-tuple-element.40) | copy-start | bytes 1966084
  927.0 13.2 %copy-start.18 = (f32[64,2560]{1,0:T(8,128)S(1)}, f32[64,2560]{1,0:T(8,128)}, u32[]{:S(2)}) copy-start(f32[64,2560]{1,0:T(8,128)} %get-tuple-element.41) | copy-start | bytes 1966084
  927.0 14.1 %copy-start.1 = (bf16[160,960]{1,0:T(8,128)(2,1)S(1)}, bf16[160,960]{1,0:T(8,128)(2,1)}, u32[]{:S(2)}) copy-start(bf16[160,960]{1,0:T(8,128)(2,1)} %param.28) | copy-start | bytes 921604
  (16 other events, 41.8 us)

commit v2 on v1

v2 whole, which is shorter than its diff:
```python
import math
import jax
import jax.numpy as jnp
from jax import lax
from jax.experimental import pallas as pl
from jax.experimental.pallas import tpu as pltpu
from jax.sharding import PartitionSpec as P

NORM_EPS = 1e-6
ROPE_THETA = 1.0e6
AXIS_NAME = 'fsdp'
D = 960
DP = 1024
SHARDS = 16
SUB = 60
SUBP = 64
QKVP = 1920
FF = 2560
ROWS_FF = 160
MESH_ID = pl.DeviceIdType.MESH
BITS = {'z': 8, 'y': 4, 'x': 2, 'c': 1}
QKV_PIECES = ((0, 0, 896, 'xyz'), (0, 896, 1024, 'yzx'), (1, 0, DP, 'zxy'))
DOWN_PIECES = ((2, 0, 384, 'xyz'), (2, 384, 384, 'yzx'), (2, 768, 256, 'zxy'))
AG_PIECES = QKV_PIECES + DOWN_PIECES
UP_PIECES = tuple((a, first, count, order) for a in (0, 1) for first, count, order in ((0, 896, 'xyz'), (896, 896, 'yzx'), (1792, 768, 'zxy')))
MLP_PIECES = ((2, 0, FF, 'xyz'), (3, 0, FF, 'yzx'), (4, 0, DP, 'zxy'))
ATT_PIECES = QKV_PIECES + ((5, 0, 128, 'yzx'),)
ROW_PIECES = tuple((0, half + lo, count, order) for half in (0, 512) for lo, count, order in ((0, 176, 'xyz'), (176, 176, 'yzx'), (352, 160, 'zxy')))
ROWS = (SUBP, SUBP, SUBP, SUBP, ROWS_FF, SUBP)
COLS = (QKVP, DP, FF, FF, DP, 128)
TOKS = 1024
ROWS_TABLE = 3072
UNROLL = 8
HEADS, KV_HEADS, GROUP, HEAD, SEQ, HALF = 15, 5, 3, 64, 512, 256
GROUP_IN = 384
GROUP_OUT = 256
SCALE = HEAD ** -0.5
MIB = 1024 * 1024
*Q_LANES, K_LANES, V_LANES = (slice(h * HEAD, (h + 1) * HEAD) for h in range(GROUP + 2))
FIRST_ORDER = (3, 7, 5, 1, 2, 6, 4, 0)
ANY_SPEC = pl.BlockSpec(memory_space=pl.ANY)
VMEM_SPEC = pl.BlockSpec(memory_space=pltpu.VMEM)
FRONT = (0, 1, 4)
MIDDLE = (2, 3)
MLP = (2, 3, 4)
LAST = (0, 1, 5)
HOPS = ((0, 0), (0, 2), (0, 4), (0, 6), (1, 0), (1, 4), (2, 0))


def own_bits():
    me = lax.axis_index(AXIS_NAME)
    return {'z': me // 8, 'y': (me // 4) % 2, 'x': (me // 2) % 2, 'c': me % 2}


def device_at(bits, flips):
    total = 0
    for name, weight in BITS.items():
        total = total + ((1 - bits[name]) if name in flips else bits[name]) * weight
    return total


def flips_of(code, order):
    return ''.join(order[i] for i in range(3) if (code >> i) & 1)


def greet(bits):
    barrier = pltpu.get_barrier_semaphore()
    for name in BITS:
        pl.semaphore_signal(barrier, inc=1, device_id=(device_at(bits, name),), device_id_type=MESH_ID)
    pl.semaphore_wait(barrier, 4)


def split(refs, *counts):
    parts = []
    for count in counts:
        parts.append(refs[:count])
        refs = refs[count:]
    return (*parts, refs)


class Doubling:
    def __init__(self, bits, pieces, ins, outs, view, send_sem, recv_sem):
        self.bits, self.pieces, self.ins, self.outs, self.view = bits, pieces, ins, outs, view
        self.send_sem, self.recv_sem = send_sem, recv_sem
        self.started = []

    def copy(self, p, code, step, src_code):
        piece = self.pieces[p]
        a, order = piece[0], piece[3]
        shard = device_at(self.bits, flips_of(src_code, order))
        src = self.ins[a] if src_code == 0 else self.outs[a].at[shard]
        target = device_at(self.bits, 'c' if step == 3 else order[step])
        slot = 8 + src_code if step == 3 else code
        return pltpu.make_async_remote_copy(
            src_ref=self.view(src, piece), dst_ref=self.view(self.outs[a].at[shard], piece),
            send_sem=self.send_sem.at[p, slot], recv_sem=self.recv_sem.at[p, slot],
            device_id=(target,), device_id_type=MESH_ID)

    def begin(self, *args):
        self.copy(*args).start()
        self.started.append(args)

    def arrived(self, p, slot):
        piece = self.pieces[p]
        flips = flips_of(slot % 8, piece[3]) + ('c' if slot >= 8 else '')
        dst = self.view(self.outs[piece[0]].at[device_at(self.bits, flips)], piece)
        pltpu.make_async_remote_copy(
            src_ref=dst, dst_ref=dst, send_sem=self.send_sem.at[p, slot], recv_sem=self.recv_sem.at[p, slot],
            device_id=(device_at(self.bits, 'c'),), device_id_type=MESH_ID).wait_recv()

    def open(self):
        for step in range(3):
            for p in range(len(self.pieces)):
                self.begin(p, 1 << step, step, 0)
        for p in range(len(self.pieces)):
            self.begin(p, 0, 3, 0)

    def forward(self, code):
        top = 0 if code == 1 else (1 if code < 4 else 2)
        for p in range(len(self.pieces)):
            self.arrived(p, code)
            for step in range(top + 1, 3):
                self.begin(p, code | (1 << step), step, code)
            self.begin(p, 0, 3, code)

    def close(self):
        for code in range(8):
            for p in range(len(self.pieces)):
                self.arrived(p, 8 + code)
        for args in self.started:
            self.copy(*args).wait_send()


def columns_of(ref, piece):
    return ref.at[:, pl.ds(piece[1], piece[2])]


def rows_of(ref, piece):
    return ref.at[pl.ds(piece[1], piece[2])]


class OwnShards:
    def __init__(self, bits, ins, outs, stage, load_sem, store_sem):
        each = range(len(ins))
        self.loads = [pltpu.make_async_copy(ins[a], stage[a], load_sem.at[a]) for a in each]
        self.stores = [pltpu.make_async_copy(stage[a], outs[a].at[device_at(bits, '')], store_sem.at[a]) for a in each]

    def load(self):
        for load in self.loads:
            load.start()

    def store(self):
        for load, store in zip(self.loads, self.stores):
            load.wait()
            store.start()

    def close(self):
        for store in self.stores:
            store.wait()


class Halving:
    def __init__(self, bits, pieces, source, acc, got, send_sem, recv_sem):
        self.bits, self.pieces, self.source, self.acc, self.got = bits, pieces, source, acc, got
        self.send_sem, self.recv_sem = send_sem, recv_sem

    def cross(self, p, code):
        return pltpu.make_async_remote_copy(
            src_ref=self.source(p, code), dst_ref=self.acc[p].at[code],
            send_sem=self.send_sem.at[p, code], recv_sem=self.recv_sem.at[p, code],
            device_id=(device_at(self.bits, 'c'),), device_id_type=MESH_ID)

    def hop(self, p, step, code):
        sem = UNROLL + HOPS.index((step, code))
        return pltpu.make_async_remote_copy(
            src_ref=self.acc[p].at[code | (1 << step)], dst_ref=self.got[step][p].at[code >> (step + 1)],
            send_sem=self.send_sem.at[p, sem], recv_sem=self.recv_sem.at[p, sem],
            device_id=(device_at(self.bits, self.pieces[p][3][step]),), device_id_type=MESH_ID)

    def total(self, p, code, at, steps):
        total = self.acc[p][code, at]
        for step in steps:
            total = total + self.got[step][p][code >> (step + 1), at]
        return total

    def add(self, p, code, steps, put=None):
        for step in steps:
            self.hop(p, step, code).wait_recv()

        def chunk(i, carry):
            at = pl.ds(pl.multiple_of(i * UNROLL, UNROLL), UNROLL)
            total = self.total(p, code, at, steps)
            if put is None:
                self.acc[p][code, at] = total
            else:
                put(p, at, total)
            return carry

        lax.fori_loop(0, self.acc[p].shape[1] // UNROLL, chunk, 0)

    def first(self, n, fill):
        code = FIRST_ORDER[n]
        for p in range(len(self.pieces)):
            self.cross(p, code).wait_recv()
            fill(p, n, code)
            if code & 1:
                self.hop(p, 0, code - 1).start()

    def second(self):
        for code in (2, 6):
            for p in range(len(self.pieces)):
                self.add(p, code, (0,))
                self.hop(p, 1, code - 2).start()

    def third(self):
        for p in range(len(self.pieces)):
            self.add(p, 4, (0, 1))
            self.hop(p, 2, 0).start()

    def last(self, put):
        for p in range(len(self.pieces)):
            self.add(p, 0, (0, 1, 2), put)

    def close(self):
        for p in range(len(self.pieces)):
            for code in FIRST_ORDER:
                self.cross(p, code).wait_send()
            for step, code in HOPS:
                self.hop(p, step, code).wait_send()


class GradTree(Halving):
    def __init__(self, bits, pieces, ins, outs, scratch):
        np_ = len(pieces)
        acc, self.own, *got, marks = split(scratch, np_, np_, np_, np_, np_)
        send_sem, recv_sem, self.own_sem = marks
        self.ins, self.outs = ins, outs
        super().__init__(bits, pieces, lambda p, code: self.part(p, code, 'c'), acc, got, send_sem, recv_sem)

    def part(self, p, code, flips):
        piece = self.pieces[p]
        shard = device_at(self.bits, flips_of(code, piece[3]) + flips)
        return columns_of(self.ins[piece[0]].at[shard], piece)

    def own_copy(self, p, n):
        return pltpu.make_async_copy(self.part(p, FIRST_ORDER[n], ''), self.own[p].at[n % 2], self.own_sem.at[p, n % 2])

    def load(self):
        for p in range(len(self.pieces)):
            self.own_copy(p, 0).start()
            self.own_copy(p, 1).start()

    def open(self):
        for code in FIRST_ORDER:
            for p in range(len(self.pieces)):
                self.cross(p, code).start()

    def fill(self, p, n, code):
        self.own_copy(p, n).wait()
        acc, own = self.acc[p], self.own[p]

        def chunk(i, carry):
            at = pl.ds(pl.multiple_of(i * UNROLL, UNROLL), UNROLL)
            acc[code, at] = acc[code, at] + own[n % 2, at]
            return carry

        lax.fori_loop(0, acc.shape[1] // UNROLL, chunk, 0)
        if n + 2 < len(FIRST_ORDER):
            self.own_copy(p, n + 2).start()

    def put(self, p, at, total):
        a, first, cols, order = self.pieces[p]
        self.outs[a][at, pl.ds(first, cols)] = total


def tree_scratch(pieces):
    scratch = []
    for lead in (8, 2, 4, 2, 1):
        scratch += [pltpu.VMEM((lead, ROWS[piece[0]], piece[2]), jnp.float32) for piece in pieces]
    return scratch + sems(len(pieces)) + [pltpu.SemaphoreType.DMA((len(pieces), 2))]


def grad_shape(a):
    return jax.ShapeDtypeStruct((ROWS[a], COLS[a]), jnp.float32)


def columns_of(ref, piece):
    return ref.at[:, pl.ds(piece[1], piece[2])]


def rows_of(ref, piece):
    return ref.at[pl.ds(piece[1], piece[2])]


def sems(count):
    return [pltpu.SemaphoreType.DMA((count, 16))] * 2


def cost(gflops):
    return pl.CostEstimate(flops=gflops * 10 ** 9, bytes_accessed=10 ** 8, transcendentals=0)


def front_body(*refs):
    num = len(FRONT)
    np_ = len(ROW_PIECES)
    where_ref, table_ref, *refs = refs
    ins, outs, (x_ref,), stage, away, acc, *got, marks = split(refs, num, num, 1, num, np_, np_, np_, np_, np_)
    w_send, w_recv, load_sem, store_sem, x_send, x_recv = marks
    bits = own_bits()
    pieces = range(np_)
    shards = OwnShards(bits, ins, outs, stage, load_sem, store_sem)
    shards.load()
    greet(bits)
    ring = Doubling(bits, AG_PIECES, ins, outs, columns_of, w_send, w_recv)
    ring.open()
    tree = Halving(bits, ROW_PIECES, lambda p, code: away[p].at[code], acc, got, x_send, x_recv)

    def pick(p, code, other):
        first, count, order = ROW_PIECES[p][1:]
        base = device_at(bits, flips_of(code, order) + ('c' if other else '')) * TOKS + first

        def step(i, carry):
            for k in range(UNROLL):
                t = i * UNROLL + k
                row = table_ref[where_ref[base + t]]
                if other:
                    away[p][code, t] = row
                else:
                    acc[p][code, t] = acc[p][code, t] + row
            return carry

        lax.fori_loop(0, count // UNROLL, step, 0)

    for code in FIRST_ORDER:
        for p in pieces:
            pick(p, code, True)
            tree.cross(p, code).start()
    shards.store()
    for code in range(1, 4):
        ring.forward(code)
    for n in range(len(FIRST_ORDER)):
        tree.first(n, lambda p, n, code: pick(p, code, False))
    for code in range(4, UNROLL):
        ring.forward(code)

    def put(p, at, total):
        x_ref[pl.ds(ROW_PIECES[p][1] + at.start, UNROLL)] = total

    tree.second()
    tree.third()
    tree.last(put)
    tree.close()
    ring.close()
    shards.close()


def gathered_shape(a):
    return jax.ShapeDtypeStruct((SHARDS, ROWS[a], COLS[a]), jnp.bfloat16)


def shard_scratch(arrays, count):
    stage = [pltpu.VMEM((ROWS[a], COLS[a]), jnp.bfloat16) for a in arrays]
    return stage, sems(count) + [pltpu.SemaphoreType.DMA((len(arrays),))] * 2


def comm(collective_id, mib):
    return pltpu.CompilerParams(collective_id=collective_id, has_side_effects=True, vmem_limit_bytes=mib * MIB)


def front(where, table, shards):
    num = len(shards)
    scratch, marks = shard_scratch(FRONT, len(AG_PIECES))
    for lead in (8, 8, 4, 2, 1):
        scratch += [pltpu.VMEM((lead, piece[2], 8, 128), jnp.bfloat16) for piece in ROW_PIECES]
    return pl.pallas_call(
        front_body,
        out_shape=tuple(gathered_shape(a) for a in FRONT) + (jax.ShapeDtypeStruct((TOKS, 8, 128), jnp.bfloat16),),
        in_specs=[pl.BlockSpec(memory_space=pltpu.SMEM), VMEM_SPEC] + [ANY_SPEC] * num,
        out_specs=(ANY_SPEC,) * num + (VMEM_SPEC,),
        scratch_shapes=scratch + marks + sems(len(ROW_PIECES)),
        compiler_params=comm(1, 63),
        cost_estimate=cost(60),
        name='front',
    )(where, table, *shards)


def back_body(rows_ref, qkv_ref, out_ref, small_ref, all_ref, *rest):
    results, (stage, send_sem, recv_sem, own_sem), scratch = split(rest, 3, 4)
    bits = own_bits()
    load = pltpu.make_async_copy(rows_ref, stage, own_sem.at[0])
    load.start()
    tree = GradTree(bits, ATT_PIECES, dict(zip(LAST, (qkv_ref, out_ref, small_ref))), dict(zip(LAST, results)), scratch)
    tree.load()
    greet(bits)
    ring = Doubling(bits, ROW_PIECES, (rows_ref,), (all_ref,), rows_of, send_sem, recv_sem)
    tree.open()
    ring.open()
    load.wait()
    store = pltpu.make_async_copy(stage, all_ref.at[device_at(bits, '')], own_sem.at[1])
    store.start()
    for n in range(len(FIRST_ORDER)):
        tree.first(n, tree.fill)
    ring.forward(1)
    tree.second()
    ring.forward(2)
    ring.forward(3)
    tree.third()
    ring.forward(4)
    tree.last(tree.put)
    for code in range(5, UNROLL):
        ring.forward(code)
    tree.close()
    ring.close()
    store.wait()


def back(rows, *grads):
    return pl.pallas_call(
        back_body,
        out_shape=(jax.ShapeDtypeStruct((SHARDS, TOKS, 8, 128), jnp.float32), *(grad_shape(a) for a in LAST)),
        in_specs=[ANY_SPEC] * 4,
        out_specs=(ANY_SPEC,) + (VMEM_SPEC,) * 3,
        scratch_shapes=[pltpu.VMEM((TOKS, 8, 128), jnp.float32)] + sems(len(ROW_PIECES)) + [pltpu.SemaphoreType.DMA((2,))] + tree_scratch(ATT_PIECES),
        compiler_params=comm(3, 40),
        cost_estimate=cost(80),
        name='back',
    )(rows, *grads)


def spread_matrix():
    src = lax.broadcasted_iota(jnp.int32, (D, DP), 0)
    dst = lax.broadcasted_iota(jnp.int32, (D, DP), 1)
    return ((src // SUB) * SUBP + src % SUB == dst).astype(jnp.bfloat16)


def heads_matrix():
    src = lax.broadcasted_iota(jnp.int32, (KV_HEADS * GROUP_OUT, DP), 0)
    dst = lax.broadcasted_iota(jnp.int32, (KV_HEADS * GROUP_OUT, DP), 1)
    lane = src % GROUP_OUT
    feature = (src // GROUP_OUT) * GROUP * HEAD + lane
    return ((lane < GROUP * HEAD) & ((feature // SUB) * SUBP + feature % SUB == dst)).astype(jnp.bfloat16)


def matmul(spec, lhs, rhs):
    return jnp.einsum(spec, lhs, rhs, preferred_element_type=jnp.float32)


def spread(values, matrix):
    return matmul('...d,de->...e', values, matrix).astype(jnp.bfloat16)


def gather_back(values, matrix):
    return matmul('...e,de->...d', values, matrix).astype(jnp.bfloat16)


def unspread_columns(values):
    rows = values.shape[0]
    return values.reshape(rows, SHARDS, SUBP)[:, :, :SUB].reshape(rows, D)


def merge_groups(w_query, w_key, w_value, gains):
    parts = []
    for g in range(KV_HEADS):
        at = slice(g * HEAD, (g + 1) * HEAD)
        spare = jnp.pad(gains if g == 0 else gains[:, :0], ((0, 0), (0, HEAD - (2 if g == 0 else 0))))
        parts += [w_query[:, g * GROUP * HEAD:(g + 1) * GROUP * HEAD], w_key[:, at], w_value[:, at], spare]
    return jnp.concatenate(parts, axis=1)


def split_groups(merged):
    grouped = merged.reshape(merged.shape[0], KV_HEADS, GROUP_IN)
    edges = (0, GROUP * HEAD, (GROUP + 1) * HEAD, (GROUP + 2) * HEAD)
    return tuple(grouped[:, :, lo:hi].reshape(merged.shape[0], -1) for lo, hi in zip(edges, edges[1:]))


def sort_by_id(tok):
    row = lax.broadcasted_iota(jnp.int32, (TOKS, TOKS), 0)
    col = lax.broadcasted_iota(jnp.int32, (TOKS, TOKS), 1)
    ahead = (tok[None, :] < tok[:, None]) | ((tok[None, :] == tok[:, None]) & (col < row))
    place = jnp.sum(ahead.astype(jnp.int32), axis=1)
    edge = (jnp.arange(SHARDS, dtype=jnp.int32) * ROWS_TABLE)[:, None]
    below = tok[None, :] < edge
    first = jnp.sum(below.astype(jnp.int32), axis=1)
    count = jnp.sum(((tok[None, :] < edge + ROWS_TABLE) & ~below).astype(jnp.int32), axis=1)
    local = tok % ROWS_TABLE
    halves = jnp.stack([local // HEAD, local % HEAD], axis=-1).astype(jnp.bfloat16)
    halves = matmul('st,tk->sk', (row == place[None, :]).astype(jnp.bfloat16), halves).astype(jnp.int32)
    return place, halves[:, 0] * HEAD + halves[:, 1], count, first


def order_body(place_ref, in_ref, out_ref):
    def step(i, carry):
        for k in range(UNROLL):
            t = i * UNROLL + k
            out_ref[place_ref[t]] = in_ref[t]
        return carry

    lax.fori_loop(0, TOKS // UNROLL, step, 0)


def order_rows(place, rows):
    whole = pl.BlockSpec((TOKS, 8, 128), lambda i, *_: (0, 0, 0))
    return pl.pallas_call(
        order_body,
        grid_spec=pltpu.PrefetchScalarGridSpec(num_scalar_prefetch=1, grid=(1,), in_specs=[whole], out_specs=whole),
        out_shape=jax.ShapeDtypeStruct((TOKS, 8, 128), jnp.float32),
        compiler_params=pltpu.CompilerParams(vmem_limit_bytes=40 * MIB),
        name='order_rows',
    )(place, rows)


def add_body(ids_ref, first_ref, count_ref, in_ref, out_ref, acc):
    j = pl.program_id(0)
    first = first_ref[j]
    count = count_ref[j]

    @pl.when(j == 0)
    def _():
        def clear(i, carry):
            acc[pl.ds(i * UNROLL, UNROLL)] = jnp.zeros((UNROLL, 8, 128), jnp.float32)
            return carry

        lax.fori_loop(0, ROWS_TABLE // UNROLL, clear, 0)

    def add(start, num):
        ids = [ids_ref[j * TOKS + start + k] for k in range(num)]
        olds = [acc[r] for r in ids]
        total = None
        totals = []
        for k in range(num):
            base = olds[k] if k == 0 else jnp.where(ids[k] == ids[k - 1], total, olds[k])
            total = base + in_ref[start + k]
            totals.append(total)
        for r, total in zip(ids, totals):
            acc[r] = total

    def step(i, carry):
        add(first + i * UNROLL, UNROLL)
        return carry

    def tail(i, carry):
        add(first + i, 1)
        return carry

    groups = count // UNROLL
    lax.fori_loop(0, groups, step, 0)
    lax.fori_loop(groups * UNROLL, count, tail, 0)

    @pl.when(j == SHARDS - 1)
    def _():
        def flush(i, carry):
            at = pl.ds(pl.multiple_of(i * 128, 128), 128)
            for k in range(UNROLL):
                block = acc[at, k, :].T
                for half in range(2):
                    out_ref[pl.ds((2 * k + half) * SUB, SUB), at] = block[half * SUBP:half * SUBP + SUB]
            return carry

        lax.fori_loop(0, ROWS_TABLE // 128, flush, 0)


def add_rows(ids, first, count, rows):
    return pl.pallas_call(
        add_body,
        grid_spec=pltpu.PrefetchScalarGridSpec(
            num_scalar_prefetch=3, grid=(SHARDS,),
            in_specs=[pl.BlockSpec((TOKS, 8, 128), lambda j, *_: (j, 0, 0))],
            out_specs=pl.BlockSpec((D, ROWS_TABLE), lambda j, *_: (0, 0)),
            scratch_shapes=[pltpu.VMEM((ROWS_TABLE, 8, 128), jnp.float32)]),
        out_shape=jax.ShapeDtypeStruct((D, ROWS_TABLE), jnp.float32),
        compiler_params=pltpu.CompilerParams(vmem_limit_bytes=60 * MIB),
        name='add_rows',
    )(ids, first, count, rows)


def rope_tables(positions):
    half_dim = HEAD // 2
    inv_freq = jnp.exp(jnp.arange(half_dim, dtype=jnp.float32) * (-2.0 * math.log(ROPE_THETA) / HEAD))
    angles = positions.astype(jnp.float32)[:, :, None] * inv_freq
    cos_t, sin_t = jnp.cos(angles), jnp.sin(angles)
    return jnp.concatenate([cos_t, cos_t], axis=-1), jnp.concatenate([-sin_t, sin_t], axis=-1)


def swap_halves(values):
    half_dim = HEAD // 2
    return jnp.concatenate([values[:, half_dim:], values[:, :half_dim]], axis=-1)


def norm_fwd(values, width=HEAD):
    values_f = values.astype(jnp.float32)
    inv_rms = lax.rsqrt(jnp.sum(values_f * values_f, axis=-1, keepdims=True) * (1.0 / width) + NORM_EPS)
    return values_f * inv_rms, inv_rms


def norm_bwd(grad_out, normed, inv_rms, norm_gain, width=HEAD):
    grad_normed = grad_out * norm_gain.astype(jnp.float32)
    mean_term = jnp.sum(grad_normed * normed, axis=-1, keepdims=True) * (1.0 / width)
    return inv_rms * (grad_normed - normed * mean_term)


def rope_fwd(normed, gain, cos_w, sin_w):
    scaled = normed * gain
    return (scaled * cos_w + swap_halves(scaled) * sin_w).astype(jnp.bfloat16)


def dot_nt(lhs, rhs):
    return lax.dot_general(lhs, rhs, (((1,), (1,)), ((), ())), preferred_element_type=jnp.float32)


def dot_nn(lhs, rhs):
    return lax.dot_general(lhs, rhs, (((1,), (0,)), ((), ())), preferred_element_type=jnp.float32)


def dot_tn(lhs, rhs):
    return lax.dot_general(lhs, rhs, (((0,), (0,)), ((), ())), preferred_element_type=jnp.float32)


def mask_last(scores, axis):
    split = scores.shape[axis] - HALF
    key = lax.broadcasted_iota(jnp.int32, (HALF, HALF), axis)
    query = lax.broadcasted_iota(jnp.int32, (HALF, HALF), 1 - axis)
    last = jnp.where(key <= query, lax.slice_in_dim(scores, split, split + HALF, axis=axis), -1e30)
    if split == 0:
        return last
    return jnp.concatenate([lax.slice_in_dim(scores, 0, split, axis=axis), last], axis=axis)


def softmax_of(scores, axis):
    scores = mask_last(scores, axis)
    weights = jnp.exp(scores - jnp.max(scores, axis=axis, keepdims=True))
    return weights * (1.0 / jnp.sum(weights, axis=axis, keepdims=True))


def attn_fwd_unit(b, g, qkv_ref, cos_ref, sin_ref, gq_ref, gk_ref, o_ref, block):
    cos_w, sin_w = cos_ref[b], sin_ref[b]
    lanes_out = pl.ds(pl.multiple_of(g * GROUP_OUT, 128), GROUP_OUT)
    all_heads = qkv_ref[b, :, pl.ds(pl.multiple_of(g * GROUP_IN, 128), GROUP_IN)]
    k_rot = rope_fwd(norm_fwd(all_heads[:, K_LANES])[0], gk_ref[...], cos_w, sin_w)
    v_raw = all_heads[:, V_LANES]
    for r in range(GROUP):
        q_rot = rope_fwd(norm_fwd(all_heads[:, Q_LANES[r]])[0], gq_ref[...], cos_w, sin_w) * SCALE
        for lo in range(0, SEQ, HALF):
            hi = lo + HALF
            probs = softmax_of(dot_nt(k_rot[:hi], q_rot[lo:hi]), 0)
            block[lo:hi, Q_LANES[r]] = dot_tn(probs.astype(jnp.bfloat16), v_raw[:hi]).astype(jnp.bfloat16)
    block[:, K_LANES] = jnp.zeros((SEQ, HEAD), jnp.bfloat16)
    o_ref[b, :, lanes_out] = block[...]


def attn_fwd_body(*refs):
    num = len(MIDDLE)
    ins, shard_refs, (o_ref,), full_refs, (block,), stage, marks = split(refs, 5, num, 1, num, 1, num)
    w_send, w_recv, load_sem, store_sem = marks
    bits = own_bits()
    shards = OwnShards(bits, shard_refs, full_refs, stage, load_sem, store_sem)
    shards.load()
    greet(bits)
    ring = Doubling(bits, UP_PIECES, shard_refs, full_refs, columns_of, w_send, w_recv)
    ring.open()
    shards.store()

    def unit(i, carry):
        attn_fwd_unit(i // KV_HEADS, i % KV_HEADS, *ins, o_ref, block)
        for code in range(1, 5):
            @pl.when(i == 2 * code - 1)
            def _(code=code):
                ring.forward(code)

        return carry

    lax.fori_loop(0, ins[0].shape[0] * KV_HEADS, unit, 0)
    for code in range(5, UNROLL):
        ring.forward(code)
    ring.close()
    shards.close()


def attn_bwd_unit(b, g, qkv_ref, cos_ref, sin_ref, gq_ref, gk_ref, do_ref, d_ref, dgq_ref, dgk_ref, block, dq_acc, dk_acc, dv_acc):
    cos_w, sin_w = cos_ref[b], sin_ref[b]
    gain_q, gain_k = gq_ref[...], gk_ref[...]
    lanes_in = pl.ds(pl.multiple_of(g * GROUP_IN, 128), GROUP_IN)
    lanes_out = pl.ds(pl.multiple_of(g * GROUP_OUT, 128), GROUP_OUT)
    block[...] = qkv_ref[b, :, lanes_in]
    k_normed, k_inv = norm_fwd(block[:, K_LANES])
    k_rot = rope_fwd(k_normed, gain_k, cos_w, sin_w)
    k_scaled = k_rot * SCALE
    v_raw = block[:, V_LANES]
    all_grads = do_ref[b, :, lanes_out]
    dk_acc[...] = jnp.zeros_like(dk_acc)
    dv_acc[...] = jnp.zeros_like(dv_acc)
    gain_total = jnp.zeros((1, HEAD), jnp.float32)
    for r in range(GROUP):
        q_normed, q_inv = norm_fwd(block[:, Q_LANES[r]])
        q_rot = rope_fwd(q_normed, gain_q, cos_w, sin_w) * SCALE
        head_grad = all_grads[:, Q_LANES[r]]
        for lo in range(0, SEQ, HALF):
            hi = lo + HALF
            out_grad = head_grad[lo:hi]
            q_part = q_rot[lo:hi]
            probs = softmax_of(dot_nt(k_rot[:hi], q_part), 0)
            grad_probs = dot_nt(v_raw[:hi], out_grad)
            dv_acc[:hi] += dot_nn(probs.astype(jnp.bfloat16), out_grad)
            delta = jnp.sum(grad_probs * probs, axis=0, keepdims=True)
            grad_scores = (probs * (grad_probs - delta)).astype(jnp.bfloat16)
            dk_acc[:hi] += dot_nn(grad_scores, q_part)
            dq_acc[lo:hi] = dot_tn(grad_scores, k_scaled[:hi])
        grad_q = dq_acc[...]
        grad_q = grad_q * cos_w - swap_halves(grad_q) * sin_w
        gain_total = gain_total + jnp.sum(grad_q * q_normed, axis=0, keepdims=True)
        block[:, Q_LANES[r]] = norm_bwd(grad_q, q_normed, q_inv, gain_q).astype(jnp.bfloat16)
    grad_k = dk_acc[...]
    grad_k = grad_k * cos_w - swap_halves(grad_k) * sin_w
    dgq_ref[...] += gain_total
    dgk_ref[...] += jnp.sum(grad_k * k_normed, axis=0, keepdims=True)
    block[:, K_LANES] = norm_bwd(grad_k, k_normed, k_inv, gain_k).astype(jnp.bfloat16)
    block[:, V_LANES.start:] = jnp.concatenate([dv_acc[...], jnp.zeros((SEQ, HEAD), jnp.float32)], axis=-1).astype(jnp.bfloat16)
    d_ref[b, :, lanes_in] = block[...]


def attn_bwd_body(*refs):
    ins, grads, outs, results, work, scratch = split(refs, 6, 3, 3, 3, 4)
    bits = own_bits()
    tree = GradTree(bits, MLP_PIECES, dict(zip(MLP, grads)), dict(zip(MLP, results)), scratch)
    tree.load()
    for ref in outs[1:]:
        ref[...] = jnp.zeros_like(ref)
    greet(bits)
    tree.open()
    tree.first(0, tree.fill)
    tree.first(1, tree.fill)

    def unit(i, carry):
        attn_bwd_unit(i // KV_HEADS, i % KV_HEADS, *ins, *outs, *work)
        for n in range(2, len(FIRST_ORDER)):
            @pl.when(i == n // 2 - 1)
            def _(n=n):
                tree.first(n, tree.fill)

        @pl.when(i == KV_HEADS)
        def _():
            tree.second()

        return carry

    lax.fori_loop(0, ins[0].shape[0] * KV_HEADS, unit, 0)
    tree.third()
    tree.last(tree.put)
    tree.close()


def attn_fwd(qkv, tables, shards):
    stage, marks = shard_scratch(MIDDLE, len(UP_PIECES))
    return pl.pallas_call(
        attn_fwd_body,
        out_shape=(jax.ShapeDtypeStruct(qkv.shape[:2] + (KV_HEADS * GROUP_OUT,), jnp.bfloat16),) + tuple(gathered_shape(a) for a in MIDDLE),
        in_specs=[VMEM_SPEC] * (len(tables) + 1) + [ANY_SPEC] * len(shards),
        out_specs=(VMEM_SPEC,) + (ANY_SPEC,) * len(shards),
        scratch_shapes=[pltpu.VMEM((SEQ, GROUP_OUT), jnp.bfloat16)] + stage + marks,
        compiler_params=comm(4, 40),
        cost_estimate=cost(20),
        name='attn_fwd',
    )(qkv, *tables, *shards)


def attn_bwd(qkv, tables, grads):
    gain_shape = jax.ShapeDtypeStruct((1, HEAD), jnp.float32)
    return pl.pallas_call(
        attn_bwd_body,
        out_shape=(jax.ShapeDtypeStruct(qkv.shape, jnp.bfloat16), gain_shape, gain_shape, *(grad_shape(a) for a in MLP)),
        in_specs=[VMEM_SPEC] * (len(tables) + 1) + [ANY_SPEC] * len(grads),
        out_specs=(VMEM_SPEC,) * 6,
        scratch_shapes=[pltpu.VMEM((SEQ, GROUP_IN), jnp.bfloat16)] + [pltpu.VMEM((SEQ, HEAD), jnp.float32)] * 3 + tree_scratch(MLP_PIECES),
        compiler_params=comm(2, 60),
        cost_estimate=cost(60),
        name='attn_bwd',
    )(qkv, *tables, *grads)


def layer_fwd(x_emb, positions, weights, shards):
    attn_norm, w_qkv, q_norm, k_norm, w_out, mlp_norm, w_down = weights
    cos_w, sin_w = rope_tables(positions)
    gain_q = q_norm.astype(jnp.float32)[None, :]
    gain_k = k_norm.astype(jnp.float32)[None, :]
    normed1, norm1_inv = norm_fwd(x_emb, D)
    attn_in = (normed1 * attn_norm.astype(jnp.float32)).astype(jnp.bfloat16)
    attn_args = (matmul('bsd,dn->bsn', attn_in, w_qkv).astype(jnp.bfloat16), cos_w, sin_w, gain_q, gain_k)
    heads, *full = attn_fwd(attn_args[0], attn_args[1:], shards)
    w_gate, w_up = (w.reshape(-1, w.shape[-1]) for w in full)
    attn_flat = spread(heads, heads_matrix())
    hidden = (x_emb.astype(jnp.float32) + matmul('bsn,nd->bsd', attn_flat, w_out)).astype(jnp.bfloat16)
    normed2, norm2_inv = norm_fwd(hidden, D)
    mlp_in = (normed2 * mlp_norm.astype(jnp.float32)).astype(jnp.bfloat16)
    gate_pre = matmul('bsd,df->bsf', mlp_in, w_gate)
    up_proj = matmul('bsd,df->bsf', mlp_in, w_up)
    mlp_act = (jax.nn.silu(gate_pre) * up_proj).astype(jnp.bfloat16)
    layer_out = (hidden.astype(jnp.float32) + matmul('bsf,fd->bsd', mlp_act, w_down)).astype(jnp.bfloat16)
    return layer_out, (normed1, norm1_inv, attn_in, attn_args, attn_flat, normed2, norm2_inv, mlp_in, gate_pre, up_proj, mlp_act, w_gate, w_up)


def layer_bwd(dy_out, saved_acts, weights):
    attn_norm, w_qkv, q_norm, k_norm, w_out, mlp_norm, w_down = weights
    normed1, norm1_inv, attn_in, attn_args, attn_flat, normed2, norm2_inv, mlp_in, gate_pre, up_proj, mlp_act, w_gate, w_up = saved_acts
    grad_w_down = matmul('bsf,bsd->fd', mlp_act, dy_out)
    grad_act = matmul('bsd,fd->bsf', dy_out, w_down)
    gate_sig = jax.nn.sigmoid(gate_pre)
    grad_gate = (grad_act * up_proj * gate_sig * (1.0 + gate_pre * (1.0 - gate_sig))).astype(jnp.bfloat16)
    grad_up = (grad_act * gate_pre * gate_sig).astype(jnp.bfloat16)
    grad_w_gate = matmul('bsd,bsf->df', mlp_in, grad_gate)
    grad_w_up = matmul('bsd,bsf->df', mlp_in, grad_up)
    grad_mlp_in = matmul('bsf,df->bsd', grad_gate, w_gate) + matmul('bsf,df->bsd', grad_up, w_up)
    grad_mlp_norm = jnp.sum(grad_mlp_in * normed2, axis=(0, 1))
    grad_hidden = dy_out.astype(jnp.float32) + norm_bwd(grad_mlp_in, normed2, norm2_inv, mlp_norm, D)
    hidden_b = grad_hidden.astype(jnp.bfloat16)
    grad_w_out = matmul('bsn,bsd->nd', attn_flat, hidden_b)
    grad_heads = gather_back(matmul('bsd,nd->bsn', hidden_b, w_out).astype(jnp.bfloat16), heads_matrix())
    mlp_grads = [g.reshape(SHARDS, -1, g.shape[-1]) for g in (grad_w_gate, grad_w_up, grad_w_down)]
    grad_qkv, gains_q, gains_k, *mlp_shards = attn_bwd(attn_args[0], attn_args[1:] + (grad_heads,), mlp_grads)
    grad_w_qkv = matmul('bsd,bsn->dn', attn_in, grad_qkv)
    grad_attn_in = matmul('bsn,dn->bsd', grad_qkv, w_qkv)
    grad_attn_norm = jnp.sum(grad_attn_in * normed1, axis=(0, 1))
    grad_x_emb = grad_hidden + norm_bwd(grad_attn_in, normed1, norm1_inv, attn_norm, D)
    head_grads = [jnp.tile(gains[0], SHARDS) for gains in (gains_q, gains_k)]
    small = jnp.stack([grad_attn_norm, grad_mlp_norm] + head_grads, axis=-1)
    small = jnp.pad(small, ((0, 0), (0, COLS[5] - small.shape[-1])))
    parts = tuple(g.reshape(SHARDS, -1, g.shape[-1]) for g in (grad_w_qkv, grad_w_out, small))
    return grad_x_emb, parts, mlp_shards


def solution(mesh):
    row_spec = P(AXIS_NAME, None)
    vec_spec = P(AXIS_NAME)
    full_spec = P(None)
    batch_spec = P(AXIS_NAME, None, None)
    weight_specs = (vec_spec, row_spec, row_spec, row_spec, full_spec, full_spec, row_spec, vec_spec, row_spec, row_spec, row_spec)

    def device_step(tokens, positions, table_shard, attn_norm, w_query, w_key, w_value, q_norm, k_norm, w_out, mlp_norm, w_gate, w_up, w_down, dy_out):
        batch_len, seq_len = tokens.shape
        me = lax.axis_index(AXIS_NAME)
        tok = tokens.reshape(-1)
        place, ids, count, first = sort_by_id(tok)
        meta = lax.all_gather(jnp.concatenate([tok, ids, count, first, jnp.zeros((TOKS - 2 * SHARDS,), jnp.int32)]), AXIS_NAME)
        local = meta[:, :TOKS].reshape(-1) - me * ROWS_TABLE
        where = jnp.where((local >= 0) & (local < ROWS_TABLE), local, ROWS_TABLE)
        all_ids = meta[:, TOKS:2 * TOKS].reshape(-1)
        mine = lax.dynamic_index_in_dim(meta[:, 2 * TOKS:2 * TOKS + 2 * SHARDS].reshape(SHARDS, 2, SHARDS), me, 2, keepdims=False)
        sent, sent_first = mine[:, 0], mine[:, 1]
        spread_m = spread_matrix()
        table_rows = jnp.pad(table_shard, ((0, UNROLL), (0, DP - D))).reshape(ROWS_TABLE + UNROLL, 8, 128)
        pad_rows = ((0, SUBP - SUB), (0, 0))
        sh_qkv = merge_groups(w_query, w_key, w_value, jnp.stack([attn_norm, mlp_norm], axis=-1))
        *full, got = front(where, table_rows, (jnp.pad(sh_qkv, pad_rows), jnp.pad(spread(w_out, spread_m), pad_rows), spread(w_down, spread_m)))
        f_qkv, f_out, f_down = (w.reshape(-1, w.shape[-1]) for w in full)
        spare = GROUP_IN - HEAD
        weights = (f_qkv[:, spare], f_qkv, q_norm, k_norm, f_out, f_qkv[:, spare + 1], f_down)
        x_emb = spread(got.reshape(batch_len, seq_len, DP)[..., :D], spread_m)
        layer_out, saved_acts = layer_fwd(x_emb, positions, weights, [jnp.pad(w, pad_rows) for w in (w_gate, w_up)])
        layer_out = gather_back(layer_out, spread_m)
        grad_x_emb, parts, (r_gate, r_up, r_down) = layer_bwd(spread(dy_out, spread_m), saved_acts, weights)
        grad_rows = grad_x_emb.reshape(TOKS, 8, 128)
        grad_rows = order_rows(place, grad_rows)
        all_rows, r_qkv, r_out, r_small = back(grad_rows, *parts)
        d_table = add_rows(all_ids, sent_first, sent, all_rows.reshape(SHARDS * TOKS, 8, 128)).T
        g_query, g_key, g_value = split_groups(r_qkv[:SUB])
        g_attn, g_mlp, g_q, g_k = (r_small[:, i] for i in range(4))
        return (layer_out, d_table, g_attn[:SUB], g_query, g_key, g_value, g_q, g_k, unspread_columns(r_out[:SUB]), g_mlp[:SUB], r_gate[:SUB], r_up[:SUB], unspread_columns(r_down))

    return jax.shard_map(device_step, mesh=mesh, in_specs=(row_spec, row_spec, row_spec) + weight_specs + (batch_spec,), out_specs=(batch_spec, row_spec) + weight_specs, check_vma=False)
```

time: 951 us -> 869 us (0.914)
  Pallas kernels: 708 us -> 644 us
  local copies, waits for them, and re-layouts: 54 us -> 37.9 us
    pallas_call x5 -> x4, Pallas kernels: 651 us -> 592 us  [the longest x1 278 us: back(): pl.pallas_call(back_body, out_shape=(jax.ShapeDtypeStruct((SHARDS, TOKS,...]
    unnamed x109 -> x106, local copies, waits for them, and re-layouts: 23.6 us -> 10.3 us
    dot_general x22 -> x23, matrix products: 151 us -> 149 us  [matmul(): return jnp.einsum(spec, lhs, rhs, preferred_element_type=jnp.float32)]
where the time goes in v2:
time: 869 us; the launch traced here: 859 us
  Pallas kernels  644 us (74%)
  matrix products  149 us (17%)
  local copies, waits for them, and re-layouts  37.9 us (4%)
  blocking collectives  15.1 us (2%)
  other arithmetic  11.6 us (1%)
    pallas_call x1, Pallas kernels, back(): pl.pallas_call(back_body, out_shape=(jax.ShapeDtypeStruct((SHARDS, TOKS,...  278 us
    pallas_call x1, Pallas kernels, front(): pl.pallas_call(front_body, out_shape=tuple((gathered_shape(a) for a in FR...  153 us
    dot_general x23, matrix products, matmul(): return jnp.einsum(spec, lhs, rhs, preferred_element_type=jnp.float32)  149 us
    pallas_call x1, Pallas kernels, attn_bwd(): pl.pallas_call(attn_bwd_body, out_shape=(jax.ShapeDtypeStruct(qkv.shape,...  115 us
    pallas_call x1, Pallas kernels, add_rows(): pl.pallas_call(add_body, grid_spec=pltpu.PrefetchScalarGridSpec(num_scala...  50 us
    pallas_call x1, Pallas kernels, attn_fwd(): pl.pallas_call(attn_fwd_body, out_shape=(jax.ShapeDtypeStruct(qkv.shape[:...  45 us

profile of v2, /device:TPU:0, one launch (start us, length us, event | category | flops | bytes accessed | tf_op | source)
XLA Modules:
  0.0 859.2 jit_solution(13840395810903405556)
XLA Ops:
  6.4 2.0 fusion.68
  10.2 15.1 %all-gather = s32[49152]{0:T(1024)S(1)} all-gather(s32[3072]{0:T(1024)S(1)} %concatenate.12), channel_id=2, replica_groups=mesh['fsdp'=16] {'fsdp'}, dimensions={0}, use_global_device_ids=true | all-gather | bytes 208896 | tf_op jit(solution)/shard_map/all_gather | solution.py:841
  33.3 4.2 fusion.56
  37.4 3.2 pad.34
  40.7 9.9 %copy.96.refs_1_ = bf16[3080,8,128]{2,1,0:T(8,128)(2,1)} copy(bf16[3080,8,128]{0,2,1:T(8,128)(2,1)} %bitcast.160) | data formatting | bytes 12615680 | tf_op jit(solution)/shard_map/reshape | solution.py:848
  50.5 153.4 %front.1 = (bf16[16,64,1920]{2,1,0:T(8,128)(2,1)}, bf16[16,64,1024]{2,1,0:T(8,128)(2,1)}, bf16[16,160,1024]{2,1,0:T(8,128)(2,1)}, bf16[1024,8,128]{2,1,0:T(8,128)(2,1)}) custom-call(s32[16384]{0:T(1024)} %and_select_fusion.refs_0_, bf16[3080,8,128]{2,1,0:T(8,128)(2,1)} %copy.96.refs_1_, bf16[64,1920]{1,0:T(8,128)(2,1)} %pad.37.refs_2_, ...), custom_call_target="tpu_custom_call" | custom-call | flops 60000002048 | bytes 100000000 | tf_op jit(solution)/shard_map/front/pallas_call | solution.py:375
  204.0 2.8 reshape.264
  206.8 3.9 fusion.24
  212.4 7.4 convolution_convert_fusion.1.refs_0_
  219.9 45.0 %attn_fwd.1 = (bf16[2,512,1280]{2,1,0:T(8,128)(2,1)S(1)}, bf16[16,64,2560]{2,1,0:T(8,128)(2,1)S(1)}, bf16[16,64,2560]{2,1,0:T(8,128)(2,1)}) custom-call(bf16[2,512,1920]{2,1,0:T(8,128)(2,1)S(1)} %convolution_convert_fusion.1.refs_0_, f32[2,512,64]{2,1,0:T(8,128)S(1)} %get-tuple-element.146.refs_1_, f32[2,512,64]{2,1,0:T(8,128)S(1)} %copy-done.5, ...), custom_call_target="tpu_custom_call" | custom-call | flops 20000000000 | bytes 100000000 | tf_op jit(solution)/shard_map/attn_fwd/pallas_call | solution.py:753
  264.9 3.5 convolution_convert_fusion.2
  269.0 2.7 fusion.32
  271.7 8.5 fusion.82
  280.2 8.7 %fusion.84 = f32[2,512,2560]{2,1,0:T(8,128)} fusion(bf16[1024,2560,1]{1,0,2:T(8,128)(2,1)S(1)} %bitcast.157, bf16[2,512,1024]{2,1,0:T(8,128)(2,1)S(1)} %get-tuple-element.130, f32[1024]{0:T(1024)S(1)} %bitcast.180, f32[2,512]{1,0:T(2,128)S(1)} %add_rsqrt_fusion), kind=kOutput, calls=%fused_computation.92 | convolution fusion | flops 5372903424 | bytes 17833984 | tf_op jit(solution)/shard_map/bsd,df->bsf/dot_general | solution.py:445
  288.9 18.5 %multiply_convert_fusion = (bf16[2,512,2560]{2,1,0:T(8,128)(2,1)}, bf16[2,512,2560]{2,1,0:T(8,128)(2,1)}, bf16[2,512,2560]{2,1,0:T(8,128)(2,1)}) fusion(f32[2,512,2560]{2,1,0:T(8,128)} %fusion.84, f32[2,512,2560]{2,1,0:T(8,128)} %fusion.82, bf16[2560,1024,1]{1,0,2:T(8,128)(2,1)} %bitcast.203, bf16[1024,2,512]{0,2,1:T(8,128)(2,1)S(1)} %copy-done.17), kind=kOutput, calls=%fused_computation | convolution fusion | flops 5410652160 | bytes 44040192 | tf_op jit(solution)/shard_map/bsd,fd->bsf/dot_general | solution.py:445
  307.4 9.4 %fusion.169 = bf16[2,512,1024]{2,1,0:T(8,128)(2,1)S(1)} fusion(bf16[2,512,1024]{2,1,0:T(8,128)(2,1)} %copy-done.18, bf16[2,512,2560]{2,1,0:T(8,128)(2,1)} %get-tuple-element.100, bf16[2560,1024,1]{1,0,2:T(8,128)(2,1)} %bitcast.204), kind=kOutput, calls=%fused_computation.48.clone.clone.clone.clone.2 | convolution fusion | flops 5371854848 | bytes 14680064 | tf_op jit(solution)/shard_map/bsf,fd->bsd/dot_general | solution.py:445
  316.8 4.4 fusion.59
  321.4 7.1 fusion.114
  328.6 8.1 fusion.31
  338.3 2.4 fusion.165
  340.6 6.3 convolution_convert_fusion.refs_5_
  347.0 4.5 fusion.74
  351.5 8.2 fusion.45
  359.7 8.4 fusion.78
  368.2 8.6 %fusion.80 = f32[1024,2560,1]{1,0,2:T(8,128)} fusion(bf16[2,512,2560]{2,1,0:T(8,128)(2,1)S(1)} %copy-done.36, bf16[2,512,1024]{2,1,0:T(8,128)(2,1)S(1)} %copy-done.19, f32[1024]{0:T(1024)S(1)} %bitcast.184, f32[2,512]{1,0:T(2,128)S(1)} %add_rsqrt_fusion), kind=kOutput, calls=%fused_computation.90 | convolution fusion | flops 5372903424 | bytes 17833984 | tf_op jit(solution)/shard_map/bsd,bsf->df/dot_general | solution.py:445
  376.8 115.2 %attn_bwd.1 = (bf16[2,512,1920]{2,1,0:T(8,128)(2,1)}, f32[1,64]{1,0:T(1,128)}, f32[1,64]{1,0:T(1,128)}, f32[64,2560]{1,0:T(8,128)}, f32[64,2560]{1,0:T(8,128)}, /*index=5*/f32[160,1024]{1,0:T(8,128)}) custom-call(bf16[2,512,1920]{2,1,0:T(8,128)(2,1)} %copy-done.14, f32[2,512,64]{2,1,0:T(8,128)} %copy-done.4, f32[2,512,64]{2,1,0:T(8,128)} %get-tuple-element.147.refs_2_, ...), custom_call_target="tpu_custom_call" | custom-call | flops 60000002048 | bytes 100000000 | tf_op jit(solution)/shard_map/attn_bwd/pallas_call | solution.py:767
  493.4 8.3 fusion.23
  504.1 2.4 order_rows.1.rows_ref
  511.5 10.8 %fusion.64 = f32[1024,1920,1]{1,0,2:T(8,128)} fusion(bf16[2,512,1920]{2,1,0:T(8,128)(2,1)} %get-tuple-element.37, bf16[2,512,1024]{2,1,0:T(8,128)(2,1)} %get-tuple-element.128, f32[1024]{0:T(1024)S(1)} %bitcast.191, f32[2,512]{1,0:T(2,128)S(1)} %copy-done.31), kind=kOutput, calls=%fused_computation.76 | convolution fusion | flops 4030726144 | bytes 13901824 | tf_op jit(solution)/shard_map/bsd,bsn->dn/dot_general | solution.py:445
  522.3 278.2 %back.1 = (f32[16,1024,8,128]{3,2,1,0:T(8,128)}, f32[64,1920]{1,0:T(8,128)S(1)}, f32[64,1024]{1,0:T(8,128)S(1)}, f32[64,128]{1,0:T(8,128)S(1)}) custom-call(f32[1024,8,128]{2,1,0:T(8,128)S(1)} %copy-done.3, f32[16,64,1920]{2,1,0:T(8,128)} %bitcast.202, f32[16,64,1024]{2,1,0:T(8,128)S(1)} %bitcast.159, f32[16,64,128]{2,1,0:T(8,128)S(1)} %bitcast.154), custom_call_target="tpu_custom_call" | custom-call | flops 80000000000 | bytes 100000000 | tf_op jit(solution)/shard_map/back/pallas_call | solution.py:418
  800.6 50.0 %add_rows.1 = f32[960,3072]{1,0:T(8,128)} custom-call(s32[16384]{0:T(1024)} %bitcast.171, s32[16]{0:T(128)} %get-tuple-element.126.first_ref, s32[16]{0:T(128)} %get-tuple-element.125.count_ref, f32[16384,8,128]{2,1,0:T(8,128)} %bitcast.48.in_ref), custom_call_target="tpu_custom_call" | custom-call | tf_op jit(solution)/shard_map/add_rows/pallas_call | solution.py:563
  855.9 2.0 copy.110
  (175 shorter events, 34.4 us)
Async XLA Ops:
  0.6 26.9 %copy-start = (bf16[160,960]{1,0:T(8,128)(2,1)S(1)}, bf16[160,960]{1,0:T(8,128)(2,1)}, u32[]{:S(2)}) copy-start(bf16[160,960]{1,0:T(8,128)(2,1)} %param.28) | copy-start | bytes 921604
  2.1 217.7 %copy-start.9 = (f32[1,64]{1,0:T(1,128)}, f32[1,64]{1,0:T(1,128)S(1)}, u32[]{:S(2)}) copy-start(f32[1,64]{1,0:T(1,128)S(1)} %get-tuple-element.148.refs_4_) | copy-start | bytes 772
  2.1 217.7 %copy-start.10 = (f32[1,64]{1,0:T(1,128)}, f32[1,64]{1,0:T(1,128)S(1)}, u32[]{:S(2)}) copy-start(f32[1,64]{1,0:T(1,128)S(1)} %get-tuple-element.149.refs_3_) | copy-start | bytes 772
  32.1 5.3 slice-start
  33.3 186.6 %copy-start.4 = (f32[2,512,64]{2,1,0:T(8,128)}, f32[2,512,64]{2,1,0:T(8,128)S(1)}, u32[]{:S(2)}) copy-start(f32[2,512,64]{2,1,0:T(8,128)S(1)} %get-tuple-element.146.refs_1_) | copy-start | bytes 786436
  210.8 9.1 %copy-start.30 = (f32[2,512]{1,0:T(2,128)}, f32[2,512]{1,0:T(2,128)S(1)}, u32[]{:S(2)}) copy-start(f32[2,512]{1,0:T(2,128)S(1)} %add_rsqrt_fusion.1) | copy-start | bytes 12292
  212.4 7.4 copy-start.28
  212.4 7.4 copy-start.5
  212.4 7.4 copy-start.6
  219.9 45.0 %copy-start.14 = (bf16[2,512,1920]{2,1,0:T(8,128)(2,1)}, bf16[2,512,1920]{2,1,0:T(8,128)(2,1)S(1)}, u32[]{:S(2)}) copy-start(bf16[2,512,1920]{2,1,0:T(8,128)(2,1)S(1)} %convolution_convert_fusion.1.refs_0_) | copy-start | bytes 11796484
  264.9 15.3 %copy-start.11 = (bf16[16,64,2560]{2,1,0:T(8,128)(2,1)}, bf16[16,64,2560]{2,1,0:T(8,128)(2,1)S(1)}, u32[]{:S(2)}) copy-start(bf16[16,64,2560]{2,1,0:T(8,128)(2,1)S(1)} %get-tuple-element.34) | copy-start | bytes 15728644
  271.7 8.5 copy-start.18
  280.2 8.7 %copy-start.17 = (bf16[1024,2,512]{0,2,1:T(8,128)(2,1)S(1)}, bf16[1024,2,512]{0,2,1:T(8,128)(2,1)}, u32[]{:S(2)}) copy-start(bf16[1024,2,512]{0,2,1:T(8,128)(2,1)} %fusion.56) | copy-start | bytes 6291460
  316.8 4.4 copy-start.12
  316.8 4.6 copy-start.36
  316.8 11.7 %slice-start.2 = ((s8[5242880]{0:T(1024)(128)(4,1)}), s8[4194304]{0:T(1024)(128)(4,1)S(1)}, s32[]{:S(2)}) async-start(s8[5242880]{0:T(1024)(128)(4,1)} %bitcast.206), calls=%async_computation.2 | async-start | bytes 8388608
  316.8 11.7 %slice-start.4 = ((s8[5242880]{0:T(1024)(128)(4,1)}), s8[4194304]{0:T(1024)(128)(4,1)S(1)}, s32[]{:S(2)}) async-start(s8[5242880]{0:T(1024)(128)(4,1)} %bitcast.211), calls=%async_computation.4 | async-start | bytes 8388608
  321.4 7.1 copy-start.19
  321.4 7.1 slice-start.3
  321.4 7.1 slice-start.5
  338.3 8.7 %copy-start.15 = (f32[2,512,1024]{2,1,0:T(8,128)}, f32[2,512,1024]{2,1,0:T(8,128)S(1)}, u32[]{:S(2)}) copy-start(f32[2,512,1024]{2,1,0:T(8,128)S(1)} %fusion.30) | copy-start | bytes 12582916
  338.3 13.2 %slice-start.6 = ((s8[5242880]{0:T(1024)(128)(4,1)}), s8[4194304]{0:T(1024)(128)(4,1)S(1)}, s32[]{:S(2)}) async-start(s8[5242880]{0:T(1024)(128)(4,1)} %bitcast.213), calls=%async_computation.6 | async-start | bytes 8388608
  340.6 6.4 copy-start.38
  340.6 10.9 %slice-start.7 = ((s8[5242880]{0:T(1024)(128)(4,1)}), s8[1048576]{0:T(1024)(128)(4,1)S(1)}, s32[]{:S(2)}) async-start(s8[5242880]{0:T(1024)(128)(4,1)} %bitcast.213), calls=%async_computation.7 | async-start | bytes 2097152
  376.8 116.6 %copy-start.21 = (bf16[2,512,1024]{2,1,0:T(8,128)(2,1)S(1)}, bf16[2,512,1024]{2,1,0:T(8,128)(2,1)}, u32[]{:S(2)}) copy-start(bf16[2,512,1024]{2,1,0:T(8,128)(2,1)} %get-tuple-element.128) | copy-start | bytes 6291460
  376.8 116.6 %copy-start.29 = (f32[1024,1]{0,1:T(1,128)S(1)}, f32[1024,1]{0,1:T(1,128)}, u32[]{:S(2)}) copy-start(f32[1024,1]{0,1:T(1,128)} %copy-done.28) | copy-start | bytes 12292
  376.8 116.6 %copy-start.31 = (f32[2,512]{1,0:T(2,128)S(1)}, f32[2,512]{1,0:T(2,128)}, u32[]{:S(2)}) copy-start(f32[2,512]{1,0:T(2,128)} %copy-done.30) | copy-start | bytes 12292
  493.4 8.4 copy-start.16
  511.5 10.8 %copy-start.3 = (f32[1024,8,128]{2,1,0:T(8,128)S(1)}, f32[1024,8,128]{2,1,0:T(8,128)}, u32[]{:S(2)}) copy-start(f32[1024,8,128]{2,1,0:T(8,128)} %copy-done.2) | copy-start | bytes 12582916
  511.5 10.8 %copy-start.13 = (f32[1024,1024,1]{1,0,2:T(8,128)S(1)}, f32[1024,1024,1]{1,0,2:T(8,128)}, u32[]{:S(2)}) copy-start(f32[1024,1024,1]{1,0,2:T(8,128)} %fusion.74) | copy-start | bytes 12582916
  850.5 7.3 copy-start.22
  851.9 6.8 copy-start.1
  (15 other events, 42.8 us)

commit v3 on v2

--- a/solution.py
+++ b/solution.py
@@ -31,6 +31,7 @@
 TOKS = 1024
 ROWS_TABLE = 3072
 UNROLL = 8
+LANES = 128
 HEADS, KV_HEADS, GROUP, HEAD, SEQ, HALF = 15, 5, 3, 64, 512, 256
 GROUP_IN = 384
 GROUP_OUT = 256
@@ -40,6 +41,7 @@
 FIRST_ORDER = (3, 7, 5, 1, 2, 6, 4, 0)
 ANY_SPEC = pl.BlockSpec(memory_space=pl.ANY)
 VMEM_SPEC = pl.BlockSpec(memory_space=pltpu.VMEM)
+FORWARD_AT = (0, 2, 4, 5, 6, 8)
 FRONT = (0, 1, 4)
 MIDDLE = (2, 3)
 MLP = (2, 3, 4)
@@ -68,6 +70,10 @@
     for name in BITS:
         pl.semaphore_signal(barrier, inc=1, device_id=(device_at(bits, name),), device_id_type=MESH_ID)
     pl.semaphore_wait(barrier, 4)
+
+
+def loop(count, body):
+    lax.fori_loop(0, count, body, 0)
 
 
 def split(refs, *counts):
@@ -196,7 +202,7 @@
                 put(p, at, total)
             return carry
 
-        lax.fori_loop(0, self.acc[p].shape[1] // UNROLL, chunk, 0)
+        loop(self.acc[p].shape[1] // UNROLL, chunk)
 
     def first(self, n, fill):
         code = FIRST_ORDER[n]
@@ -264,7 +270,7 @@
             acc[code, at] = acc[code, at] + own[n % 2, at]
             return carry
 
-        lax.fori_loop(0, acc.shape[1] // UNROLL, chunk, 0)
+        loop(acc.shape[1] // UNROLL, chunk)
         if n + 2 < len(FIRST_ORDER):
             self.own_copy(p, n + 2).start()
 
@@ -329,7 +335,7 @@
                     acc[p][code, t] = acc[p][code, t] + row
             return carry
 
-        lax.fori_loop(0, count // UNROLL, step, 0)
+        loop(count // UNROLL, step)
 
     for code in FIRST_ORDER:
         for p in pieces:
@@ -371,10 +377,10 @@
     num = len(shards)
     scratch, marks = shard_scratch(FRONT, len(AG_PIECES))
     for lead in (8, 8, 4, 2, 1):
-        scratch += [pltpu.VMEM((lead, piece[2], 8, 128), jnp.bfloat16) for piece in ROW_PIECES]
+        scratch += [pltpu.VMEM((lead, piece[2], UNROLL, LANES), jnp.bfloat16) for piece in ROW_PIECES]
     return pl.pallas_call(
         front_body,
-        out_shape=tuple(gathered_shape(a) for a in FRONT) + (jax.ShapeDtypeStruct((TOKS, 8, 128), jnp.bfloat16),),
+        out_shape=tuple(gathered_shape(a) for a in FRONT) + (jax.ShapeDtypeStruct((TOKS, UNROLL, LANES), jnp.bfloat16),),
         in_specs=[pl.BlockSpec(memory_space=pltpu.SMEM), VMEM_SPEC] + [ANY_SPEC] * num,
         out_specs=(ANY_SPEC,) * num + (VMEM_SPEC,),
         scratch_shapes=scratch + marks + sems(len(ROW_PIECES)),
@@ -384,28 +390,102 @@
     )(where, table, *shards)
 
 
-def back_body(rows_ref, qkv_ref, out_ref, small_ref, all_ref, *rest):
-    results, (stage, send_sem, recv_sem, own_sem), scratch = split(rest, 3, 4)
+class LastTree(GradTree):
+    def multiply(self, lhs_t, rhs, away, home):
+        self.lhs_t, self.rhs, self.away, self.home = lhs_t, rhs, away, home
+
+    def mixed(self, p):
+        return self.pieces[p][0] == 0
+
+    def products(self, into, core):
+        def shard_rows(code, carry):
+            for p in range(len(into)):
+                first, cols, order = self.pieces[p][1:]
+                shard = core
+                for i, name in enumerate(order):
+                    flip = (code // (1 << i)) % 2
+                    shard = shard + (self.bits[name] + flip - 2 * self.bits[name] * flip) * BITS[name]
+                rows = pl.ds(pl.multiple_of(shard * SUBP, SUBP), SUBP)
+                into[p][code] = dot_nn(self.lhs_t[rows, :], self.rhs[:, pl.ds(first, cols)])
+            return carry
+
+        loop(UNROLL, shard_rows)
+
+    def part(self, p, code, flips):
+        return self.away[p].at[code] if self.mixed(p) else super().part(p, code, flips)
+
+    def load(self):
+        for p in range(len(self.pieces)):
+            if not self.mixed(p):
+                self.own_copy(p, 0).start()
+                self.own_copy(p, 1).start()
+
+    def open(self):
+        self.products(self.away, 1 - self.bits['c'])
+        super().open()
+        self.products(self.home, self.bits['c'])
+
+    def fill(self, p, n, code):
+        if not self.mixed(p):
+            super().fill(p, n, code)
+            return
+
+        def chunk(i, carry):
+            at = pl.ds(pl.multiple_of(i * UNROLL, UNROLL), UNROLL)
+            self.acc[p][code, at] = self.acc[p][code, at] + self.home[p][code, at]
+            return carry
+
+        loop(SUBP // UNROLL, chunk)
+
+
+def back_body(rows_ref, out_ref, small_ref, *refs):
+    num = 6
+    ins, (all_ref,), results, (y_ref,), (stage, send_sem, recv_sem, own_sem, load_sem), held, (lhs_t,), away, home, scratch = split(refs, num, 1, 3, 1, 5, num, 1, 2, 2)
+    lhs, rhs, act, down, hidden, spread_m = held
     bits = own_bits()
     load = pltpu.make_async_copy(rows_ref, stage, own_sem.at[0])
     load.start()
-    tree = GradTree(bits, ATT_PIECES, dict(zip(LAST, (qkv_ref, out_ref, small_ref))), dict(zip(LAST, results)), scratch)
+    loads = [pltpu.make_async_copy(ins[i], held[i], load_sem.at[i]) for i in range(num)]
+    for copy in loads:
+        copy.start()
+    tree = LastTree(bits, ATT_PIECES, dict(zip(LAST, (None, out_ref, small_ref))), dict(zip(LAST, results)), scratch)
+    tree.multiply(lhs_t, rhs, away, home)
     tree.load()
     greet(bits)
     ring = Doubling(bits, ROW_PIECES, (rows_ref,), (all_ref,), rows_of, send_sem, recv_sem)
+    ring.open()
+    for copy in loads:
+        copy.wait()
+
+    def turn(i, carry):
+        at = pl.ds(pl.multiple_of(i * LANES, LANES), LANES)
+        lhs_t[at, :] = lhs[:, at].T
+        return carry
+
+    loop(DP // LANES, turn)
     tree.open()
-    ring.open()
     load.wait()
     store = pltpu.make_async_copy(stage, all_ref.at[device_at(bits, '')], own_sem.at[1])
     store.start()
     for n in range(len(FIRST_ORDER)):
         tree.first(n, tree.fill)
+
+    blocks = SEQ // HALF
+
+    def project(i, carry):
+        tokens = pl.ds(pl.multiple_of(i * HALF, HALF), HALF)
+        total = (hidden[tokens, :].astype(jnp.float32) + dot_nn(act[tokens, :], down[...])).astype(jnp.bfloat16)
+        part = pl.ds(pl.multiple_of((i % blocks) * HALF, HALF), HALF)
+        y_ref[i // blocks, :, part] = dot_nt(spread_m[...], total).astype(jnp.bfloat16)
+        return carry
+
     ring.forward(1)
     tree.second()
     ring.forward(2)
     ring.forward(3)
     tree.third()
     ring.forward(4)
+    loop(TOKS // HALF, project)
     tree.last(tree.put)
     for code in range(5, UNROLL):
         ring.forward(code)
@@ -414,17 +494,22 @@
     store.wait()
 
 
-def back(rows, *grads):
+def back(*operands):
+    held = operands[3:]
+    scratch = [pltpu.VMEM((TOKS, UNROLL, LANES), jnp.float32)] + sems(len(ROW_PIECES)) + [pltpu.SemaphoreType.DMA((2,)), pltpu.SemaphoreType.DMA((len(held),))]
+    scratch += [pltpu.VMEM(array.shape, array.dtype) for array in held]
+    scratch += [pltpu.VMEM((DP, TOKS), jnp.bfloat16)]
+    scratch += [pltpu.VMEM((UNROLL, SUBP, piece[2]), jnp.float32) for piece in QKV_PIECES[:2]] * 2
     return pl.pallas_call(
         back_body,
-        out_shape=(jax.ShapeDtypeStruct((SHARDS, TOKS, 8, 128), jnp.float32), *(grad_shape(a) for a in LAST)),
-        in_specs=[ANY_SPEC] * 4,
-        out_specs=(ANY_SPEC,) + (VMEM_SPEC,) * 3,
-        scratch_shapes=[pltpu.VMEM((TOKS, 8, 128), jnp.float32)] + sems(len(ROW_PIECES)) + [pltpu.SemaphoreType.DMA((2,))] + tree_scratch(ATT_PIECES),
-        compiler_params=comm(3, 40),
+        out_shape=(jax.ShapeDtypeStruct((SHARDS, TOKS, UNROLL, LANES), jnp.float32), *(grad_shape(a) for a in LAST), jax.ShapeDtypeStruct((TOKS // SEQ, D, SEQ), jnp.bfloat16)),
+        in_specs=[ANY_SPEC] * len(operands),
+        out_specs=(ANY_SPEC,) + (VMEM_SPEC,) * 4,
+        scratch_shapes=scratch + tree_scratch(ATT_PIECES),
+        compiler_params=comm(3, 60),
         cost_estimate=cost(80),
         name='back',
-    )(rows, *grads)
+    )(*operands)
 
 
 def spread_matrix():
@@ -478,7 +563,7 @@
     col = lax.broadcasted_iota(jnp.int32, (TOKS, TOKS), 1)
     ahead = (tok[None, :] < tok[:, None]) | ((tok[None, :] == tok[:, None]) & (col < row))
     place = jnp.sum(ahead.astype(jnp.int32), axis=1)
-    edge = (jnp.arange(SHARDS, dtype=jnp.int32) * ROWS_TABLE)[:, None]
+    edge = lax.broadcasted_iota(jnp.int32, (SHARDS, 1), 0) * ROWS_TABLE
     below = tok[None, :] < edge
     first = jnp.sum(below.astype(jnp.int32), axis=1)
     count = jnp.sum(((tok[None, :] < edge + ROWS_TABLE) & ~below).astype(jnp.int32), axis=1)
@@ -495,15 +580,15 @@
             out_ref[place_ref[t]] = in_ref[t]
         return carry
 
-    lax.fori_loop(0, TOKS // UNROLL, step, 0)
+    loop(TOKS // UNROLL, step)
 
 
 def order_rows(place, rows):
-    whole = pl.BlockSpec((TOKS, 8, 128), lambda i, *_: (0, 0, 0))
+    whole = pl.BlockSpec((TOKS, UNROLL, LANES), lambda i, *_: (0, 0, 0))
     return pl.pallas_call(
         order_body,
         grid_spec=pltpu.PrefetchScalarGridSpec(num_scalar_prefetch=1, grid=(1,), in_specs=[whole], out_specs=whole),
-        out_shape=jax.ShapeDtypeStruct((TOKS, 8, 128), jnp.float32),
+        out_shape=jax.ShapeDtypeStruct((TOKS, UNROLL, LANES), jnp.float32),
         compiler_params=pltpu.CompilerParams(vmem_limit_bytes=40 * MIB),
         name='order_rows',
     )(place, rows)
@@ -517,10 +602,10 @@
     @pl.when(j == 0)
     def _():
         def clear(i, carry):
-            acc[pl.ds(i * UNROLL, UNROLL)] = jnp.zeros((UNROLL, 8, 128), jnp.float32)
+            acc[pl.ds(i * UNROLL, UNROLL)] = jnp.zeros((UNROLL, UNROLL, LANES), jnp.float32)
             return carry
 
-        lax.fori_loop(0, ROWS_TABLE // UNROLL, clear, 0)
+        loop(ROWS_TABLE // UNROLL, clear)
 
     def add(start, num):
         ids = [ids_ref[j * TOKS + start + k] for k in range(num)]
@@ -543,20 +628,20 @@
         return carry
 
     groups = count // UNROLL
-    lax.fori_loop(0, groups, step, 0)
+    loop(groups, step)
     lax.fori_loop(groups * UNROLL, count, tail, 0)
 
     @pl.when(j == SHARDS - 1)
     def _():
         def flush(i, carry):
-            at = pl.ds(pl.multiple_of(i * 128, 128), 128)
+            at = pl.ds(pl.multiple_of(i * LANES, LANES), LANES)
             for k in range(UNROLL):
                 block = acc[at, k, :].T
                 for half in range(2):
-                    out_ref[pl.ds((2 * k + half) * SUB, SUB), at] = block[half * SUBP:half * SUBP + SUB]
+                    out_ref[pl.ds((2 * k + half) * SUB, SUB), at] = block[half * SUBP:][:SUB]
             return carry
 
-        lax.fori_loop(0, ROWS_TABLE // 128, flush, 0)
+        loop(ROWS_TABLE // LANES, flush)
 
 
 def add_rows(ids, first, count, rows):
@@ -564,9 +649,9 @@
         add_body,
         grid_spec=pltpu.PrefetchScalarGridSpec(
             num_scalar_prefetch=3, grid=(SHARDS,),
-            in_specs=[pl.BlockSpec((TOKS, 8, 128), lambda j, *_: (j, 0, 0))],
+            in_specs=[pl.BlockSpec((TOKS, UNROLL, LANES), lambda j, *_: (j, 0, 0))],
             out_specs=pl.BlockSpec((D, ROWS_TABLE), lambda j, *_: (0, 0)),
-            scratch_shapes=[pltpu.VMEM((ROWS_TABLE, 8, 128), jnp.float32)]),
+            scratch_shapes=[pltpu.VMEM((ROWS_TABLE, UNROLL, LANES), jnp.float32)]),
         out_shape=jax.ShapeDtypeStruct((D, ROWS_TABLE), jnp.float32),
         compiler_params=pltpu.CompilerParams(vmem_limit_bytes=60 * MIB),
         name='add_rows',
@@ -633,8 +718,8 @@
 
 def attn_fwd_unit(b, g, qkv_ref, cos_ref, sin_ref, gq_ref, gk_ref, o_ref, block):
     cos_w, sin_w = cos_ref[b], sin_ref[b]
-    lanes_out = pl.ds(pl.multiple_of(g * GROUP_OUT, 128), GROUP_OUT)
-    all_heads = qkv_ref[b, :, pl.ds(pl.multiple_of(g * GROUP_IN, 128), GROUP_IN)]
+    lanes_out = pl.ds(pl.multiple_of(g * GROUP_OUT, LANES), GROUP_OUT)
+    all_heads = qkv_ref[b, :, pl.ds(pl.multiple_of(g * GROUP_IN, LANES), GROUP_IN)]
     k_rot = rope_fwd(norm_fwd(all_heads[:, K_LANES])[0], gk_ref[...], cos_w, sin_w)
     v_raw = all_heads[:, V_LANES]
     for r in range(GROUP):
@@ -661,16 +746,15 @@
 
     def unit(i, carry):
         attn_fwd_unit(i // KV_HEADS, i % KV_HEADS, *ins, o_ref, block)
-        for code in range(1, 5):
-            @pl.when(i == 2 * code - 1)
+        for code, turn in enumerate(FORWARD_AT, 1):
+            @pl.when(i == turn)
             def _(code=code):
                 ring.forward(code)
 
         return carry
 
-    lax.fori_loop(0, ins[0].shape[0] * KV_HEADS, unit, 0)
-    for code in range(5, UNROLL):
-        ring.forward(code)
+    loop(ins[0].shape[0] * KV_HEADS, unit)
+    ring.forward(UNROLL - 1)
     ring.close()
     shards.close()
 
@@ -678,8 +762,8 @@
 def attn_bwd_unit(b, g, qkv_ref, cos_ref, sin_ref, gq_ref, gk_ref, do_ref, d_ref, dgq_ref, dgk_ref, block, dq_acc, dk_acc, dv_acc):
     cos_w, sin_w = cos_ref[b], sin_ref[b]
     gain_q, gain_k = gq_ref[...], gk_ref[...]
-    lanes_in = pl.ds(pl.multiple_of(g * GROUP_IN, 128), GROUP_IN)
-    lanes_out = pl.ds(pl.multiple_of(g * GROUP_OUT, 128), GROUP_OUT)
+    lanes_in = pl.ds(pl.multiple_of(g * GROUP_IN, LANES), GROUP_IN)
+    lanes_out = pl.ds(pl.multiple_of(g * GROUP_OUT, LANES), GROUP_OUT)
     block[...] = qkv_ref[b, :, lanes_in]
     k_normed, k_inv = norm_fwd(block[:, K_LANES])
     k_rot = rope_fwd(k_normed, gain_k, cos_w, sin_w)
@@ -718,7 +802,7 @@
 
 
 def attn_bwd_body(*refs):
-    ins, grads, outs, results, work, scratch = split(refs, 6, 3, 3, 3, 4)
+    ins, (w_qkv,), grads, outs, (in_grad,), results, work, scratch = split(refs, 6, 1, 3, 3, 1, 3, 4)
     bits = own_bits()
     tree = GradTree(bits, MLP_PIECES, dict(zip(MLP, grads)), dict(zip(MLP, results)), scratch)
     tree.load()
@@ -742,7 +826,15 @@
 
         return carry
 
-    lax.fori_loop(0, ins[0].shape[0] * KV_HEADS, unit, 0)
+    loop(ins[0].shape[0] * KV_HEADS, unit)
+    qkv_grad, blocks = outs[0], SEQ // HALF
+
+    def input_grad(i, carry):
+        rows = pl.ds(pl.multiple_of((i % blocks) * HALF, HALF), HALF)
+        in_grad[i // blocks, rows, :] = dot_nt(qkv_grad[i // blocks, rows, :], w_qkv[...])
+        return carry
+
+    loop(blocks * qkv_grad.shape[0], input_grad)
     tree.third()
     tree.last(tree.put)
     tree.close()
@@ -762,21 +854,21 @@
     )(qkv, *tables, *shards)
 
 
-def attn_bwd(qkv, tables, grads):
+def attn_bwd(qkv, tables, w_qkv, grads):
     gain_shape = jax.ShapeDtypeStruct((1, HEAD), jnp.float32)
     return pl.pallas_call(
         attn_bwd_body,
-        out_shape=(jax.ShapeDtypeStruct(qkv.shape, jnp.bfloat16), gain_shape, gain_shape, *(grad_shape(a) for a in MLP)),
-        in_specs=[VMEM_SPEC] * (len(tables) + 1) + [ANY_SPEC] * len(grads),
-        out_specs=(VMEM_SPEC,) * 6,
+        out_shape=(jax.ShapeDtypeStruct(qkv.shape, jnp.bfloat16), gain_shape, gain_shape, jax.ShapeDtypeStruct(qkv.shape[:2] + (DP,), jnp.float32), *(grad_shape(a) for a in MLP)),
+        in_specs=[VMEM_SPEC] * (len(tables) + 2) + [ANY_SPEC] * len(grads),
+        out_specs=(VMEM_SPEC,) * 7,
         scratch_shapes=[pltpu.VMEM((SEQ, GROUP_IN), jnp.bfloat16)] + [pltpu.VMEM((SEQ, HEAD), jnp.float32)] * 3 + tree_scratch(MLP_PIECES),
-        compiler_params=comm(2, 60),
+        compiler_params=comm(2, 63),
         cost_estimate=cost(60),
         name='attn_bwd',
-    )(qkv, *tables, *grads)
-
-
-def layer_fwd(x_emb, positions, weights, shards):
+    )(qkv, *tables, w_qkv, *grads)
+
+
+def layer_fwd(x_emb, positions, weights, shards, dy_s):
     attn_norm, w_qkv, q_norm, k_norm, w_out, mlp_norm, w_down = weights
     cos_w, sin_w = rope_tables(positions)
     gain_q = q_norm.astype(jnp.float32)[None, :]
@@ -792,9 +884,9 @@
     mlp_in = (normed2 * mlp_norm.astype(jnp.float32)).astype(jnp.bfloat16)
     gate_pre = matmul('bsd,df->bsf', mlp_in, w_gate)
     up_proj = matmul('bsd,df->bsf', mlp_in, w_up)
+    gate_pre, up_proj, dy_s = lax.optimization_barrier((gate_pre, up_proj, dy_s))
     mlp_act = (jax.nn.silu(gate_pre) * up_proj).astype(jnp.bfloat16)
-    layer_out = (hidden.astype(jnp.float32) + matmul('bsf,fd->bsd', mlp_act, w_down)).astype(jnp.bfloat16)
-    return layer_out, (normed1, norm1_inv, attn_in, attn_args, attn_flat, normed2, norm2_inv, mlp_in, gate_pre, up_proj, mlp_act, w_gate, w_up)
+    return (mlp_act.reshape(TOKS, FF), w_down, hidden.reshape(TOKS, DP)), dy_s, (normed1, norm1_inv, attn_in, attn_args, attn_flat, normed2, norm2_inv, mlp_in, gate_pre, up_proj, mlp_act, w_gate, w_up)
 
 
 def layer_bwd(dy_out, saved_acts, weights):
@@ -814,16 +906,14 @@
     grad_w_out = matmul('bsn,bsd->nd', attn_flat, hidden_b)
     grad_heads = gather_back(matmul('bsd,nd->bsn', hidden_b, w_out).astype(jnp.bfloat16), heads_matrix())
     mlp_grads = [g.reshape(SHARDS, -1, g.shape[-1]) for g in (grad_w_gate, grad_w_up, grad_w_down)]
-    grad_qkv, gains_q, gains_k, *mlp_shards = attn_bwd(attn_args[0], attn_args[1:] + (grad_heads,), mlp_grads)
-    grad_w_qkv = matmul('bsd,bsn->dn', attn_in, grad_qkv)
-    grad_attn_in = matmul('bsn,dn->bsd', grad_qkv, w_qkv)
+    grad_qkv, gains_q, gains_k, grad_attn_in, *mlp_shards = attn_bwd(attn_args[0], attn_args[1:] + (grad_heads,), w_qkv, mlp_grads)
     grad_attn_norm = jnp.sum(grad_attn_in * normed1, axis=(0, 1))
     grad_x_emb = grad_hidden + norm_bwd(grad_attn_in, normed1, norm1_inv, attn_norm, D)
     head_grads = [jnp.tile(gains[0], SHARDS) for gains in (gains_q, gains_k)]
     small = jnp.stack([grad_attn_norm, grad_mlp_norm] + head_grads, axis=-1)
     small = jnp.pad(small, ((0, 0), (0, COLS[5] - small.shape[-1])))
-    parts = tuple(g.reshape(SHARDS, -1, g.shape[-1]) for g in (grad_w_qkv, grad_w_out, small))
-    return grad_x_emb, parts, mlp_shards
+    parts = tuple(g.reshape(SHARDS, -1, g.shape[-1]) for g in (grad_w_out, small))
+    return grad_x_emb, (*parts, attn_in.reshape(TOKS, DP), grad_qkv.reshape(TOKS, QKVP)), mlp_shards
 
 
 def solution(mesh):
@@ -845,7 +935,7 @@
         mine = lax.dynamic_index_in_dim(meta[:, 2 * TOKS:2 * TOKS + 2 * SHARDS].reshape(SHARDS, 2, SHARDS), me, 2, keepdims=False)
         sent, sent_first = mine[:, 0], mine[:, 1]
         spread_m = spread_matrix()
-        table_rows = jnp.pad(table_shard, ((0, UNROLL), (0, DP - D))).reshape(ROWS_TABLE + UNROLL, 8, 128)
+        table_rows = jnp.pad(table_shard, ((0, UNROLL), (0, DP - D))).reshape(ROWS_TABLE + UNROLL, UNROLL, LANES)
         pad_rows = ((0, SUBP - SUB), (0, 0))
         sh_qkv = merge_groups(w_query, w_key, w_value, jnp.stack([attn_norm, mlp_norm], axis=-1))
         *full, got = front(where, table_rows, (jnp.pad(sh_qkv, pad_rows), jnp.pad(spread(w_out, spread_m), pad_rows), spread(w_down, spread_m)))
@@ -853,13 +943,13 @@
         spare = GROUP_IN - HEAD
         weights = (f_qkv[:, spare], f_qkv, q_norm, k_norm, f_out, f_qkv[:, spare + 1], f_down)
         x_emb = spread(got.reshape(batch_len, seq_len, DP)[..., :D], spread_m)
-        layer_out, saved_acts = layer_fwd(x_emb, positions, weights, [jnp.pad(w, pad_rows) for w in (w_gate, w_up)])
-        layer_out = gather_back(layer_out, spread_m)
-        grad_x_emb, parts, (r_gate, r_up, r_down) = layer_bwd(spread(dy_out, spread_m), saved_acts, weights)
-        grad_rows = grad_x_emb.reshape(TOKS, 8, 128)
+        last, dy_s, saved_acts = layer_fwd(x_emb, positions, weights, [jnp.pad(w, pad_rows) for w in (w_gate, w_up)], spread(dy_out, spread_m))
+        grad_x_emb, parts, (r_gate, r_up, r_down) = layer_bwd(dy_s, saved_acts, weights)
+        grad_rows = grad_x_emb.reshape(TOKS, UNROLL, LANES)
         grad_rows = order_rows(place, grad_rows)
-        all_rows, r_qkv, r_out, r_small = back(grad_rows, *parts)
-        d_table = add_rows(all_ids, sent_first, sent, all_rows.reshape(SHARDS * TOKS, 8, 128)).T
+        all_rows, r_qkv, r_out, r_small, y_t = back(grad_rows, *parts, *last, spread_m)
+        layer_out = y_t.transpose(0, 2, 1)
+        d_table = add_rows(all_ids, sent_first, sent, all_rows.reshape(SHARDS * TOKS, UNROLL, LANES)).T
         g_query, g_key, g_value = split_groups(r_qkv[:SUB])
         g_attn, g_mlp, g_q, g_k = (r_small[:, i] for i in range(4))
         return (layer_out, d_table, g_attn[:SUB], g_query, g_key, g_value, g_q, g_k, unspread_columns(r_out[:SUB]), g_mlp[:SUB], r_gate[:SUB], r_up[:SUB], unspread_columns(r_down))

time: 869 us -> 850 us (0.978)
  matrix products: 149 us -> 116 us
    dot_general x23 -> x19, matrix products: 149 us -> 116 us  [matmul(): return jnp.einsum(spec, lhs, rhs, preferred_element_type=jnp.float32)]
where the time goes in v3:
time: 850 us; the launch traced here: 842 us
  Pallas kernels  648 us (76%)
  matrix products  116 us (14%)
  local copies, waits for them, and re-layouts  41.4 us (5%)
  other arithmetic  20 us (2%)
  blocking collectives  15.1 us (2%)
    pallas_call x1, Pallas kernels, back(): pl.pallas_call(back_body, out_shape=(jax.ShapeDtypeStruct((SHARDS, TOKS,...  279 us
    pallas_call x1, Pallas kernels, front(): pl.pallas_call(front_body, out_shape=tuple((gathered_shape(a) for a in FR...  153 us
    pallas_call x1, Pallas kernels, attn_bwd(): pl.pallas_call(attn_bwd_body, out_shape=(jax.ShapeDtypeStruct(qkv.shape,...  117 us
    dot_general x19, matrix products, matmul(): return jnp.einsum(spec, lhs, rhs, preferred_element_type=jnp.float32)  116 us
    pallas_call x1, Pallas kernels, add_rows(): pl.pallas_call(add_body, grid_spec=pltpu.PrefetchScalarGridSpec(num_scala...  50.2 us
    pallas_call x1, Pallas kernels, attn_fwd(): pl.pallas_call(attn_fwd_body, out_shape=(jax.ShapeDtypeStruct(qkv.shape[:...  46.3 us

profile of v3, /device:TPU:0, one launch (start us, length us, event | category | flops | bytes accessed | tf_op | source)
XLA Modules:
  0.0 842.4 jit_solution(7950131944057004970)
XLA Ops:
  6.4 2.0 fusion.51
  10.2 15.1 %all-gather = s32[49152]{0:T(1024)S(1)} all-gather(s32[3072]{0:T(1024)S(1)} %concatenate.12), channel_id=2, replica_groups=mesh['fsdp'=16] {'fsdp'}, dimensions={0}, use_global_device_ids=true | all-gather | bytes 208896 | tf_op jit(solution)/shard_map/all_gather | solution.py:931
  27.5 1.9 fusion.50.refs_4_
  33.3 2.7 fusion.91.refs_5_
  36.0 4.1 convert_bitcast_fusion
  40.1 3.2 pad.34
  43.3 9.8 %copy.85.refs_1_ = bf16[3080,8,128]{2,1,0:T(8,128)(2,1)} copy(bf16[3080,8,128]{0,2,1:T(8,128)(2,1)} %bitcast.132) | data formatting | bytes 12615680 | tf_op jit(solution)/shard_map/reshape | solution.py:938
  53.1 153.4 %front.1 = (bf16[16,64,1920]{2,1,0:T(8,128)(2,1)}, bf16[16,64,1024]{2,1,0:T(8,128)(2,1)}, bf16[16,160,1024]{2,1,0:T(8,128)(2,1)}, bf16[1024,8,128]{2,1,0:T(8,128)(2,1)}) custom-call(s32[16384]{0:T(1024)} %and_select_fusion.refs_0_, bf16[3080,8,128]{2,1,0:T(8,128)(2,1)} %copy.85.refs_1_, bf16[64,1920]{1,0:T(8,128)(2,1)} %pad.37.refs_2_, ...), custom_call_target="tpu_custom_call" | custom-call | flops 60000002048 | bytes 100000000 | tf_op jit(solution)/shard_map/front/pallas_call | solution.py:381
  206.5 2.8 reshape.270
  209.4 2.7 fusion.31
  214.4 4.9 convolution_convert_fusion.1.refs_0_
  219.3 46.3 %attn_fwd.1 = (bf16[2,512,1280]{2,1,0:T(8,128)(2,1)S(1)}, bf16[16,64,2560]{2,1,0:T(8,128)(2,1)S(1)}, bf16[16,64,2560]{2,1,0:T(8,128)(2,1)}) custom-call(bf16[2,512,1920]{2,1,0:T(8,128)(2,1)S(1)} %convolution_convert_fusion.1.refs_0_, f32[2,512,64]{2,1,0:T(8,128)S(1)} %get-tuple-element.155.refs_1_, f32[2,512,64]{2,1,0:T(8,128)S(1)} %copy-done.4, ...), custom_call_target="tpu_custom_call" | custom-call | flops 20000000000 | bytes 100000000 | tf_op jit(solution)/shard_map/attn_fwd/pallas_call | solution.py:845
  265.7 3.5 convolution_convert_fusion.2
  269.2 2.6 fusion.24
  272.4 8.3 fusion.63
  280.7 8.8 %fusion.65 = f32[2,512,2560]{2,1,0:T(8,128)} fusion(bf16[1024,2560,1]{1,0,2:T(8,128)(2,1)S(1)} %bitcast.130, bf16[2,512,1024]{2,1,0:T(8,128)(2,1)S(1)} %get-tuple-element.140, f32[1024]{0:T(1024)S(1)} %get-tuple-element.100, f32[2,512]{1,0:T(2,128)S(1)} %add_rsqrt_fusion), kind=kOutput, calls=%fused_computation.81 | convolution fusion | flops 5372903424 | bytes 17833984 | tf_op jit(solution)/shard_map/bsd,df->bsf/dot_general | solution.py:530
  289.5 19.4 %multiply_convert_fusion = (bf16[2,512,2560]{2,1,0:T(8,128)(2,1)}, bf16[2,512,2560]{2,1,0:T(8,128)(2,1)}, bf16[2,512,2560]{2,1,0:T(8,128)(2,1)}) fusion(f32[2,512,2560]{2,1,0:T(8,128)} %fusion.63, f32[2,512,2560]{2,1,0:T(8,128)} %fusion.65, bf16[2,512,1024]{2,1,0:T(8,128)(2,1)} %convert_bitcast_fusion, bf16[2560,1024,1]{1,0,2:T(8,128)(2,1)} %bitcast.170), kind=kOutput, calls=%fused_computation | convolution fusion | flops 5410652160 | bytes 44040192 | tf_op jit(solution)/shard_map/bsd,fd->bsf/dot_general | solution.py:530
  308.9 9.3 %fusion.96 = f32[2,512,1024]{2,1,0:T(8,128)S(1)} fusion(bf16[2,512,2560]{2,1,0:T(8,128)(2,1)} %get-tuple-element.111, bf16[1024,2560,1]{1,0,2:T(8,128)(2,1)} %bitcast.131), kind=kOutput, calls=%fused_computation.154 | convolution fusion | flops 5368709120 | bytes 14680064 | tf_op jit(solution)/shard_map/bsf,df->bsd/dot_general | solution.py:530
  318.2 8.4 fusion.23
  328.2 2.4 fusion.134
  330.6 6.3 convolution_convert_fusion.refs_5_
  336.9 4.6 fusion.55
  341.5 8.4 %fusion.59 = f32[1024,2560,1]{1,0,2:T(8,128)} fusion(bf16[2,512,2560]{2,1,0:T(8,128)(2,1)S(1)} %copy-done.40, bf16[2,512,1024]{2,1,0:T(8,128)(2,1)S(1)} %get-tuple-element.140, f32[1024]{0:T(1024)S(1)} %get-tuple-element.100, f32[2,512]{1,0:T(2,128)S(1)} %add_rsqrt_fusion), kind=kOutput, calls=%fused_computation.78 | convolution fusion | flops 5372903424 | bytes 17833984 | tf_op jit(solution)/shard_map/bsd,bsf->df/dot_general | solution.py:530
  350.0 8.7 %fusion.61 = f32[1024,2560,1]{1,0,2:T(8,128)} fusion(bf16[2,512,2560]{2,1,0:T(8,128)(2,1)S(1)} %bitcast.182, bf16[2,512,1024]{2,1,0:T(8,128)(2,1)S(1)} %get-tuple-element.140, f32[1024]{0:T(1024)S(1)} %get-tuple-element.100, f32[2,512]{1,0:T(2,128)S(1)} %add_rsqrt_fusion), kind=kOutput, calls=%fused_computation.79 | convolution fusion | flops 5372903424 | bytes 17833984 | tf_op jit(solution)/shard_map/bsd,bsf->df/dot_general | solution.py:530
  358.7 8.5 %fusion.97 = f32[2560,1024,1]{1,0,2:T(8,128)} fusion(bf16[2,512,2560]{2,1,0:T(8,128)(2,1)S(1)} %bitcast.174, bf16[2,512,1024]{2,1,0:T(8,128)(2,1)S(1)} %copy-done.17), kind=kOutput, calls=%fused_computation.155 | convolution fusion | flops 5368709120 | bytes 17825792 | tf_op jit(solution)/shard_map/bsf,bsd->fd/dot_general | solution.py:530
  367.2 117.2 %attn_bwd.1 = (bf16[2,512,1920]{2,1,0:T(8,128)(2,1)}, f32[1,64]{1,0:T(1,128)}, f32[1,64]{1,0:T(1,128)}, f32[2,512,1024]{2,1,0:T(8,128)}, f32[64,2560]{1,0:T(8,12...) custom-call(bf16[2,512,1920]{2,1,0:T(8,128)(2,1)} %copy-done.11, f32[2,512,64]{2,1,0:T(8,128)} %copy-done.3, ...), custom_call_target="tpu_custom_call" | custom-call | flops 60000002048 | bytes 100000000 | tf_op jit(solution)/shard_map/attn_bwd/pallas_call | solution.py:859
  485.9 4.3 fusion.30
  490.2 3.0 fusion.29
  494.3 2.4 order_rows.1.rows_ref
  496.7 2.0 copy-done.2
  501.5 279.0 %back.1 = (f32[16,1024,8,128]{3,2,1,0:T(8,128)}, f32[64,1920]{1,0:T(8,128)}, f32[64,1024]{1,0:T(8,128)}, f32[64,128]{1,0:T(8,128)}, bf16[2,960,512]{2,1,0:T(8,128)(2,1)}) custom-call(f32[1024,8,128]{2,1,0:T(8,128)} %copy-done.2, f32[16,64,1024]{2,1,0:T(8,128)} %bitcast.177, f32[16,64,128]{2,1,0:T(8,128)} %bitcast.146, bf16[1024,1024]{1,0:T(8,128)(2,1)} %bitcast.139, ...), custom_call_target="tpu_custom_call" | custom-call | flops 80000000000 | bytes 100000000 | tf_op jit(solution)/shard_map/back/pallas_call | solution.py:503
  780.6 50.2 %add_rows.1 = f32[960,3072]{1,0:T(8,128)} custom-call(s32[16384]{0:T(1024)} %bitcast.148, s32[16]{0:T(128)} %get-tuple-element.136.first_ref, s32[16]{0:T(128)} %get-tuple-element.135.count_ref, f32[16384,8,128]{2,1,0:T(8,128)} %bitcast.47.in_ref), custom_call_target="tpu_custom_call" | custom-call | tf_op jit(solution)/shard_map/add_rows/pallas_call | solution.py:648
  (176 shorter events, 34.4 us)
Async XLA Ops:
  0.6 26.9 %copy-start = (bf16[160,960]{1,0:T(8,128)(2,1)S(1)}, bf16[160,960]{1,0:T(8,128)(2,1)}, u32[]{:S(2)}) copy-start(bf16[160,960]{1,0:T(8,128)(2,1)} %param.28) | copy-start | bytes 921604
  2.1 217.2 %copy-start.8 = (f32[1,64]{1,0:T(1,128)}, f32[1,64]{1,0:T(1,128)S(1)}, u32[]{:S(2)}) copy-start(f32[1,64]{1,0:T(1,128)S(1)} %get-tuple-element.157.refs_4_) | copy-start | bytes 772
  2.1 217.2 %copy-start.9 = (f32[1,64]{1,0:T(1,128)}, f32[1,64]{1,0:T(1,128)S(1)}, u32[]{:S(2)}) copy-start(f32[1,64]{1,0:T(1,128)S(1)} %get-tuple-element.158.refs_3_) | copy-start | bytes 772
  29.4 6.5 copy-start.36
  33.3 186.0 %copy-start.3 = (f32[2,512,64]{2,1,0:T(8,128)}, f32[2,512,64]{2,1,0:T(8,128)S(1)}, u32[]{:S(2)}) copy-start(f32[2,512,64]{2,1,0:T(8,128)S(1)} %get-tuple-element.155.refs_1_) | copy-start | bytes 786436
  33.3 6.8 slice-start
  36.0 4.1 slice-start.1
  212.1 57.1 %copy-start.12 = (bf16[2,512,1024]{2,1,0:T(8,128)(2,1)}, bf16[2,512,1024]{2,1,0:T(8,128)(2,1)S(1)}, u32[]{:S(2)}) copy-start(bf16[2,512,1024]{2,1,0:T(8,128)(2,1)S(1)} %get-tuple-element.138) | copy-start | bytes 6291460
  214.4 4.9 copy-start.4
  214.4 4.9 copy-start.5
  219.3 46.3 %copy-start.11 = (bf16[2,512,1920]{2,1,0:T(8,128)(2,1)}, bf16[2,512,1920]{2,1,0:T(8,128)(2,1)S(1)}, u32[]{:S(2)}) copy-start(bf16[2,512,1920]{2,1,0:T(8,128)(2,1)S(1)} %convolution_convert_fusion.1.refs_0_) | copy-start | bytes 11796484
  265.6 15.1 %copy-start.10 = (bf16[16,64,2560]{2,1,0:T(8,128)(2,1)}, bf16[16,64,2560]{2,1,0:T(8,128)(2,1)S(1)}, u32[]{:S(2)}) copy-start(bf16[16,64,2560]{2,1,0:T(8,128)(2,1)S(1)} %get-tuple-element.39) | copy-start | bytes 15728644
  271.8 78.2 %copy-start.16 = (bf16[2,512,1024]{2,1,0:T(8,128)(2,1)}, bf16[2,512,1024]{2,1,0:T(8,128)(2,1)S(1)}, u32[]{:S(2)}) copy-start(bf16[2,512,1024]{2,1,0:T(8,128)(2,1)S(1)} %get-tuple-element.140) | copy-start | bytes 6291460
  308.9 9.3 %copy-start.40 = (bf16[2,512,2560]{2,1,0:T(8,128)(2,1)S(1)}, bf16[2,512,2560]{2,1,0:T(8,128)(2,1)}, u32[]{:S(2)}) copy-start(bf16[2,512,2560]{2,1,0:T(8,128)(2,1)} %get-tuple-element.112) | copy-start | bytes 15728644
  318.2 8.4 copy-start.17
  328.2 8.7 %copy-start.14 = (f32[2,512,1024]{2,1,0:T(8,128)}, f32[2,512,1024]{2,1,0:T(8,128)S(1)}, u32[]{:S(2)}) copy-start(f32[2,512,1024]{2,1,0:T(8,128)S(1)} %fusion.22) | copy-start | bytes 12582916
  330.6 6.4 copy-start.42
  336.9 13.0 %slice-start.4 = ((s8[5242880]{0:T(1024)(128)(4,1)}), s8[4194304]{0:T(1024)(128)(4,1)S(1)}, s32[]{:S(2)}) async-start(s8[5242880]{0:T(1024)(128)(4,1)} %bitcast.181), calls=%async_computation.4 | async-start | bytes 8388608
  341.5 8.5 %slice-start.5 = ((s8[5242880]{0:T(1024)(128)(4,1)}), s8[1048576]{0:T(1024)(128)(4,1)S(1)}, s32[]{:S(2)}) async-start(s8[5242880]{0:T(1024)(128)(4,1)} %bitcast.181), calls=%async_computation.5 | async-start | bytes 2097152
  341.5 17.2 %slice-start.2 = ((s8[5242880]{0:T(1024)(128)(4,1)}), s8[4194304]{0:T(1024)(128)(4,1)S(1)}, s32[]{:S(2)}) async-start(s8[5242880]{0:T(1024)(128)(4,1)} %bitcast.173), calls=%async_computation.2 | async-start | bytes 8388608
  350.0 8.7 %slice-start.3 = ((s8[5242880]{0:T(1024)(128)(4,1)}), s8[1048576]{0:T(1024)(128)(4,1)S(1)}, s32[]{:S(2)}) async-start(s8[5242880]{0:T(1024)(128)(4,1)} %bitcast.173), calls=%async_computation.3 | async-start | bytes 2097152
  367.2 118.7 %copy-start.33 = (f32[1024]{0:T(1024)S(1)}, f32[1024]{0:T(1024)}, u32[]{:S(2)}) copy-start(f32[1024]{0:T(1024)} %copy-done.32) | copy-start | bytes 12292
  367.2 118.7 %copy-start.35 = (f32[2,512]{1,0:T(2,128)S(1)}, f32[2,512]{1,0:T(2,128)}, u32[]{:S(2)}) copy-start(f32[2,512]{1,0:T(2,128)} %copy-done.34) | copy-start | bytes 12292
  484.3 5.8 copy-start.13
  485.9 4.3 copy-start.15
  494.3 5.5 copy-start.22
  780.6 50.2 %copy-start.23 = (f32[64,128]{1,0:T(8,128)S(1)}, f32[64,128]{1,0:T(8,128)}, u32[]{:S(2)}) copy-start(f32[64,128]{1,0:T(8,128)} %get-tuple-element.51) | copy-start | bytes 98308
  780.6 51.6 %copy-start.27 = (f32[64,1024]{1,0:T(8,128)S(1)}, f32[64,1024]{1,0:T(8,128)}, u32[]{:S(2)}) copy-start(f32[64,1024]{1,0:T(8,128)} %get-tuple-element.53) | copy-start | bytes 786436
  780.6 52.7 %copy-start.24 = (f32[64,1920]{1,0:T(8,128)S(1)}, f32[64,1920]{1,0:T(8,128)}, u32[]{:S(2)}) copy-start(f32[64,1920]{1,0:T(8,128)} %get-tuple-element.52) | copy-start | bytes 1474564
  830.8 7.9 copy-start.19
  833.4 8.6 %copy-start.1 = (bf16[160,960]{1,0:T(8,128)(2,1)S(1)}, bf16[160,960]{1,0:T(8,128)(2,1)}, u32[]{:S(2)}) copy-start(bf16[160,960]{1,0:T(8,128)(2,1)} %param.28) | copy-start | bytes 921604
  834.2 6.9 copy-start.20
  (17 other events, 38.2 us)

commit v4 on v3

--- a/solution.py
+++ b/solution.py
@@ -467,9 +467,6 @@
     load.wait()
     store = pltpu.make_async_copy(stage, all_ref.at[device_at(bits, '')], own_sem.at[1])
     store.start()
-    for n in range(len(FIRST_ORDER)):
-        tree.first(n, tree.fill)
-
     blocks = SEQ // HALF
 
     def project(i, carry):
@@ -479,16 +476,19 @@
         y_ref[i // blocks, :, part] = dot_nt(spread_m[...], total).astype(jnp.bfloat16)
         return carry
 
+    for n in range(len(FIRST_ORDER)):
+        tree.first(n, tree.fill)
     ring.forward(1)
-    tree.second()
     ring.forward(2)
     ring.forward(3)
+    tree.second()
+    loop(TOKS // HALF, project)
+    ring.forward(4)
+    ring.forward(5)
+    ring.forward(6)
     tree.third()
-    ring.forward(4)
-    loop(TOKS // HALF, project)
+    ring.forward(7)
     tree.last(tree.put)
-    for code in range(5, UNROLL):
-        ring.forward(code)
     tree.close()
     ring.close()
     store.wait()

time: 850 us -> 834 us (0.981)
  Pallas kernels: 648 us -> 633 us
    pallas_call x1, Pallas kernels: 279 us -> 264 us  [back(): pl.pallas_call(back_body, out_shape=(jax.ShapeDtypeStruct((SHARDS, TOKS,...]
where the time goes in v4:
time: 834 us; the launch traced here: 827 us
  Pallas kernels  633 us (76%)
  matrix products  116 us (14%)
  local copies, waits for them, and re-layouts  41.4 us (5%)
  other arithmetic  20 us (2%)
  blocking collectives  15.1 us (2%)
    pallas_call x1, Pallas kernels, back(): pl.pallas_call(back_body, out_shape=(jax.ShapeDtypeStruct((SHARDS, TOKS,...  264 us
    pallas_call x1, Pallas kernels, front(): pl.pallas_call(front_body, out_shape=tuple((gathered_shape(a) for a in FR...  153 us
    pallas_call x1, Pallas kernels, attn_bwd(): pl.pallas_call(attn_bwd_body, out_shape=(jax.ShapeDtypeStruct(qkv.shape,...  117 us
    dot_general x19, matrix products, matmul(): return jnp.einsum(spec, lhs, rhs, preferred_element_type=jnp.float32)  116 us
    pallas_call x1, Pallas kernels, add_rows(): pl.pallas_call(add_body, grid_spec=pltpu.PrefetchScalarGridSpec(num_scala...  50.2 us
    pallas_call x1, Pallas kernels, attn_fwd(): pl.pallas_call(attn_fwd_body, out_shape=(jax.ShapeDtypeStruct(qkv.shape[:...  46.3 us

profile of v4, /device:TPU:0, one launch (start us, length us, event | category | flops | bytes accessed | tf_op | source)
XLA Modules:
  0.0 826.8 jit_solution(5802034085794227530)
XLA Ops:
  6.4 2.0 fusion.51
  10.2 15.1 %all-gather = s32[49152]{0:T(1024)S(1)} all-gather(s32[3072]{0:T(1024)S(1)} %concatenate.12), channel_id=2, replica_groups=mesh['fsdp'=16] {'fsdp'}, dimensions={0}, use_global_device_ids=true | all-gather | bytes 208896 | tf_op jit(solution)/shard_map/all_gather | solution.py:931
  27.5 1.9 fusion.50.refs_4_
  33.3 2.7 fusion.91.refs_5_
  36.0 4.1 convert_bitcast_fusion
  40.1 3.2 pad.34
  43.3 9.8 %copy.85.refs_1_ = bf16[3080,8,128]{2,1,0:T(8,128)(2,1)} copy(bf16[3080,8,128]{0,2,1:T(8,128)(2,1)} %bitcast.132) | data formatting | bytes 12615680 | tf_op jit(solution)/shard_map/reshape | solution.py:938
  53.1 153.4 %front.1 = (bf16[16,64,1920]{2,1,0:T(8,128)(2,1)}, bf16[16,64,1024]{2,1,0:T(8,128)(2,1)}, bf16[16,160,1024]{2,1,0:T(8,128)(2,1)}, bf16[1024,8,128]{2,1,0:T(8,128)(2,1)}) custom-call(s32[16384]{0:T(1024)} %and_select_fusion.refs_0_, bf16[3080,8,128]{2,1,0:T(8,128)(2,1)} %copy.85.refs_1_, bf16[64,1920]{1,0:T(8,128)(2,1)} %pad.37.refs_2_, ...), custom_call_target="tpu_custom_call" | custom-call | flops 60000002048 | bytes 100000000 | tf_op jit(solution)/shard_map/front/pallas_call | solution.py:381
  206.5 2.8 reshape.270
  209.4 2.7 fusion.31
  214.4 4.9 convolution_convert_fusion.1.refs_0_
  219.3 46.3 %attn_fwd.1 = (bf16[2,512,1280]{2,1,0:T(8,128)(2,1)S(1)}, bf16[16,64,2560]{2,1,0:T(8,128)(2,1)S(1)}, bf16[16,64,2560]{2,1,0:T(8,128)(2,1)}) custom-call(bf16[2,512,1920]{2,1,0:T(8,128)(2,1)S(1)} %convolution_convert_fusion.1.refs_0_, f32[2,512,64]{2,1,0:T(8,128)S(1)} %get-tuple-element.155.refs_1_, f32[2,512,64]{2,1,0:T(8,128)S(1)} %copy-done.4, ...), custom_call_target="tpu_custom_call" | custom-call | flops 20000000000 | bytes 100000000 | tf_op jit(solution)/shard_map/attn_fwd/pallas_call | solution.py:845
  265.7 3.5 convolution_convert_fusion.2
  269.2 2.6 fusion.24
  272.4 8.3 %fusion.63 = f32[2,512,2560]{2,1,0:T(8,128)} fusion(bf16[1024,2560,1]{1,0,2:T(8,128)(2,1)S(1)} %bitcast.176, bf16[2,512,1024]{2,1,0:T(8,128)(2,1)S(1)} %get-tuple-element.140, f32[1024]{0:T(1024)S(1)} %get-tuple-element.100, f32[2,512]{1,0:T(2,128)S(1)} %add_rsqrt_fusion), kind=kOutput, calls=%fused_computation.80 | convolution fusion | flops 5372903424 | bytes 17833984 | tf_op jit(solution)/shard_map/bsd,df->bsf/dot_general | solution.py:530
  280.7 8.8 %fusion.65 = f32[2,512,2560]{2,1,0:T(8,128)} fusion(bf16[1024,2560,1]{1,0,2:T(8,128)(2,1)S(1)} %bitcast.130, bf16[2,512,1024]{2,1,0:T(8,128)(2,1)S(1)} %get-tuple-element.140, f32[1024]{0:T(1024)S(1)} %get-tuple-element.100, f32[2,512]{1,0:T(2,128)S(1)} %add_rsqrt_fusion), kind=kOutput, calls=%fused_computation.81 | convolution fusion | flops 5372903424 | bytes 17833984 | tf_op jit(solution)/shard_map/bsd,df->bsf/dot_general | solution.py:530
  289.5 19.4 %multiply_convert_fusion = (bf16[2,512,2560]{2,1,0:T(8,128)(2,1)}, bf16[2,512,2560]{2,1,0:T(8,128)(2,1)}, bf16[2,512,2560]{2,1,0:T(8,128)(2,1)}) fusion(f32[2,512,2560]{2,1,0:T(8,128)} %fusion.63, f32[2,512,2560]{2,1,0:T(8,128)} %fusion.65, bf16[2,512,1024]{2,1,0:T(8,128)(2,1)} %convert_bitcast_fusion, bf16[2560,1024,1]{1,0,2:T(8,128)(2,1)} %bitcast.170), kind=kOutput, calls=%fused_computation | convolution fusion | flops 5410652160 | bytes 44040192 | tf_op jit(solution)/shard_map/bsd,fd->bsf/dot_general | solution.py:530
  308.9 9.3 %fusion.96 = f32[2,512,1024]{2,1,0:T(8,128)S(1)} fusion(bf16[2,512,2560]{2,1,0:T(8,128)(2,1)} %get-tuple-element.111, bf16[1024,2560,1]{1,0,2:T(8,128)(2,1)} %bitcast.131), kind=kOutput, calls=%fused_computation.154 | convolution fusion | flops 5368709120 | bytes 14680064 | tf_op jit(solution)/shard_map/bsf,df->bsd/dot_general | solution.py:530
  318.2 8.4 %fusion.23 = (f32[1024]{0:T(1024)S(1)}, f32[2,512]{1,0:T(2,128)S(1)}, f32[2,512,1024]{2,1,0:T(8,128)S(1)}) fusion(bf16[2,512,1024]{2,1,0:T(8,128)(2,1)S(1)} %get-tuple-element.140, f32[2,512]{1,0:T(2,128)S(1)} %add_rsqrt_fusion, f32[1024]{0:T(1024)S(1)} %get-tuple-element.100, f32[2,512,1024]{2,1,0:T(8,128)S(1)} %fusion.96, ...), kind=kOutput, calls=%fused_computation.37 | convolution fusion | flops 5377095680 | bytes 20987904 | tf_op jit(solution)/shard_map/bsf,df->bsd/dot_general | solution.py:530
  328.2 2.4 fusion.134
  330.6 6.3 convolution_convert_fusion.refs_5_
  336.9 4.6 fusion.55
  341.5 8.4 %fusion.59 = f32[1024,2560,1]{1,0,2:T(8,128)} fusion(bf16[2,512,2560]{2,1,0:T(8,128)(2,1)S(1)} %copy-done.40, bf16[2,512,1024]{2,1,0:T(8,128)(2,1)S(1)} %get-tuple-element.140, f32[1024]{0:T(1024)S(1)} %get-tuple-element.100, f32[2,512]{1,0:T(2,128)S(1)} %add_rsqrt_fusion), kind=kOutput, calls=%fused_computation.78 | convolution fusion | flops 5372903424 | bytes 17833984 | tf_op jit(solution)/shard_map/bsd,bsf->df/dot_general | solution.py:530
  350.0 8.7 %fusion.61 = f32[1024,2560,1]{1,0,2:T(8,128)} fusion(bf16[2,512,2560]{2,1,0:T(8,128)(2,1)S(1)} %bitcast.182, bf16[2,512,1024]{2,1,0:T(8,128)(2,1)S(1)} %get-tuple-element.140, f32[1024]{0:T(1024)S(1)} %get-tuple-element.100, f32[2,512]{1,0:T(2,128)S(1)} %add_rsqrt_fusion), kind=kOutput, calls=%fused_computation.79 | convolution fusion | flops 5372903424 | bytes 17833984 | tf_op jit(solution)/shard_map/bsd,bsf->df/dot_general | solution.py:530
  358.7 8.5 %fusion.97 = f32[2560,1024,1]{1,0,2:T(8,128)} fusion(bf16[2,512,2560]{2,1,0:T(8,128)(2,1)S(1)} %bitcast.174, bf16[2,512,1024]{2,1,0:T(8,128)(2,1)S(1)} %copy-done.17), kind=kOutput, calls=%fused_computation.155 | convolution fusion | flops 5368709120 | bytes 17825792 | tf_op jit(solution)/shard_map/bsf,bsd->fd/dot_general | solution.py:530
  367.2 117.2 %attn_bwd.1 = (bf16[2,512,1920]{2,1,0:T(8,128)(2,1)}, f32[1,64]{1,0:T(1,128)}, f32[1,64]{1,0:T(1,128)}, f32[2,512,1024]{2,1,0:T(8,128)}, f32[64,2560]{1,0:T(8,12...) custom-call(bf16[2,512,1920]{2,1,0:T(8,128)(2,1)} %copy-done.11, f32[2,512,64]{2,1,0:T(8,128)} %copy-done.3, ...), custom_call_target="tpu_custom_call" | custom-call | flops 60000002048 | bytes 100000000 | tf_op jit(solution)/shard_map/attn_bwd/pallas_call | solution.py:859
  485.9 4.3 fusion.30
  490.2 3.0 fusion.29
  494.3 2.4 order_rows.1.rows_ref
  496.7 2.0 copy-done.2
  501.5 263.5 %back.1 = (f32[16,1024,8,128]{3,2,1,0:T(8,128)}, f32[64,1920]{1,0:T(8,128)}, f32[64,1024]{1,0:T(8,128)}, f32[64,128]{1,0:T(8,128)}, bf16[2,960,512]{2,1,0:T(8,128)(2,1)}) custom-call(f32[1024,8,128]{2,1,0:T(8,128)} %copy-done.2, f32[16,64,1024]{2,1,0:T(8,128)} %bitcast.177, f32[16,64,128]{2,1,0:T(8,128)} %bitcast.146, bf16[1024,1024]{1,0:T(8,128)(2,1)} %bitcast.139, ...), custom_call_target="tpu_custom_call" | custom-call | flops 80000000000 | bytes 100000000 | tf_op jit(solution)/shard_map/back/pallas_call | solution.py:503
  765.1 50.2 %add_rows.1 = f32[960,3072]{1,0:T(8,128)} custom-call(s32[16384]{0:T(1024)} %bitcast.148, s32[16]{0:T(128)} %get-tuple-element.136.first_ref, s32[16]{0:T(128)} %get-tuple-element.135.count_ref, f32[16384,8,128]{2,1,0:T(8,128)} %bitcast.47.in_ref), custom_call_target="tpu_custom_call" | custom-call | tf_op jit(solution)/shard_map/add_rows/pallas_call | solution.py:648
  (176 shorter events, 34.4 us)
Async XLA Ops:
  0.6 26.9 %copy-start = (bf16[160,960]{1,0:T(8,128)(2,1)S(1)}, bf16[160,960]{1,0:T(8,128)(2,1)}, u32[]{:S(2)}) copy-start(bf16[160,960]{1,0:T(8,128)(2,1)} %param.28) | copy-start | bytes 921604
  2.1 217.2 %copy-start.8 = (f32[1,64]{1,0:T(1,128)}, f32[1,64]{1,0:T(1,128)S(1)}, u32[]{:S(2)}) copy-start(f32[1,64]{1,0:T(1,128)S(1)} %get-tuple-element.157.refs_4_) | copy-start | bytes 772
  2.1 217.2 %copy-start.9 = (f32[1,64]{1,0:T(1,128)}, f32[1,64]{1,0:T(1,128)S(1)}, u32[]{:S(2)}) copy-start(f32[1,64]{1,0:T(1,128)S(1)} %get-tuple-element.158.refs_3_) | copy-start | bytes 772
  29.4 6.5 copy-start.36
  33.3 186.0 %copy-start.3 = (f32[2,512,64]{2,1,0:T(8,128)}, f32[2,512,64]{2,1,0:T(8,128)S(1)}, u32[]{:S(2)}) copy-start(f32[2,512,64]{2,1,0:T(8,128)S(1)} %get-tuple-element.155.refs_1_) | copy-start | bytes 786436
  33.3 6.8 slice-start
  36.0 4.1 slice-start.1
  212.1 57.1 %copy-start.12 = (bf16[2,512,1024]{2,1,0:T(8,128)(2,1)}, bf16[2,512,1024]{2,1,0:T(8,128)(2,1)S(1)}, u32[]{:S(2)}) copy-start(bf16[2,512,1024]{2,1,0:T(8,128)(2,1)S(1)} %get-tuple-element.138) | copy-start | bytes 6291460
  214.4 4.9 copy-start.4
  214.4 4.9 copy-start.5
  219.3 46.3 %copy-start.11 = (bf16[2,512,1920]{2,1,0:T(8,128)(2,1)}, bf16[2,512,1920]{2,1,0:T(8,128)(2,1)S(1)}, u32[]{:S(2)}) copy-start(bf16[2,512,1920]{2,1,0:T(8,128)(2,1)S(1)} %convolution_convert_fusion.1.refs_0_) | copy-start | bytes 11796484
  265.6 15.1 %copy-start.10 = (bf16[16,64,2560]{2,1,0:T(8,128)(2,1)}, bf16[16,64,2560]{2,1,0:T(8,128)(2,1)S(1)}, u32[]{:S(2)}) copy-start(bf16[16,64,2560]{2,1,0:T(8,128)(2,1)S(1)} %get-tuple-element.39) | copy-start | bytes 15728644
  271.8 78.2 %copy-start.16 = (bf16[2,512,1024]{2,1,0:T(8,128)(2,1)}, bf16[2,512,1024]{2,1,0:T(8,128)(2,1)S(1)}, u32[]{:S(2)}) copy-start(bf16[2,512,1024]{2,1,0:T(8,128)(2,1)S(1)} %get-tuple-element.140) | copy-start | bytes 6291460
  308.9 9.3 %copy-start.40 = (bf16[2,512,2560]{2,1,0:T(8,128)(2,1)S(1)}, bf16[2,512,2560]{2,1,0:T(8,128)(2,1)}, u32[]{:S(2)}) copy-start(bf16[2,512,2560]{2,1,0:T(8,128)(2,1)} %get-tuple-element.112) | copy-start | bytes 15728644
  318.2 8.4 %copy-start.17 = (bf16[2,512,1024]{2,1,0:T(8,128)(2,1)S(1)}, bf16[2,512,1024]{2,1,0:T(8,128)(2,1)}, u32[]{:S(2)}) copy-start(bf16[2,512,1024]{2,1,0:T(8,128)(2,1)} %convert_bitcast_fusion) | copy-start | bytes 6291460
  328.2 8.7 %copy-start.14 = (f32[2,512,1024]{2,1,0:T(8,128)}, f32[2,512,1024]{2,1,0:T(8,128)S(1)}, u32[]{:S(2)}) copy-start(f32[2,512,1024]{2,1,0:T(8,128)S(1)} %fusion.22) | copy-start | bytes 12582916
  330.6 6.4 copy-start.42
  336.9 13.0 %slice-start.4 = ((s8[5242880]{0:T(1024)(128)(4,1)}), s8[4194304]{0:T(1024)(128)(4,1)S(1)}, s32[]{:S(2)}) async-start(s8[5242880]{0:T(1024)(128)(4,1)} %bitcast.181), calls=%async_computation.4 | async-start | bytes 8388608
  341.5 8.5 %slice-start.5 = ((s8[5242880]{0:T(1024)(128)(4,1)}), s8[1048576]{0:T(1024)(128)(4,1)S(1)}, s32[]{:S(2)}) async-start(s8[5242880]{0:T(1024)(128)(4,1)} %bitcast.181), calls=%async_computation.5 | async-start | bytes 2097152
  341.5 17.2 %slice-start.2 = ((s8[5242880]{0:T(1024)(128)(4,1)}), s8[4194304]{0:T(1024)(128)(4,1)S(1)}, s32[]{:S(2)}) async-start(s8[5242880]{0:T(1024)(128)(4,1)} %bitcast.173), calls=%async_computation.2 | async-start | bytes 8388608
  350.0 8.7 %slice-start.3 = ((s8[5242880]{0:T(1024)(128)(4,1)}), s8[1048576]{0:T(1024)(128)(4,1)S(1)}, s32[]{:S(2)}) async-start(s8[5242880]{0:T(1024)(128)(4,1)} %bitcast.173), calls=%async_computation.3 | async-start | bytes 2097152
  367.2 118.7 %copy-start.33 = (f32[1024]{0:T(1024)S(1)}, f32[1024]{0:T(1024)}, u32[]{:S(2)}) copy-start(f32[1024]{0:T(1024)} %copy-done.32) | copy-start | bytes 12292
  367.2 118.7 %copy-start.35 = (f32[2,512]{1,0:T(2,128)S(1)}, f32[2,512]{1,0:T(2,128)}, u32[]{:S(2)}) copy-start(f32[2,512]{1,0:T(2,128)} %copy-done.34) | copy-start | bytes 12292
  484.3 5.8 copy-start.13
  485.9 4.3 copy-start.15
  494.3 5.5 copy-start.22
  765.1 50.2 %copy-start.23 = (f32[64,128]{1,0:T(8,128)S(1)}, f32[64,128]{1,0:T(8,128)}, u32[]{:S(2)}) copy-start(f32[64,128]{1,0:T(8,128)} %get-tuple-element.51) | copy-start | bytes 98308
  765.1 51.6 %copy-start.27 = (f32[64,1024]{1,0:T(8,128)S(1)}, f32[64,1024]{1,0:T(8,128)}, u32[]{:S(2)}) copy-start(f32[64,1024]{1,0:T(8,128)} %get-tuple-element.53) | copy-start | bytes 786436
  765.1 52.6 %copy-start.24 = (f32[64,1920]{1,0:T(8,128)S(1)}, f32[64,1920]{1,0:T(8,128)}, u32[]{:S(2)}) copy-start(f32[64,1920]{1,0:T(8,128)} %get-tuple-element.52) | copy-start | bytes 1474564
  815.2 7.9 copy-start.19
  817.8 8.6 %copy-start.1 = (bf16[160,960]{1,0:T(8,128)(2,1)S(1)}, bf16[160,960]{1,0:T(8,128)(2,1)}, u32[]{:S(2)}) copy-start(bf16[160,960]{1,0:T(8,128)(2,1)} %param.28) | copy-start | bytes 921604
  818.7 6.9 copy-start.20
  (17 other events, 38.2 us)
